TPU v7x, 16 devices: a whole 2x2x2 slice. The times are simulated.
16 devices in a mesh: graph: 16 (over z, y, x, core).
Axes of the slice: x: 2, y: 2, z: 2, core: 2. Of those that a mesh axis runs over, the one named last changes fastest.
Arguments:
- node_feats: bfloat16 [32768, 128], P('graph')
- w_one: float32 [128, 256], replicated
- w_two: float32 [256, 172], replicated
- send_idx: int32 [32, 1024], P('graph')
- edge_src: int32 [131072], P('graph')
- edge_dst: int32 [131072], P('graph')
- edge_w: float32 [131072], P('graph')
- labels: int32 [32768], P('graph')
- label_mask: int32 [32768], P('graph')
Outputs:
- output 1: float32 [], replicated
- output 2: float32 [128, 256], replicated
- output 3: float32 [256, 172], replicated
All inputs are finite; a program needn't handle non-finite values.
Results may differ from a plain program's by a relative error of at most 0.001.
Values are sent between devices in bfloat16 or wider.
A program may use at most 1 GiB of HBM per device.

v0:
```python
import jax
import jax.numpy as jnp
from jax import lax
from jax.sharding import PartitionSpec as P

GRAPH_AXIS = "graph"
CONTRACT_ROWS = (((0,), (0,)), ((), ()))
CONTRACT_COLS = (((1,), (1,)), ((), ()))


def solution(mesh):
    num_dev = mesh.shape[GRAPH_AXIS]
    to_next = [(dev_id, (dev_id + 1) % num_dev) for dev_id in range(num_dev)]
    to_prev = [(dev_id, (dev_id - 1) % num_dev) for dev_id in range(num_dev)]

    def halo_extend(node_table, send_rows):
        from_prev = lax.ppermute(node_table[send_rows[1]], GRAPH_AXIS, to_next)
        from_next = lax.ppermute(node_table[send_rows[0]], GRAPH_AXIS, to_prev)
        return jnp.concatenate([node_table, from_prev, from_next], axis=0)

    def aggregate(ext_table, edge_src, edge_dst, edge_w, rows_loc):
        return jax.ops.segment_sum(edge_w[:, None] * ext_table[edge_src], edge_dst, num_segments=rows_loc)

    def scatter_back(grad_rows, send_rows, edge_src, edge_dst, edge_w):
        rows_loc = grad_rows.shape[0]
        halo_rows = send_rows.shape[1]
        ext_grad = jax.ops.segment_sum(edge_w[:, None] * grad_rows[edge_dst], edge_src, num_segments=rows_loc + 2 * halo_rows)
        back_prev = lax.ppermute(ext_grad[rows_loc:rows_loc + halo_rows], GRAPH_AXIS, to_prev)
        back_next = lax.ppermute(ext_grad[rows_loc + halo_rows:], GRAPH_AXIS, to_next)
        row_ids = jnp.concatenate([send_rows[1], send_rows[0]])
        return ext_grad[:rows_loc].at[row_ids].add(jnp.concatenate([back_prev, back_next], axis=0))

    def device_step(node_feats, w_one, w_two, send_rows, edge_src, edge_dst, edge_w, labels, label_mask):
        rows_loc = node_feats.shape[0]
        w_one_b = w_one.astype(jnp.bfloat16)
        w_two_b = w_two.astype(jnp.bfloat16)
        tab_one = jnp.dot(node_feats, w_one_b, preferred_element_type=jnp.float32).astype(jnp.bfloat16)
        pre_one = aggregate(halo_extend(tab_one, send_rows), edge_src, edge_dst, edge_w, rows_loc)
        hidden = jnp.maximum(pre_one, 0.0).astype(jnp.bfloat16)
        tab_two = jnp.dot(hidden, w_two_b, preferred_element_type=jnp.float32).astype(jnp.bfloat16)
        logits = aggregate(halo_extend(tab_two, send_rows), edge_src, edge_dst, edge_w, rows_loc)
        mask_f = label_mask.astype(jnp.float32)
        label_count = jnp.maximum(lax.psum(jnp.sum(mask_f), GRAPH_AXIS), 1.0)
        log_norm = jax.nn.logsumexp(logits, axis=1)
        one_hot = (labels[:, None] == jnp.arange(logits.shape[1])[None, :]).astype(jnp.float32)
        picked = jnp.sum(logits * one_hot, axis=1)
        mean_loss = lax.psum(jnp.sum(mask_f * (log_norm - picked)), GRAPH_AXIS) / label_count
        d_logits = (jnp.exp(logits - log_norm[:, None]) - one_hot) * (mask_f / label_count)[:, None]
        d_tab_two = scatter_back(d_logits, send_rows, edge_src, edge_dst, edge_w).astype(jnp.bfloat16)
        grad_two = lax.psum(lax.dot_general(hidden, d_tab_two, CONTRACT_ROWS, preferred_element_type=jnp.float32), GRAPH_AXIS)
        d_hidden = lax.dot_general(d_tab_two, w_two_b, CONTRACT_COLS, preferred_element_type=jnp.float32)
        d_pre = jnp.where(pre_one > 0.0, d_hidden, 0.0)
        d_tab_one = scatter_back(d_pre, send_rows, edge_src, edge_dst, edge_w).astype(jnp.bfloat16)
        grad_one = lax.psum(lax.dot_general(node_feats, d_tab_one, CONTRACT_ROWS, preferred_element_type=jnp.float32), GRAPH_AXIS)
        return mean_loss, grad_one, grad_two

    row_spec = P(GRAPH_AXIS)
    return jax.shard_map(device_step, mesh=mesh, in_specs=(row_spec, P(), P(), row_spec, row_spec, row_spec, row_spec, row_spec, row_spec), out_specs=(P(), P(), P()), check_vma=False)
```

profile of v0, /device:TPU:0, one launch (start us, length us, event | category | flops | bytes accessed | tf_op | source)
XLA Modules:
  0.0 654.1 jit_solution(1577382763162343415)
XLA Ops:
  7.2 0.0 copy-start
  7.2 0.0 all-reduce.4.cloned.1.call-start
  7.2 0.8 compare_select_fusion.5
  8.0 0.2 copy-done
  8.2 1.3 convolution_convert_fusion
  9.6 3.9 gather_fusion
  13.5 0.8 collective-permute-start
  14.3 0.6 copy-done.11
  14.9 4.9 gather_fusion.1
  19.9 3.9 collective-permute-start.1
  23.8 1.3 collective-permute-done
  25.1 5.4 collective-permute-done.1
  30.5 1.5 pad_maximum_fusion
  32.0 100.1 %scatter_custom_fusion = f32[2048,256]{1,0:T(8,128)S(1)} fusion(s32[8192]{0:T(1024)} %param.14, f32[8192]{0:T(1024)S(1)} %copy-done.5, f32[]{:T(128)} %constant.6.clone.1, bf16[4096,256]{1,0:T(8,128)(2,1)} %pad_maximum_fusion, s32[8192]{0:T(1024)S(1)} %fusion.32), kind=kCustom, calls=%fused_computation.21 | custom fusion | flops 6291456 | bytes 4260352 | tf_op jit(solution)/shard_map/scatter-add | solution.py:22
  132.0 1.3 copy-done.1
  133.4 0.5 convolution_convert_fusion.1
  133.9 0.5 copy.30
  134.4 4.4 gather_fusion.3
  138.8 4.4 gather_fusion.2
  143.3 0.2 copy.31
  143.4 0.2 copy.33
  143.6 3.8 collective-permute-start.3
  147.5 1.4 fusion.33
  148.8 5.4 collective-permute-done.3
  154.2 3.0 collective-permute-done.2
  157.2 0.1 pad_maximum_fusion.1
  157.4 2.5 copy.34
  159.8 99.9 %scatter_custom_fusion.1 = f32[2048,172]{1,0:T(8,128)S(1)} fusion(s32[8192]{0:T(1024)} %param.14, f32[8192]{0:T(1024)S(1)} %copy-done.5, f32[]{:T(128)} %constant.6.clone.1, bf16[4096,172]{1,0:T(8,128)(2,1)} %copy.34, s32[8192]{0:T(1024)S(1)} %copy-done.9), kind=kCustom, calls=%fused_computation.18 | custom fusion | flops 4227072 | bytes 3572224 | tf_op jit(solution)/shard_map/scatter-add | solution.py:22
  259.7 0.0 copy-start.12
  259.7 0.0 copy-start.15
  259.8 0.3 reduce_max.9
  260.1 0.3 copy-done.12
  260.4 1.3 select_reduce_fusion
  261.7 0.6 convert_reduce_fusion
  262.3 31.9 %all-reduce = (f32[]{:T(128)}, f32[]{:T(128)}) all-reduce(f32[]{:T(128)} %get-tuple-element.18, f32[]{:T(128)} %get-tuple-element.17), channel_id=1, replica_groups=mesh['graph'=16] {'graph'}, use_global_device_ids=true, to_apply=%region_6.0 | all-reduce | flops 2 | bytes 16 | tf_op jit(solution)/shard_map/psum | solution.py:47
  294.9 2.7 subtract_multiply_fusion
  297.6 95.2 %scatter_custom_fusion.2 = f32[4096,172]{1,0:T(8,128)} fusion(s32[8192]{0:T(1024)} %param.13, f32[8192]{0:T(1024)S(1)} %copy-done.5, f32[]{:T(128)} %constant.6.clone.1, f32[2048,172]{1,0:T(8,128)} %subtract_multiply_fusion, s32[8192]{0:T(1024)S(1)} %copy-done.6), kind=kCustom, calls=%fused_computation.16 | custom fusion | flops 2818048 | bytes 4981248 | tf_op jit(solution)/shard_map/scatter-add | solution.py:27
  392.8 1.7 fusion.41
  394.5 0.3 copy.35
  394.8 0.3 copy.36
  395.1 0.1 collective-permute-start.5
  395.2 3.5 collective-permute-start.4
  398.7 0.8 slice_bitcast_fusion.1
  399.5 0.6 compare_select_fusion.3
  400.1 13.7 %collective-permute-done.5 = f32[1024,172]{0,1:T(8,128)S(1)} collective-permute-done((f32[1024,172]{0,1:T(8,128)S(1)}, f32[1024,172]{0,1:T(8,128)S(1)}, u32[]{:S(2)}, u32[]{:S(2)}) %collective-permute-start.5) | collective-permute-done | bytes 704544 | tf_op jit(solution)/shard_map/ppermute | solution.py:29
  413.8 1.3 pad_maximum_fusion.2
  415.1 2.9 copy.37
  418.0 13.0 %scatter_fusion = f32[2048,172]{1,0:T(8,128)S(1)} fusion(f32[2048,172]{1,0:T(8,128)S(1)} %slice-done, s32[2048]{0:T(1024)S(1)} %bitcast.15, f32[2048,172]{1,0:T(8,128)} %copy.37), kind=kCustom, calls=%fused_computation.11 | custom fusion | flops 352256 | bytes 4235264 | tf_op jit(solution)/shard_map/scatter-add | solution.py:31
  431.1 0.0 copy-start.7
  431.1 3.4 compare_select_fusion
  434.4 95.2 %scatter_custom_fusion.4 = f32[4096,256]{1,0:T(8,128)} fusion(s32[8192]{0:T(1024)} %param.13, f32[8192]{0:T(1024)S(1)} %copy-done.5, f32[]{:T(128)} %constant.6.clone.1, f32[2048,256]{1,0:T(8,128)} %compare_select_fusion, s32[8192]{0:T(1024)S(1)} %copy-done.7), kind=kCustom, calls=%fused_computation.14 | custom fusion | flops 4194304 | bytes 6357504 | tf_op jit(solution)/shard_map/scatter-add | solution.py:27
  529.7 1.8 fusion.40
  531.5 3.4 collective-permute-start.6
  534.9 1.5 slice.57
  536.4 0.9 copy-done.2
  537.2 1.2 fusion.23
  538.5 19.0 %collective-permute-done.6 = f32[1024,256]{1,0:T(8,128)} collective-permute-done((f32[1024,256]{1,0:T(8,128)S(1)}, f32[1024,256]{1,0:T(8,128)}, u32[]{:S(2)}, u32[]{:S(2)}) %collective-permute-start.6) | collective-permute-done | bytes 1048608 | tf_op jit(solution)/shard_map/ppermute | solution.py:28
  557.5 1.4 collective-permute-done.7
  558.9 15.2 %scatter_custom_fusion.5 = f32[2048,256]{1,0:T(8,128)} fusion(f32[2048,256]{1,0:T(8,128)} %slice.57, s32[2048]{0:T(1024)S(1)} %bitcast.16, f32[1024,256]{1,0:T(8,128)} %collective-permute-done.7, f32[]{:T(128)} %constant.10.clone.1, f32[1024,256]{1,0:T(8,128)} %collective-permute-done.6), kind=kCustom, calls=%fused_computation.31 | custom fusion | flops 1048576 | bytes 4194816 | tf_op jit(solution)/shard_map/scatter-add | solution.py:31
  574.1 2.7 convolution_bitcast_fusion
  576.8 0.0 all-reduce.4.cloned.1.call-update
  577.4 65.4 %all-reduce.4.cloned.1.call-done = (f32[128,256]{0,1:T(8,128)}, f32[256,172]{0,1:T(8,128)}) async-done(((f32[128,256]{0,1:T(8,128)}, f32[256,172]{0,1:T(8,128)}), (f32[128,256]{0,1:T(8,128)}, f32[256,172]{0,1:T(8,128)})) %all-reduce.4.cloned.1.call-update) | async-done | bytes 307216 | tf_op jit(solution)/shard_map/psum | solution.py:54
  642.8 1.7 copy.38
  644.5 1.6 copy.43
  (33 shorter events, 0.1 us)
Async XLA Ops:
  7.2 1.1 copy-start
  7.2 635.7 %all-reduce.4.cloned.1.call-start = ((), (), s32[]{:S(2)}) async-start(), calls=%async_computation | async-start | bytes 622592 | tf_op jit(solution)/shard_map/psum | solution.py:54
  8.2 1.3 copy-start.10
  13.5 11.5 %collective-permute-start = (bf16[1024,256]{1,0:T(8,128)(2,1)S(1)}, bf16[1024,256]{1,0:T(8,128)(2,1)S(1)}, u32[]{:S(2)}, u32[]{:S(2)}) collective-permute-start(bf16[1024,256]{1,0:T(8,128)(2,1)S(1)} %gather_fusion), channel_id=1, source_target_pairs={{0,1},{1,2},{2,3},{3,4},{4,5},{5,6},{6,7},{7,8},{8,9},{9,10},{10,1... | collective-permute-start | bytes 1572872 | tf_op jit(solution)/shard_map/ppermute | solution.py:17
  14.3 0.6 copy-start.11
  14.9 8.9 %copy-start.14 = (s32[8192]{0:T(1024)S(1)}, s32[8192]{0:T(1024)}, u32[]{:S(2)}) copy-start(s32[8192]{0:T(1024)} %param.13) | copy-start | bytes 98308
  19.9 10.6 %collective-permute-start.1 = (bf16[1024,256]{1,0:T(8,128)(2,1)}, bf16[1024,256]{1,0:T(8,128)(2,1)S(1)}, u32[]{:S(2)}, u32[]{:S(2)}) collective-permute-start(bf16[1024,256]{1,0:T(8,128)(2,1)} %gather_fusion.1), channel_id=1, source_target_pairs={{0,15},{1,0},{2,1},{3,2},{4,3},{5,4},{6,5},{7,6},{8,7},{9,8},{10,9... | collective-permute-start | bytes 1572872 | tf_op jit(solution)/shard_map/ppermute | solution.py:18
  23.8 8.2 %copy-start.8 = (s32[8192]{0:T(1024)}, s32[8192]{0:T(1024)S(1)}, u32[]{:S(2)}) copy-start(s32[8192]{0:T(1024)S(1)} %fusion.32) | copy-start | bytes 98308
  23.8 8.1 %copy-start.5 = (f32[8192]{0:T(1024)S(1)}, f32[8192]{0:T(1024)}, u32[]{:S(2)}) copy-start(f32[8192]{0:T(1024)} %param.15) | copy-start | bytes 98308
  32.0 101.4 %copy-start.4 = (f32[256,172]{0,1:T(8,128)S(1)}, f32[256,172]{0,1:T(8,128)}, u32[]{:S(2)}) copy-start(f32[256,172]{0,1:T(8,128)} %param.11) | copy-start | bytes 528388
  132.0 1.3 copy-start.1
  143.6 10.6 %collective-permute-start.3 = (bf16[1024,172]{0,1:T(8,128)(2,1)S(1)}, bf16[1024,172]{0,1:T(8,128)(2,1)S(1)}, u32[]{:S(2)}, u32[]{:S(2)}) collective-permute-start(bf16[1024,172]{0,1:T(8,128)(2,1)S(1)} %copy.33), channel_id=1, source_target_pairs={{0,15},{1,0},{2,1},{3,2},{4,3},{5,4},{6,5},{7,6},{8,7},{9,8},{10,9... | collective-permute-start | bytes 1056776 | tf_op jit(solution)/shard_map/ppermute | solution.py:18
  147.5 9.8 %collective-permute-start.2 = (bf16[1024,172]{0,1:T(8,128)(2,1)S(1)}, bf16[1024,172]{0,1:T(8,128)(2,1)S(1)}, u32[]{:S(2)}, u32[]{:S(2)}) collective-permute-start(bf16[1024,172]{0,1:T(8,128)(2,1)S(1)} %copy.31), channel_id=1, source_target_pairs={{0,1},{1,2},{2,3},{3,4},{4,5},{5,6},{6,7},{7,8},{8,9},{9,10},{10,1... | collective-permute-start | bytes 1056776 | tf_op jit(solution)/shard_map/ppermute | solution.py:17
  157.3 2.5 copy-start.9
  259.7 0.7 copy-start.12
  259.7 2.0 copy-start.15
  294.9 2.7 copy-start.6
  395.1 18.6 %collective-permute-start.5 = (f32[1024,172]{0,1:T(8,128)S(1)}, f32[1024,172]{0,1:T(8,128)S(1)}, u32[]{:S(2)}, u32[]{:S(2)}) collective-permute-start(f32[1024,172]{0,1:T(8,128)S(1)} %copy.36), channel_id=1, source_target_pairs={{0,1},{1,2},{2,3},{3,4},{4,5},{5,6},{6,7},{7,8},{8,9},{9,10},{10,1... | collective-permute-start | bytes 2113544 | tf_op jit(solution)/shard_map/ppermute | solution.py:29
  395.2 18.6 %collective-permute-start.4 = (f32[1024,172]{0,1:T(8,128)S(1)}, f32[1024,172]{0,1:T(8,128)S(1)}, u32[]{:S(2)}, u32[]{:S(2)}) collective-permute-start(f32[1024,172]{0,1:T(8,128)S(1)} %copy.35), channel_id=1, source_target_pairs={{0,15},{1,0},{2,1},{3,2},{4,3},{5,4},{6,5},{7,6},{8,7},{9,8},{10,9... | collective-permute-start | bytes 2113544 | tf_op jit(solution)/shard_map/ppermute | solution.py:28
  415.1 2.9 slice-start
  415.1 2.9 copy-start.13
  431.1 3.4 copy-start.7
  529.7 5.2 copy-start.3
  531.5 26.0 %collective-permute-start.6 = (f32[1024,256]{1,0:T(8,128)S(1)}, f32[1024,256]{1,0:T(8,128)}, u32[]{:S(2)}, u32[]{:S(2)}) collective-permute-start(f32[1024,256]{1,0:T(8,128)S(1)} %get-tuple-element.24), channel_id=1, source_target_pairs={{0,15},{1,0},{2,1},{3,2},{4,3},{5,4},{6,5},{7,6},{8,7},{9,8},{10,9... | collective-permute-start | bytes 3145736 | tf_op jit(solution)/shard_map/ppermute | solution.py:28
  534.9 2.3 copy-start.2
  534.9 24.0 %collective-permute-start.7 = (f32[1024,256]{1,0:T(8,128)S(1)}, f32[1024,256]{1,0:T(8,128)}, u32[]{:S(2)}, u32[]{:S(2)}) collective-permute-start(f32[1024,256]{1,0:T(8,128)S(1)} %get-tuple-element.25), channel_id=1, source_target_pairs={{0,1},{1,2},{2,3},{3,4},{4,5},{5,6},{6,7},{7,8},{8,9},{9,10},{10,1... | collective-permute-start | bytes 3145736 | tf_op jit(solution)/shard_map/ppermute | solution.py:29
Sparse Core Ops, SparseCore 0:
  577.0 65.8 all-reduce.3
where the time goes:
time: 657 us; the launch traced here: 654 us
  other arithmetic  429 us (65%)
  waiting for transfers between devices  115 us (18%)
  local copies, waits for them, and re-layouts  37.1 us (6%)
  blocking collectives  31.9 us (5%)
  between operations  16.7 us (3%)
  starting transfers between devices  15.5 us (2%)
  matrix products  9.14 us (1%)
    scatter-add x2, other arithmetic, aggregate(): jax.ops.segment_sum(edge_w[:, None] * ext_table[edge_src], edge_dst, num_...  200 us
    scatter-add x2, other arithmetic, scatter_back(): jax.ops.segment_sum(edge_w[:, None] * grad_rows[edge_dst], edge_src, num_...  190 us
    psum x1, waiting for transfers between devices, device_step(): lax.psum(lax.dot_general(node_feats, d_tab_one, CONTRACT_ROWS, preferred_...  65.4 us
    psum x1, blocking collectives, device_step(): lax.psum(jnp.sum(mask_f * (log_norm - picked)), GRAPH_AXIS) / label_count  31.9 us
    scatter-add x2, other arithmetic, scatter_back(): ext_grad[:rows_loc].at[row_ids]  28.2 us
    ppermute x2, waiting for transfers between devices, scatter_back(): lax.ppermute(ext_grad[rows_loc:rows_loc + halo_rows], GRAPH_AXIS, to_prev)  19 us
    ppermute x2, waiting for transfers between devices, scatter_back(): lax.ppermute(ext_grad[rows_loc + halo_rows:], GRAPH_AXIS, to_next)  15.1 us
  transfers between devices with their start and end apart: 9, of which 8 were waited for; matrix products, arithmetic and copies ran while one was open for 2% of the time, Pallas kernels for 0%

commit v1 on v0

v1 whole, which is shorter than its diff:
```python
import functools

import jax
import jax.numpy as jnp
from jax import lax
from jax.experimental import pallas as pl
from jax.experimental.pallas import tpu as pltpu
from jax.sharding import PartitionSpec as P

AXIS = "graph"
LANES = 128
ROWS_A = (((0,), (0,)), ((), ()))
COLS_A = (((1,), (1,)), ((), ()))
F32, BF16 = jnp.float32, jnp.bfloat16
VMEM = pl.BlockSpec(memory_space=pltpu.VMEM)
SMEM = pl.BlockSpec(memory_space=pltpu.SMEM)
STEP = 512


def dot(a, b, dims=(((1,), (0,)), ((), ()))):
    return lax.dot_general(a, b, dims, preferred_element_type=F32)


def fill_zero(ref):
    zero = jnp.zeros((STEP, LANES), F32)

    @pl.loop(0, ref.shape[0], step=STEP)
    def _(i):
        ref[pl.ds(i, STEP), :] = zero


def copy_in(dst, src):
    @pl.loop(0, dst.shape[0], step=STEP)
    def _(i):
        dst[pl.ds(i, STEP), :] = src[pl.ds(i, STEP), :].astype(F32)


def walk_edges(first, last, chunk, from_idx, to_idx, w, table, accs):
    group = len(accs)

    def body(c, _):
        base = c * chunk
        for g in range(0, chunk, group):
            pend = []
            for u in range(group):
                k = base + g + u
                s = pl.multiple_of(from_idx[k], 2)
                d = pl.multiple_of(to_idx[k], 2)
                pend.append((d, accs[u][pl.ds(d, 2), :] + table[pl.ds(s, 2), :] * w[k]))
            for u in range(group):
                accs[u][pl.ds(pend[u][0], 2), :] = pend[u][1]
        return 0

    lax.fori_loop(first, last, body, 0)


def gather_rows(idx, which, table, buf, chunk=32):
    @pl.loop(0, idx.shape[1] // chunk)
    def _(c):
        for u in range(chunk):
            j = c * chunk + u
            s = pl.multiple_of(idx[which, j] * 2, 2)
            buf[pl.ds(pl.multiple_of(j * 2, 2), 2), :] = table[pl.ds(s, 2), :]


def return_rows(idx, which, vals, accs, chunk=32):
    group = len(accs)

    @pl.loop(0, idx.shape[1] // chunk)
    def _(c):
        for g in range(0, chunk, group):
            pend = []
            for u in range(group):
                j = c * chunk + g + u
                d = pl.multiple_of(idx[which, j] * 2, 2)
                pend.append((d, accs[u][pl.ds(d, 2), :] + vals[pl.ds(pl.multiple_of(j * 2, 2), 2), :]))
            for u in range(group):
                accs[u][pl.ds(pend[u][0], 2), :] = pend[u][1]


def send_halo(idx, table, buf, prev_out, next_out):
    gather_rows(idx, 0, table, buf)
    prev_out[...] = buf[...].astype(BF16)
    gather_rows(idx, 1, table, buf)
    next_out[...] = buf[...].astype(BF16)


def halves(accs, i, n):
    even = functools.reduce(jnp.add, [a[pl.ds(2 * i, n, stride=2), :] for a in accs])
    odd = functools.reduce(jnp.add, [a[pl.ds(2 * i + 1, n, stride=2), :] for a in accs])
    return even, odd


def put_halves(table, i, n, even, odd):
    table[pl.ds(2 * i, n, stride=2), :] = even
    table[pl.ds(2 * i + 1, n, stride=2), :] = odd


def first_kernel(x, w1, send, tab, to_prev, to_next, buf):
    rows = x.shape[0]
    w = w1[...].astype(BF16)

    @pl.loop(0, rows, step=256)
    def _(i):
        t = dot(x[pl.ds(i, 256), :], w).astype(BF16).astype(F32)
        put_halves(tab, i, 256, t[:, :LANES], t[:, LANES:])

    send_halo(send, tab, buf, to_prev, to_next)


def local_kernel(chunk, n_acc, counts, from_idx, to_idx, w, table, out, *accs):
    for a in accs:
        fill_zero(a)
    walk_edges(0, (counts[0] + chunk - 1) // chunk, chunk, from_idx, to_idx, w, table, accs)

    @pl.loop(0, out.shape[0], step=STEP)
    def _(i):
        out[pl.ds(i, STEP), :] = functools.reduce(jnp.add, [a[pl.ds(i, STEP), :] for a in accs])


def halo_range(counts, chunk):
    return counts[0] // chunk, (counts[0] + counts[1] + chunk - 1) // chunk


def forward_halo(chunk, counts, src, dst, w, from_prev, from_next, part, htab, accs):
    half = from_prev.shape[0]
    copy_in(htab.at[pl.ds(0, half)], from_prev)
    copy_in(htab.at[pl.ds(half, half)], from_next)
    copy_in(accs[0], part)
    for a in accs[1:]:
        fill_zero(a)
    first, last = halo_range(counts, chunk)
    walk_edges(first, last, chunk, src, dst, w, htab, accs)


def backward_halo(chunk, counts, src, dst, w, grad, back_prev, back_next, accs):
    for a in accs:
        fill_zero(a)
    first, last = halo_range(counts, chunk)
    walk_edges(first, last, chunk, dst, src, w, grad, accs)
    half = back_prev.shape[0]

    @pl.loop(0, half, step=STEP)
    def _(i):
        back_prev[pl.ds(i, STEP), :] = functools.reduce(jnp.add, [a[pl.ds(i, STEP), :] for a in accs])
        back_next[pl.ds(i, STEP), :] = functools.reduce(jnp.add, [a[pl.ds(half + i, STEP), :] for a in accs])


def hidden_kernel(chunk, counts, src, dst, w, send, from_prev, from_next, part, w2, hid, tab, to_prev, to_next, htab, buf, *accs):
    forward_halo(chunk, counts, src, dst, w, from_prev, from_next, part, htab, accs)

    @pl.loop(0, hid.shape[0], step=256)
    def _(i):
        even, odd = halves(accs, i, 256)
        h = jnp.concatenate([jnp.maximum(even, 0.0), jnp.maximum(odd, 0.0)], axis=1).astype(BF16)
        hid[pl.ds(i, 256), :] = h
        t = dot(h, w2[...]).astype(BF16).astype(F32)
        put_halves(tab, i, 256, t[:, :LANES], t[:, LANES:])

    send_halo(send, tab, buf, to_prev, to_next)


def spread(row):
    return jnp.transpose(jnp.broadcast_to(row, (LANES, LANES)))


def loss_kernel(chunk, classes, counts, src, dst, w, inv_count, from_prev, from_next, part, labels, mask, loss, grad, back_prev, back_next, htab, *accs):
    forward_halo(chunk, counts, src, dst, w, from_prev, from_next, part, htab, accs)
    lane = lax.broadcasted_iota(jnp.int32, (LANES, LANES), 1)
    live = lane < classes - LANES
    scale = inv_count[0, 0]
    loss[...] = jnp.zeros_like(loss)

    @pl.loop(0, labels.shape[0])
    def _(b):
        even, odd = halves(accs, b * LANES, LANES)
        label = spread(labels[pl.ds(b, 1), :])
        keep = spread(mask[pl.ds(b, 1), :])
        odd = jnp.where(live, odd, -jnp.inf)
        top = jnp.max(jnp.maximum(even, odd), axis=1, keepdims=True)
        total = jnp.sum(jnp.exp(even - top) + jnp.exp(odd - top), axis=1, keepdims=True)
        norm = top + jnp.log(total)
        hit_even, hit_odd = lane == label, lane + LANES == label
        picked = jnp.where(hit_even, even, 0.0) + jnp.where(hit_odd, odd, 0.0)
        per_row = jnp.where(lane == 0, norm, 0.0) - picked
        loss[...] += jnp.sum((keep * per_row).reshape(LANES // 8, 8, LANES), axis=0)
        d_even = (jnp.exp(even - norm) - hit_even.astype(F32)) * (keep * scale)
        d_odd = (jnp.exp(odd - norm) - hit_odd.astype(F32)) * (keep * scale)
        put_halves(grad, b * LANES, LANES, d_even, d_odd)

    backward_halo(chunk, counts, src, dst, w, grad, back_prev, back_next, accs)


def take_returns(send, part, got_prev, got_next, accs):
    copy_in(accs[0], part)
    for a in accs[1:]:
        fill_zero(a)
    return_rows(send, 1, got_prev, accs)
    return_rows(send, 0, got_next, accs)


def middle_kernel(chunk, counts, src, dst, w, send, got_prev, got_next, part, hid, w2, grad_two, grad, back_prev, back_next, *accs):
    take_returns(send, part, got_prev, got_next, accs)
    grad_two[...] = jnp.zeros_like(grad_two)

    @pl.loop(0, hid.shape[0], step=256)
    def _(i):
        even, odd = halves(accs, i, 256)
        d_tab = jnp.concatenate([even, odd], axis=1).astype(BF16)
        h = hid[pl.ds(i, 256), :]
        grad_two[...] += dot(h, d_tab, ROWS_A)
        d_hid = dot(d_tab, w2[...], COLS_A)
        d_pre = jnp.where(h > 0, d_hid, 0.0)
        put_halves(grad, i, 256, d_pre[:, :LANES], d_pre[:, LANES:])

    backward_halo(chunk, counts, src, dst, w, grad, back_prev, back_next, accs)


def last_kernel(send, got_prev, got_next, part, x, grad_one, *accs):
    take_returns(send, part, got_prev, got_next, accs)
    grad_one[...] = jnp.zeros_like(grad_one)

    @pl.loop(0, x.shape[0], step=256)
    def _(i):
        even, odd = halves(accs, i, 256)
        d_tab = jnp.concatenate([even, odd], axis=1).astype(BF16)
        grad_one[...] += dot(x[pl.ds(i, 256), :], d_tab, ROWS_A)


def call(body, name, outs, ins, scratch, flops=10**9):
    return pl.pallas_call(
        body, name=name, out_shape=outs, in_specs=ins, out_specs=jax.tree.map(lambda _: VMEM, outs),
        scratch_shapes=[pltpu.VMEM(s, F32) for s in scratch],
        compiler_params=pltpu.CompilerParams(vmem_limit_bytes=60 * 2**20),
        cost_estimate=pl.CostEstimate(flops=flops, bytes_accessed=8 * 2**20, transcendentals=0),
    )


def solution(mesh):
    num_dev = mesh.shape[AXIS]
    to_next = [(d, (d + 1) % num_dev) for d in range(num_dev)]
    to_prev = [(d, (d - 1) % num_dev) for d in range(num_dev)]

    def step(x, w_one, w_two, send, edge_src, edge_dst, edge_w, labels, mask):
        rows, halo, edges, classes = x.shape[0], send.shape[1], edge_src.shape[0], w_two.shape[1]
        tab = (2 * rows, LANES)
        half = (2 * halo, LANES)
        sds = jax.ShapeDtypeStruct
        tab_f, half_f, half_b = sds(tab, F32), sds(half, F32), sds(half, BF16)
        chunk_l, chunk_h = 64, 32
        w2 = jnp.pad(w_two, ((0, 0), (0, 2 * LANES - classes))).astype(BF16)
        mask_f = mask.astype(F32)

        tab_one, to_p, to_n = call(first_kernel, "first", [tab_f, half_b, half_b], [VMEM, VMEM, SMEM], [half])(x, w_one, send)
        from_prev = lax.ppermute(to_n, AXIS, to_next)
        from_next = lax.ppermute(to_p, AXIS, to_prev)

        kind = jnp.where(edge_w == 0.0, 2, (edge_src >= rows).astype(jnp.int32))
        key = (kind << 23) | (edge_src << 11) | edge_dst
        key, w = lax.sort((key, edge_w), num_keys=1, is_stable=False)
        kind, src, dst = key >> 23, (key >> 11) & 4095, (key & 2047) * 2
        is_local, is_halo = kind == 0, kind == 1
        src_l, w_l = jnp.where(is_local, src * 2, 0), jnp.where(is_local, w, 0.0)
        src_h, w_h = jnp.where(is_halo, (src - rows) * 2, 0), jnp.where(is_halo, w, 0.0)
        counts = jnp.stack([jnp.sum(is_local.astype(jnp.int32)), jnp.sum(is_halo.astype(jnp.int32))])
        label_count = jnp.maximum(lax.psum(jnp.sum(mask_f), AXIS), 1.0)

        walk_l = [SMEM, SMEM, SMEM, SMEM]
        local = call(functools.partial(local_kernel, chunk_l, 4), "local_edges", tab_f, walk_l + [VMEM], [tab] * 4, 10**10)
        part = local(counts, src_l, dst, w_l, tab_one)
        hid, tab_two, to_p, to_n = call(
            functools.partial(hidden_kernel, chunk_h), "hidden", [sds((rows, 2 * LANES), BF16), tab_f, half_b, half_b],
            walk_l + [SMEM] + [VMEM] * 4, [tab, half] + [tab] * 4,
        )(counts, src_h, dst, w_h, send, from_prev, from_next, part, w2)
        from_prev = lax.ppermute(to_n, AXIS, to_next)
        from_next = lax.ppermute(to_p, AXIS, to_prev)
        part = local(counts, src_l, dst, w_l, tab_two)
        loss, grad, to_p, to_n = call(
            functools.partial(loss_kernel, chunk_h, classes), "loss", [sds((8, LANES), F32), tab_f, half_f, half_f],
            walk_l + [SMEM] + [VMEM] * 5, [tab] + [tab] * 4,
        )(counts, src_h, dst, w_h, (1.0 / label_count).reshape(1, 1), from_prev, from_next, part, labels.reshape(-1, LANES), mask_f.reshape(-1, LANES))
        got_prev = lax.ppermute(to_p, AXIS, to_prev)
        got_next = lax.ppermute(to_n, AXIS, to_next)
        part = local(counts, dst, src_l, w_l, grad)
        grad_two, grad, to_p, to_n = call(
            functools.partial(middle_kernel, chunk_h), "middle", [sds((2 * LANES, 2 * LANES), F32), tab_f, half_f, half_f],
            walk_l + [SMEM] + [VMEM] * 5, [tab] * 4,
        )(counts, src_h, dst, w_h, send, got_prev, got_next, part, hid, w2)
        got_prev = lax.ppermute(to_p, AXIS, to_prev)
        got_next = lax.ppermute(to_n, AXIS, to_next)
        part = local(counts, dst, src_l, w_l, grad)
        grad_one = call(last_kernel, "last", sds((x.shape[1], 2 * LANES), F32), [SMEM] + [VMEM] * 4, [tab] * 4)(send, got_prev, got_next, part, x)
        loss, grad_one, grad_two = lax.psum((jnp.sum(loss), grad_one, grad_two[:, :classes]), AXIS)
        return loss / label_count, grad_one, grad_two

    row = P(AXIS)
    return jax.shard_map(
        step, mesh=mesh, in_specs=(row, P(), P(), row, row, row, row, row, row), out_specs=(P(), P(), P()), check_vma=False
    )
```

time: 657 us -> 283 us (0.43)
  other arithmetic: 429 us -> 11.4 us
  Pallas kernels: 0 us -> 89.3 us
  waiting for transfers between devices: 115 us -> 70.8 us
  blocking collectives: 31.9 us -> 73.6 us
  local copies, waits for them, and re-layouts: 37.1 us -> 7.92 us
  matrix products: 9.14 us -> 0 us
    scatter-add x6 -> x0, other arithmetic: 419 us -> none  [the longest x2 200 us: aggregate(): jax.ops.segment_sum(edge_w[:, None] * ext_table[edge_src], edge_dst, num_...]
    pallas_call x0 -> x9, Pallas kernels: none -> 89.3 us  [the longest x2 16.3 us: step(): part = local(counts, dst, src_l, w_l, grad)]
    psum x1 -> x2, blocking collectives: 31.9 us -> 73.6 us  [the longest x1 40.3 us: step(): label_count = jnp.maximum(lax.psum(jnp.sum(mask_f), AXIS), 1.0)]
    psum x1, waiting for transfers between devices: 65.4 us -> 33 us  [step(): lax.psum((jnp.sum(loss), grad_one, grad_two[:, :classes]), AXIS)]
    gather x6 -> x0, local copies, waits for them, and re-layouts: 18.1 us -> none  [the longest x3 9.55 us: halo_extend(): from_next = lax.ppermute(node_table[send_rows[0]], GRAPH_AXIS, to_prev)]
    ppermute x8, waiting for transfers between devices: 49.1 us -> 37.8 us  [the longest x2 29 us: step(): got_prev = lax.ppermute(to_p, AXIS, to_prev)]
    dot_general x5 -> x0, matrix products: 9.14 us -> none  [the longest x1 3.36 us: device_step(): lax.dot_general(d_tab_two, w_two_b, CONTRACT_COLS, preferred_element_type...]
  transfers between devices with their start and end apart: 9 -> 9, of which waited for: 8 -> 7; matrix products, arithmetic and copies ran while one was open for 2% -> 4% of each run, Pallas kernels for 0% -> 11%
where the time goes in v1:
time: 283 us; the launch traced here: 285 us
  Pallas kernels  89.3 us (32%)
  blocking collectives  73.6 us (26%)
  waiting for transfers between devices  70.8 us (25%)
  between operations  16.6 us (6%)
  starting transfers between devices  15.7 us (6%)
  other arithmetic  11.4 us (4%)
  local copies, waits for them, and re-layouts  7.92 us (3%)
    psum x1, blocking collectives, step(): label_count = jnp.maximum(lax.psum(jnp.sum(mask_f), AXIS), 1.0)  40.3 us
    psum x1, blocking collectives, step(): lax.psum((jnp.sum(loss), grad_one, grad_two[:, :classes]), AXIS)  33.3 us
    psum x1, waiting for transfers between devices, step(): lax.psum((jnp.sum(loss), grad_one, grad_two[:, :classes]), AXIS)  33 us
    ppermute x2, waiting for transfers between devices, step(): got_prev = lax.ppermute(to_p, AXIS, to_prev)  29 us
    pallas_call x2, Pallas kernels, step(): part = local(counts, dst, src_l, w_l, grad)  16.3 us
    pallas_call x1, Pallas kernels, step(): call(functools.partial(middle_kernel, chunk_h), 'middle', [sds((2 * LANES...  13.8 us
    pallas_call x1, Pallas kernels, step(): call(functools.partial(hidden_kernel, chunk_h), 'hidden', [sds((rows, 2 *...  12.4 us
    pallas_call x1, Pallas kernels, step(): call(functools.partial(loss_kernel, chunk_h, classes), 'loss', [sds((8, L...  11.1 us
  transfers between devices with their start and end apart: 9, of which 7 were waited for; matrix products, arithmetic and copies ran while one was open for 4% of the time, Pallas kernels for 11%

profile of v1, /device:TPU:0, one launch (start us, length us, event | category | flops | bytes accessed | tf_op | source)
XLA Modules:
  0.0 285.4 jit_solution(13461140399864256928)
XLA Ops:
  7.2 0.0 copy-start.6
  7.2 0.0 copy-start.5
  7.2 0.0 copy-start.7
  7.2 0.0 copy-start.8
  7.2 0.0 all-reduce.4.cloned.1.call-start
  7.3 9.1 %first.1 = (f32[4096,128]{1,0:T(8,128)}, bf16[2048,128]{1,0:T(8,128)(2,1)}, bf16[2048,128]{1,0:T(8,128)(2,1)}) custom-call(bf16[2048,128]{1,0:T(8,128)(2,1)} %x.5, f32[128,256]{1,0:T(8,128)} %w1.1, s32[2,1024]{1,0:T(2,128)} %send.7), custom_call_target="tpu_custom_call" | custom-call | flops 1000000000 | bytes 8388608 | tf_op jit(solution)/shard_map/first/pallas_call | solution.py:254
  16.3 0.7 collective-permute-start
  17.1 3.9 %collective-permute-start.1 = (bf16[2048,128]{1,0:T(8,128)(2,1)}, bf16[2048,128]{1,0:T(8,128)(2,1)S(1)}, u32[]{:S(2)}, u32[]{:S(2)}) collective-permute-start(bf16[2048,128]{1,0:T(8,128)(2,1)} %get-tuple-element.23), channel_id=1, source_target_pairs={{0,15},{1,0},{2,1},{3,2},{4,3},{5,4},{6,5},{7,6},{8,7},{9,8},{10,9... | collective-permute-start | bytes 1572872 | tf_op jit(solution)/shard_map/ppermute | solution.py:256
  21.0 0.0 copy-done.6
  21.0 0.6 convert_reduce_fusion.2
  21.6 0.0 copy-done.5
  21.6 0.0 copy-done.7
  21.6 0.0 copy-done.8
  21.6 5.7 %sort.15 = (s32[8192]{0:T(1024)S(1)}, f32[8192]{0:T(1024)S(1)}) sort(s32[8192]{0:T(1024)S(1)} %or_or_fusion, f32[8192]{0:T(1024)S(1)} %copy-done.5), dimensions={0}, to_apply=%region_0.1 | sort | flops 106496 | bytes 131072 | tf_op jit(solution)/shard_map/sort | solution.py:260
  27.3 1.3 multiply_select_fusion
  28.6 0.6 broadcast_select_fusion
  29.2 2.0 pad_add_fusion.counts
  31.2 0.0 copy-start.4
  31.2 8.3 %local_edges.4.part = f32[4096,128]{1,0:T(8,128)} custom-call(s32[2]{0:T(128)} %pad_add_fusion.counts, s32[8192]{0:T(1024)} %get-tuple-element.49.from_idx.to_idx, s32[8192]{0:T(1024)} %get-tuple-element.50.to_idx.dst.from_idx, f32[8192]{0:T(1024)} %get-tuple-element.47.w, f32[4096,128]{1,0:T(8,128)} %get-tuple-element.24.table), custom_call_target="tpu_custom_call" | custom-call | flops 10000000000 | bytes 8388608 | tf_op jit(solution)/shard_map/local_edges/pallas_call | solution.py:270
  39.5 40.3 %psum.28 = f32[]{:T(128)} all-reduce(f32[]{:T(128)} %convert_reduce_fusion.2), channel_id=1, replica_groups=mesh['graph'=16] {'graph'}, use_global_device_ids=true, to_apply=%region_4.5 | all-reduce | flops 1 | bytes 8 | tf_op jit(solution)/shard_map/psum | solution.py:266
  80.5 0.0 copy-done.4
  80.5 0.1 copy.14
  80.6 0.7 pad.5.w2
  81.3 0.6 convert_bitcast_fusion.mask
  81.9 0.0 collective-permute-done.from_prev
  81.9 0.0 copy-start.10
  81.9 0.0 collective-permute-done.1.from_next
  81.9 0.0 copy-start.11
  81.9 0.8 copy-done.10
  82.7 0.2 copy-done.11
  82.8 12.4 %hidden.1 = (bf16[2048,256]{1,0:T(8,128)(2,1)}, f32[4096,128]{1,0:T(8,128)}, bf16[2048,128]{1,0:T(8,128)(2,1)}, bf16[2048,128]{1,0:T(8,128)(2,1)}) custom-call(s32[2]{0:T(128)} %pad_add_fusion.counts, s32[8192]{0:T(1024)} %get-tuple-element.51.src, s32[8192]{0:T(1024)} %get-tuple-element.50.to_idx.dst.from_idx, f32[8192]{0:T(1024)} %get-tuple-element.48.w, ...), custom_call_target="tpu_custom_call" | custom-call | flops 1000000000 | bytes 8388608 | tf_op jit(solution)/shard_map/hidden/pallas_call | solution.py:271
  95.2 0.0 collective-permute-start.2
  95.2 3.5 %collective-permute-start.3 = (bf16[2048,128]{1,0:T(8,128)(2,1)}, bf16[2048,128]{1,0:T(8,128)(2,1)S(1)}, u32[]{:S(2)}, u32[]{:S(2)}) collective-permute-start(bf16[2048,128]{1,0:T(8,128)(2,1)} %get-tuple-element.26), channel_id=1, source_target_pairs={{0,15},{1,0},{2,1},{3,2},{4,3},{5,4},{6,5},{7,6},{8,7},{9,8},{10,9... | collective-permute-start | bytes 1572872 | tf_op jit(solution)/shard_map/ppermute | solution.py:276
  98.8 8.2 %local_edges.5.part = f32[4096,128]{1,0:T(8,128)} custom-call(s32[2]{0:T(128)} %pad_add_fusion.counts, s32[8192]{0:T(1024)} %get-tuple-element.49.from_idx.to_idx, s32[8192]{0:T(1024)} %get-tuple-element.50.to_idx.dst.from_idx, f32[8192]{0:T(1024)} %get-tuple-element.47.w, f32[4096,128]{1,0:T(8,128)} %get-tuple-element.27.table), custom_call_target="tpu_custom_call" | custom-call | flops 10000000000 | bytes 8388608 | tf_op jit(solution)/shard_map/local_edges/pallas_call | solution.py:277
  106.9 1.9 collective-permute-done.2.from_prev
  108.9 0.0 copy-start.12
  108.9 0.6 collective-permute-done.3.from_next
  109.5 0.0 copy-start.13
  109.5 0.2 copy-done.12
  109.7 0.6 copy-done.13
  110.3 11.1 %loss.1 = (f32[8,128]{1,0:T(8,128)}, f32[4096,128]{1,0:T(8,128)}, f32[2048,128]{1,0:T(8,128)}, f32[2048,128]{1,0:T(8,128)}) custom-call(s32[2]{0:T(128)} %pad_add_fusion.counts, s32[8192]{0:T(1024)} %get-tuple-element.51.src, s32[8192]{0:T(1024)} %get-tuple-element.50.to_idx.dst.from_idx, f32[8192]{0:T(1024)} %get-tuple-element.48.w, ...), custom_call_target="tpu_custom_call" | custom-call | flops 1000000000 | bytes 8388608 | tf_op jit(solution)/shard_map/loss/pallas_call | solution.py:278
  121.4 5.2 %collective-permute-start.4 = (f32[2048,128]{1,0:T(8,128)}, f32[2048,128]{1,0:T(8,128)S(1)}, u32[]{:S(2)}, u32[]{:S(2)}) collective-permute-start(f32[2048,128]{1,0:T(8,128)} %get-tuple-element.29), channel_id=1, source_target_pairs={{0,15},{1,0},{2,1},{3,2},{4,3},{5,4},{6,5},{7,6},{8,7},{9,8},{10,9... | collective-permute-start | bytes 3145736 | tf_op jit(solution)/shard_map/ppermute | solution.py:282
  126.6 0.0 collective-permute-start.5
  126.6 8.1 %local_edges.6.part = f32[4096,128]{1,0:T(8,128)} custom-call(s32[2]{0:T(128)} %pad_add_fusion.counts, s32[8192]{0:T(1024)} %get-tuple-element.50.to_idx.dst.from_idx, s32[8192]{0:T(1024)} %get-tuple-element.49.from_idx.to_idx, f32[8192]{0:T(1024)} %get-tuple-element.47.w, f32[4096,128]{1,0:T(8,128)} %get-tuple-element.31.table), custom_call_target="tpu_custom_call" | custom-call | flops 10000000000 | bytes 8388608 | tf_op jit(solution)/shard_map/local_edges/pallas_call | solution.py:284
  134.8 15.3 %collective-permute-done.4.got_prev = f32[2048,128]{1,0:T(8,128)S(1)} collective-permute-done((f32[2048,128]{1,0:T(8,128)}, f32[2048,128]{1,0:T(8,128)S(1)}, u32[]{:S(2)}, u32[]{:S(2)}) %collective-permute-start.4) | collective-permute-done | bytes 1048608 | tf_op jit(solution)/shard_map/ppermute | solution.py:282
  150.1 2.5 collective-permute-done.5.got_next
  152.6 0.0 copy-done.2
  152.6 1.1 copy-done.3
  153.7 13.8 %middle.1 = (f32[256,256]{1,0:T(8,128)}, f32[4096,128]{1,0:T(8,128)}, f32[2048,128]{1,0:T(8,128)}, f32[2048,128]{1,0:T(8,128)}) custom-call(s32[2]{0:T(128)} %pad_add_fusion.counts, s32[8192]{0:T(1024)} %get-tuple-element.51.src, s32[8192]{0:T(1024)} %get-tuple-element.50.to_idx.dst.from_idx, f32[8192]{0:T(1024)} %get-tuple-element.48.w, s32[2,1024]{1,0:T(2,128)} %send.7, ...), custom_call_target="tpu_custom_call" | custom-call | flops 1000000000 | bytes 8388608 | tf_op jit(solution)/shard_map/middle/pallas_call | solution.py:285
  167.5 2.3 collective-permute-start.6
  169.8 0.0 collective-permute-start.7
  169.8 8.1 %local_edges.7.part = f32[4096,128]{1,0:T(8,128)} custom-call(s32[2]{0:T(128)} %pad_add_fusion.counts, s32[8192]{0:T(1024)} %get-tuple-element.50.to_idx.dst.from_idx, s32[8192]{0:T(1024)} %get-tuple-element.49.from_idx.to_idx, f32[8192]{0:T(1024)} %get-tuple-element.47.w, f32[4096,128]{1,0:T(8,128)} %get-tuple-element.35.table), custom_call_target="tpu_custom_call" | custom-call | flops 10000000000 | bytes 8388608 | tf_op jit(solution)/shard_map/local_edges/pallas_call | solution.py:291
  178.0 13.7 %collective-permute-done.6.got_prev = f32[2048,128]{1,0:T(8,128)S(1)} collective-permute-done((f32[2048,128]{1,0:T(8,128)}, f32[2048,128]{1,0:T(8,128)S(1)}, u32[]{:S(2)}, u32[]{:S(2)}) %collective-permute-start.6) | collective-permute-done | bytes 1048608 | tf_op jit(solution)/shard_map/ppermute | solution.py:289
  191.6 3.7 %collective-permute-done.7.got_next = f32[2048,128]{1,0:T(8,128)S(1)} collective-permute-done((f32[2048,128]{1,0:T(8,128)}, f32[2048,128]{1,0:T(8,128)S(1)}, u32[]{:S(2)}, u32[]{:S(2)}) %collective-permute-start.7) | collective-permute-done | bytes 1048608 | tf_op jit(solution)/shard_map/ppermute | solution.py:290
  195.4 0.0 copy-done
  195.4 1.0 copy-done.1
  196.4 10.1 %last.1 = f32[128,256]{1,0:T(8,128)} custom-call(s32[2,1024]{1,0:T(2,128)} %send.7, f32[2048,128]{1,0:T(8,128)} %copy-done, f32[2048,128]{1,0:T(8,128)} %copy-done.1, f32[4096,128]{1,0:T(8,128)} %local_edges.7.part, bf16[2048,128]{1,0:T(8,128)(2,1)} %x.5), custom_call_target="tpu_custom_call" | custom-call | flops 1000000000 | bytes 8388608 | tf_op jit(solution)/shard_map/last/pallas_call | solution.py:292
  206.6 0.0 all-reduce.4.cloned.1.call-update
  206.6 0.0 copy-done.9
  206.6 0.6 reduce_sum.39
  207.2 33.3 %psum.29 = f32[]{:T(128)} all-reduce(f32[]{:T(128)} %reduce_sum.39), channel_id=1, replica_groups=mesh['graph'=16] {'graph'}, use_global_device_ids=true, to_apply=%region_6.7 | all-reduce | flops 1 | bytes 8 | tf_op jit(solution)/shard_map/psum | solution.py:293
  241.1 33.0 %all-reduce.4.cloned.1.call-done = (f32[128,256]{1,0:T(8,128)}, f32[256,172]{1,0:T(8,128)}) async-done(((f32[128,256]{1,0:T(8,128)}, f32[256,172]{1,0:T(8,128)}), (f32[128,256]{1,0:T(8,128)}, f32[256,172]{1,0:T(8,128)})) %all-reduce.4.cloned.1.call-update) | async-done | bytes 307216 | tf_op jit(solution)/shard_map/psum | solution.py:293
  274.1 1.7 copy.15
  275.9 1.6 copy.18
  (7 shorter events, 0.0 us)
Async XLA Ops:
  7.2 13.8 %copy-start.6 = (s32[2048]{0:T(1024)S(1)}, s32[2048]{0:T(1024)}, u32[]{:S(2)}) copy-start(s32[2048]{0:T(1024)} %param.17) | copy-start | bytes 24580
  7.2 14.4 %copy-start.5 = (f32[8192]{0:T(1024)S(1)}, f32[8192]{0:T(1024)}, u32[]{:S(2)}) copy-start(f32[8192]{0:T(1024)} %param.15) | copy-start | bytes 98308
  7.2 14.4 %copy-start.7 = (s32[8192]{0:T(1024)S(1)}, s32[8192]{0:T(1024)}, u32[]{:S(2)}) copy-start(s32[8192]{0:T(1024)} %param.14) | copy-start | bytes 98308
  7.2 14.4 %copy-start.8 = (s32[8192]{0:T(1024)S(1)}, s32[8192]{0:T(1024)}, u32[]{:S(2)}) copy-start(s32[8192]{0:T(1024)} %param.13) | copy-start | bytes 98308
  7.2 266.9 %all-reduce.4.cloned.1.call-start = ((), (), s32[]{:S(2)}) async-start(), calls=%async_computation | async-start | bytes 786432 | tf_op jit(solution)/shard_map/psum | solution.py:293
  16.3 65.5 %collective-permute-start = (bf16[2048,128]{1,0:T(8,128)(2,1)}, bf16[2048,128]{1,0:T(8,128)(2,1)S(1)}, u32[]{:S(2)}, u32[]{:S(2)}) collective-permute-start(bf16[2048,128]{1,0:T(8,128)(2,1)} %get-tuple-element.22), channel_id=1, source_target_pairs={{0,1},{1,2},{2,3},{3,4},{4,5},{5,6},{6,7},{7,8},{8,9},{9,10},{10,1... | collective-permute-start | bytes 1572872 | tf_op jit(solution)/shard_map/ppermute | solution.py:255
  17.1 64.8 %collective-permute-start.1 = (bf16[2048,128]{1,0:T(8,128)(2,1)}, bf16[2048,128]{1,0:T(8,128)(2,1)S(1)}, u32[]{:S(2)}, u32[]{:S(2)}) collective-permute-start(bf16[2048,128]{1,0:T(8,128)(2,1)} %get-tuple-element.23), channel_id=1, source_target_pairs={{0,15},{1,0},{2,1},{3,2},{4,3},{5,4},{6,5},{7,6},{8,7},{9,8},{10,9... | collective-permute-start | bytes 1572872 | tf_op jit(solution)/shard_map/ppermute | solution.py:256
  31.2 49.3 %copy-start.4 = (f32[256,172]{0,1:T(8,128)S(1)}, f32[256,172]{0,1:T(8,128)}, u32[]{:S(2)}) copy-start(f32[256,172]{0,1:T(8,128)} %param.11) | copy-start | bytes 528388
  81.9 0.8 copy-start.10
  81.9 0.9 copy-start.11
  95.2 13.7 %collective-permute-start.2 = (bf16[2048,128]{1,0:T(8,128)(2,1)}, bf16[2048,128]{1,0:T(8,128)(2,1)S(1)}, u32[]{:S(2)}, u32[]{:S(2)}) collective-permute-start(bf16[2048,128]{1,0:T(8,128)(2,1)} %get-tuple-element.25), channel_id=1, source_target_pairs={{0,1},{1,2},{2,3},{3,4},{4,5},{5,6},{6,7},{7,8},{8,9},{9,10},{10,1... | collective-permute-start | bytes 1572872 | tf_op jit(solution)/shard_map/ppermute | solution.py:275
  95.2 14.3 %collective-permute-start.3 = (bf16[2048,128]{1,0:T(8,128)(2,1)}, bf16[2048,128]{1,0:T(8,128)(2,1)S(1)}, u32[]{:S(2)}, u32[]{:S(2)}) collective-permute-start(bf16[2048,128]{1,0:T(8,128)(2,1)} %get-tuple-element.26), channel_id=1, source_target_pairs={{0,15},{1,0},{2,1},{3,2},{4,3},{5,4},{6,5},{7,6},{8,7},{9,8},{10,9... | collective-permute-start | bytes 1572872 | tf_op jit(solution)/shard_map/ppermute | solution.py:276
  108.9 0.8 copy-start.12
  109.5 0.8 copy-start.13
  121.4 28.7 %collective-permute-start.4 = (f32[2048,128]{1,0:T(8,128)}, f32[2048,128]{1,0:T(8,128)S(1)}, u32[]{:S(2)}, u32[]{:S(2)}) collective-permute-start(f32[2048,128]{1,0:T(8,128)} %get-tuple-element.29), channel_id=1, source_target_pairs={{0,15},{1,0},{2,1},{3,2},{4,3},{5,4},{6,5},{7,6},{8,7},{9,8},{10,9... | collective-permute-start | bytes 3145736 | tf_op jit(solution)/shard_map/ppermute | solution.py:282
  126.6 26.0 %collective-permute-start.5 = (f32[2048,128]{1,0:T(8,128)}, f32[2048,128]{1,0:T(8,128)S(1)}, u32[]{:S(2)}, u32[]{:S(2)}) collective-permute-start(f32[2048,128]{1,0:T(8,128)} %get-tuple-element.30), channel_id=1, source_target_pairs={{0,1},{1,2},{2,3},{3,4},{4,5},{5,6},{6,7},{7,8},{8,9},{9,10},{10,1... | collective-permute-start | bytes 3145736 | tf_op jit(solution)/shard_map/ppermute | solution.py:283
  150.1 2.5 copy-start.2
  152.6 1.1 copy-start.3
  167.5 24.1 %collective-permute-start.6 = (f32[2048,128]{1,0:T(8,128)}, f32[2048,128]{1,0:T(8,128)S(1)}, u32[]{:S(2)}, u32[]{:S(2)}) collective-permute-start(f32[2048,128]{1,0:T(8,128)} %get-tuple-element.33), channel_id=1, source_target_pairs={{0,15},{1,0},{2,1},{3,2},{4,3},{5,4},{6,5},{7,6},{8,7},{9,8},{10,9... | collective-permute-start | bytes 3145736 | tf_op jit(solution)/shard_map/ppermute | solution.py:289
  169.8 25.6 %collective-permute-start.7 = (f32[2048,128]{1,0:T(8,128)}, f32[2048,128]{1,0:T(8,128)S(1)}, u32[]{:S(2)}, u32[]{:S(2)}) collective-permute-start(f32[2048,128]{1,0:T(8,128)} %get-tuple-element.34), channel_id=1, source_target_pairs={{0,1},{1,2},{2,3},{3,4},{4,5},{5,6},{6,7},{7,8},{8,9},{9,10},{10,1... | collective-permute-start | bytes 3145736 | tf_op jit(solution)/shard_map/ppermute | solution.py:290
  178.0 28.6 %copy-start.9 = (f32[8,128]{1,0:T(8,128)S(1)}, f32[8,128]{1,0:T(8,128)}, u32[]{:S(2)}) copy-start(f32[8,128]{1,0:T(8,128)} %get-tuple-element.28) | copy-start | bytes 12292
  191.6 3.7 %copy-start = (f32[2048,128]{1,0:T(8,128)}, f32[2048,128]{1,0:T(8,128)S(1)}, u32[]{:S(2)}) copy-start(f32[2048,128]{1,0:T(8,128)S(1)} %collective-permute-done.6.got_prev) | copy-start | bytes 3145732
  195.4 1.0 copy-start.1
Sparse Core Ops, SparseCore 0:
  206.7 67.3 all-reduce.3

commit v2 on v1

v2 whole, which is shorter than its diff:
```python
import functools

import jax
import jax.numpy as jnp
from jax import lax
from jax.experimental import pallas as pl
from jax.experimental.pallas import tpu as pltpu
from jax.sharding import PartitionSpec as P

AXIS = "graph"
LANES = 128
ROWS_A = (((0,), (0,)), ((), ()))
COLS_A = (((1,), (1,)), ((), ()))
F32, BF16 = jnp.float32, jnp.bfloat16
VMEM = pl.BlockSpec(memory_space=pltpu.VMEM)
SMEM = pl.BlockSpec(memory_space=pltpu.SMEM)
STEP = 512
PREP_CHUNK = 64
MESH = pl.DeviceIdType.MESH


def dot(a, b, dims=(((1,), (0,)), ((), ()))):
    return lax.dot_general(a, b, dims, preferred_element_type=F32)


def fill_zero(ref):
    zero = jnp.zeros((STEP, LANES), F32)

    @pl.loop(0, ref.shape[0], step=STEP)
    def _(i):
        ref[pl.ds(i, STEP), :] = zero


def copy_in(dst, src):
    @pl.loop(0, dst.shape[0], step=STEP)
    def _(i):
        dst[pl.ds(i, STEP), :] = src[pl.ds(i, STEP), :].astype(F32)


def walk_edges(first, last, chunk, from_idx, to_idx, w, table, accs):
    group = len(accs)

    def body(c, _):
        base = c * chunk
        for g in range(0, chunk, group):
            pend = []
            for u in range(group):
                k = base + g + u
                s = pl.multiple_of(from_idx[k], 2)
                d = pl.multiple_of(to_idx[k], 2)
                pend.append((d, accs[u][pl.ds(d, 2), :] + table[pl.ds(s, 2), :] * w[k]))
            for u in range(group):
                accs[u][pl.ds(pend[u][0], 2), :] = pend[u][1]
        return 0

    lax.fori_loop(first, last, body, 0)


def gather_rows(idx, line, table, out):
    lane = lax.broadcasted_iota(jnp.int32, (LANES, LANES), 1) * 2
    groups = table.shape[0] // LANES

    @pl.loop(0, out.shape[0] // 256)
    def _(c):
        hot = []
        for q in range(2):
            want = spread(idx[pl.ds(line + c * 2 + q, 1), :])
            hot.append(jnp.concatenate([jnp.where(want == lane + 2 * LANES * j, 1.0, 0.0).astype(BF16) for j in range(groups)], axis=1))
        out[pl.ds(pl.multiple_of(c * 256, 256), 256), :] = dot(jnp.concatenate(hot, axis=0), table[...]).astype(BF16)


def spread(row):
    return jnp.transpose(jnp.broadcast_to(row, (LANES, LANES)))


def return_rows(idx, start, vals, accs, chunk=32):
    group = len(accs)

    @pl.loop(0, vals.shape[0] // (2 * chunk))
    def _(c):
        block = vals.at[pl.ds(pl.multiple_of(c * 2 * chunk, 2 * chunk), 2 * chunk)]
        for g in range(0, chunk, group):
            pend = []
            for u in range(group):
                d = pl.multiple_of(idx[start + c * chunk + g + u], 2)
                pend.append((d, accs[u][pl.ds(d, 2), :] + block[2 * (g + u) : 2 * (g + u) + 2, :]))
            for u in range(group):
                accs[u][pl.ds(pend[u][0], 2), :] = pend[u][1]


def send_halo(idx, table, prev_out, next_out):
    gather_rows(idx, 0, table, prev_out)
    gather_rows(idx, idx.shape[0] // 2, table, next_out)


def halves(accs, i, n):
    even = functools.reduce(jnp.add, [a[pl.ds(2 * i, n, stride=2), :] for a in accs])
    odd = functools.reduce(jnp.add, [a[pl.ds(2 * i + 1, n, stride=2), :] for a in accs])
    return even, odd


def put_halves(table, i, n, even, odd):
    table[pl.ds(2 * i, n, stride=2), :] = even
    table[pl.ds(2 * i + 1, n, stride=2), :] = odd


def greet(n):
    me = lax.axis_index(AXIS)
    barrier = pltpu.get_barrier_semaphore()
    for o in range(1, n):
        pl.semaphore_signal(barrier, inc=1, device_id=(lax.rem(me + o, n),), device_id_type=MESH)
    return me, lambda: pl.semaphore_wait(barrier, n - 1)


def remote(src, dst, send_sem, recv_sem, peer):
    return pltpu.make_async_remote_copy(
        src_ref=src, dst_ref=dst, send_sem=send_sem, recv_sem=recv_sem, device_id=(peer,), device_id_type=MESH
    )


def first_kernel(n, x, w1, send, mask, tab, to_prev, to_next, count, tab_b, mine, theirs, send_sem, recv_sem):
    me, met = greet(n)
    rows = x.shape[0]
    mask_f = mask[...].astype(F32)
    mine[...] = jnp.sum(mask_f.reshape(-1, 8, LANES), axis=0)
    w = w1[...].astype(BF16)

    @pl.loop(0, rows, step=256)
    def _(i):
        t = dot(x[pl.ds(i, 256), :], w).astype(BF16)
        tab_b[pl.ds(i, 256), :] = t
        t = t.astype(F32)
        put_halves(tab, i, 256, t[:, :LANES], t[:, LANES:])

    met()
    copies = [remote(mine, theirs.at[o - 1], send_sem.at[o - 1], recv_sem.at[o - 1], lax.rem(me + o, n)) for o in range(1, n)]
    for c in copies:
        c.start()
    send_halo(send, tab_b, to_prev, to_next)
    for c in copies:
        c.wait()
    total = mine[...] + jnp.sum(theirs[...], axis=0)
    count[...] = jnp.maximum(jnp.broadcast_to(jnp.sum(total, keepdims=True), count.shape), 1.0)


def reduce_kernel(n, part, *refs):
    if len(refs) == 9:
        extra, count, out, mean, got, full, mine, sems, theirs = refs
    else:
        out, got, full, mine, sems = refs
        extra = None
    me, met = greet(n)
    rows = part.shape[0] // n
    met()
    peers = [lax.rem(me + o, n) for o in range(1, n)]
    scatter = [
        remote(part.at[pl.ds(pl.multiple_of(p * rows, 8), rows)], got.at[o], sems.at[0, o], sems.at[1, o], p) for o, p in enumerate(peers)
    ]
    for c in scatter:
        c.start()
    if extra is not None:
        spread_out = [remote(extra, theirs.at[o], sems.at[4, o], sems.at[5, o], p) for o, p in enumerate(peers)]
        for c in spread_out:
            c.start()
    for c in scatter:
        c.wait_recv()
    own = pl.ds(pl.multiple_of(me * rows, 8), rows)
    mine[...] = part[own, :] + jnp.sum(got[...], axis=0)
    if extra is not None:
        for c in spread_out:
            c.wait()
        total = jnp.sum(extra[...] + jnp.sum(theirs[...], axis=0), keepdims=True)
        mean[...] = jnp.broadcast_to(total, mean.shape) / count[...]
    gather = [remote(mine, full.at[own], sems.at[2, o], sems.at[3, o], p) for o, p in enumerate(peers)]
    for c in gather:
        c.start()
    full[own, :] = mine[...]
    for c in scatter:
        c.wait_send()
    for c in gather:
        c.wait()
    out[...] = full[:, : out.shape[1]]


def prep_kernel(chunk, rows, src, dst, w, src_out, dst_out, w_out, counts, total):
    lines = src.shape[0]
    slots = src_out.shape[0]
    live = w[...] != 0.0
    halo = src[...] >= rows
    at = lambda shape, axis: lax.broadcasted_iota(jnp.int32, shape, axis)
    before = (at((LANES, LANES), 0) < at((LANES, LANES), 1)).astype(BF16)
    above = (at((lines, lines), 1) < at((lines, lines), 0)).astype(BF16)
    ones = jnp.ones((LANES, LANES), BF16)

    def rank(mask):
        m = mask.astype(F32).astype(BF16)
        return dot(m, before) + dot(above, dot(m, ones).astype(BF16))

    is_local, is_halo = jnp.logical_and(live, jnp.logical_not(halo)), jnp.logical_and(live, halo)
    n_local = jnp.sum(is_local.astype(F32)).astype(jnp.int32)
    n_halo = jnp.sum(is_halo.astype(F32)).astype(jnp.int32)
    local_chunks = (n_local + chunk - 1) // chunk
    counts[0] = local_chunks
    counts[1] = local_chunks + (n_halo + chunk - 1) // chunk
    pos = jnp.where(
        is_local, rank(is_local).astype(jnp.int32), jnp.where(is_halo, rank(is_halo).astype(jnp.int32) + local_chunks * chunk, -1)
    )
    line, lane = pos >> 7, pos & (LANES - 1)
    s = jnp.where(halo, src[...] - rows, src[...])
    d = dst[...]
    half_w = w[...] * 0.5
    w_a = half_w.astype(BF16).astype(F32)
    w_b = (half_w - w_a).astype(BF16).astype(F32)
    w_c = half_w - w_a - w_b
    high = ((s >> 8) * 8 + (d >> 8)).astype(F32)
    planes = [(s & 255).astype(F32), (d & 255).astype(F32), high, w_a, w_b, w_c]
    acc = jnp.zeros((len(planes) * slots, LANES), F32)
    for r in range(0, lines, 2):
        lhs, rhs = [], []
        for q in (r, r + 1):
            pick = at((slots, LANES), 0) == line[q : q + 1, :]
            lhs.append(jnp.concatenate([jnp.where(pick, p[q : q + 1, :], 0.0) for p in planes], axis=0))
            rhs.append((at((LANES, LANES), 0) == lane[q : q + 1, :]).astype(F32))
        acc += dot(jnp.concatenate(lhs, axis=1).astype(BF16), jnp.concatenate(rhs, axis=1).astype(BF16), COLS_A)
    total[...] = acc
    plane = lambda i: total[i * slots : (i + 1) * slots, :]
    high = plane(2).astype(jnp.int32)
    src_out[...] = ((high >> 3) * 256 + plane(0).astype(jnp.int32)) * 2
    dst_out[...] = ((high & 7) * 256 + plane(1).astype(jnp.int32)) * 2
    w_out[...] = (plane(3) + plane(4) + plane(5)) * 2.0


def local_kernel(chunk, n_acc, counts, from_idx, to_idx, w, table, out, *accs):
    for a in accs:
        fill_zero(a)
    walk_edges(0, counts[0] * (PREP_CHUNK // chunk), chunk, from_idx, to_idx, w, table, accs)

    @pl.loop(0, out.shape[0], step=STEP)
    def _(i):
        out[pl.ds(i, STEP), :] = functools.reduce(jnp.add, [a[pl.ds(i, STEP), :] for a in accs])


def halo_range(counts, chunk):
    return counts[0] * (PREP_CHUNK // chunk), counts[1] * (PREP_CHUNK // chunk)


def forward_halo(chunk, counts, src, dst, w, from_prev, from_next, part, htab, accs):
    half = from_prev.shape[0]

    @pl.loop(0, half, step=256)
    def _(i):
        for start, got in ((0, from_prev), (half, from_next)):
            t = got[pl.ds(i, 256), :].astype(F32)
            put_halves(htab, start + i, 256, t[:, :LANES], t[:, LANES:])

    copy_in(accs[0], part)
    for a in accs[1:]:
        fill_zero(a)
    first, last = halo_range(counts, chunk)
    walk_edges(first, last, chunk, src, dst, w, htab, accs)


def backward_halo(chunk, counts, src, dst, w, grad, back_prev, back_next, accs):
    for a in accs:
        fill_zero(a)
    first, last = halo_range(counts, chunk)
    walk_edges(first, last, chunk, dst, src, w, grad, accs)
    half = back_prev.shape[0]

    @pl.loop(0, half, step=STEP)
    def _(i):
        back_prev[pl.ds(i, STEP), :] = functools.reduce(jnp.add, [a[pl.ds(i, STEP), :] for a in accs])
        back_next[pl.ds(i, STEP), :] = functools.reduce(jnp.add, [a[pl.ds(half + i, STEP), :] for a in accs])


def hidden_kernel(chunk, counts, src, dst, w, send, from_prev, from_next, part, w2, hid, tab, to_prev, to_next, htab, tab_b, *accs):
    forward_halo(chunk, counts, src, dst, w, from_prev, from_next, part, htab, accs)

    @pl.loop(0, hid.shape[0], step=256)
    def _(i):
        even, odd = halves(accs, i, 256)
        h = jnp.concatenate([jnp.maximum(even, 0.0), jnp.maximum(odd, 0.0)], axis=1).astype(BF16)
        hid[pl.ds(i, 256), :] = h
        t = dot(h, w2[...]).astype(BF16)
        tab_b[pl.ds(i, 256), :] = t
        t = t.astype(F32)
        put_halves(tab, i, 256, t[:, :LANES], t[:, LANES:])

    send_halo(send, tab_b, to_prev, to_next)


def loss_kernel(chunk, classes, counts, src, dst, w, count, from_prev, from_next, part, labels, mask, loss, grad, back_prev, back_next, htab, *accs):
    forward_halo(chunk, counts, src, dst, w, from_prev, from_next, part, htab, accs)
    lane = lax.broadcasted_iota(jnp.int32, (LANES, LANES), 1)
    live = lane < classes - LANES
    scale = 1.0 / count[0:1, :]
    loss[...] = jnp.zeros_like(loss)

    @pl.loop(0, labels.shape[0])
    def _(b):
        even, odd = halves(accs, b * LANES, LANES)
        label = spread(labels[pl.ds(b, 1), :])
        keep = spread(mask[pl.ds(b, 1), :]).astype(F32)
        odd = jnp.where(live, odd, -jnp.inf)
        top = jnp.max(jnp.maximum(even, odd), axis=1, keepdims=True)
        total = jnp.sum(jnp.exp(even - top) + jnp.exp(odd - top), axis=1, keepdims=True)
        norm = top + jnp.log(total)
        hit_even, hit_odd = lane == label, lane + LANES == label
        picked = jnp.where(hit_even, even, 0.0) + jnp.where(hit_odd, odd, 0.0)
        per_row = jnp.where(lane == 0, norm, 0.0) - picked
        loss[...] += jnp.sum((keep * per_row).reshape(LANES // 8, 8, LANES), axis=0)
        d_even = (jnp.exp(even - norm) - hit_even.astype(F32)) * (keep * scale)
        d_odd = (jnp.exp(odd - norm) - hit_odd.astype(F32)) * (keep * scale)
        put_halves(grad, b * LANES, LANES, d_even, d_odd)

    backward_halo(chunk, counts, src, dst, w, grad, back_prev, back_next, accs)


def take_returns(send, part, got_prev, got_next, accs):
    copy_in(accs[0], part)
    for a in accs[1:]:
        fill_zero(a)
    return_rows(send, send.shape[0] // 2, got_prev, accs)
    return_rows(send, 0, got_next, accs)


def middle_kernel(chunk, counts, src, dst, w, send, got_prev, got_next, part, hid, w2, grad_two, grad, back_prev, back_next, *accs):
    take_returns(send, part, got_prev, got_next, accs)
    grad_two[...] = jnp.zeros_like(grad_two)

    @pl.loop(0, hid.shape[0], step=256)
    def _(i):
        even, odd = halves(accs, i, 256)
        d_tab = jnp.concatenate([even, odd], axis=1).astype(BF16)
        h = hid[pl.ds(i, 256), :]
        grad_two[...] += dot(h, d_tab, ROWS_A)
        d_hid = dot(d_tab, w2[...], COLS_A)
        d_pre = jnp.where(h > 0, d_hid, 0.0)
        put_halves(grad, i, 256, d_pre[:, :LANES], d_pre[:, LANES:])

    backward_halo(chunk, counts, src, dst, w, grad, back_prev, back_next, accs)


def last_kernel(send, got_prev, got_next, part, x, grad_one, *accs):
    take_returns(send, part, got_prev, got_next, accs)
    grad_one[...] = jnp.zeros_like(grad_one)

    @pl.loop(0, x.shape[0], step=256)
    def _(i):
        even, odd = halves(accs, i, 256)
        d_tab = jnp.concatenate([even, odd], axis=1).astype(BF16)
        grad_one[...] += dot(x[pl.ds(i, 256), :], d_tab, ROWS_A)


def call(body, name, outs, ins, scratch, flops=10**9, out_specs=None, collective=None):
    extra = {} if collective is None else dict(collective_id=collective, has_side_effects=True)
    return pl.pallas_call(
        body, name=name, out_shape=outs, in_specs=ins, out_specs=out_specs or jax.tree.map(lambda _: VMEM, outs),
        scratch_shapes=[pltpu.VMEM(s, F32) if isinstance(s, tuple) else s for s in scratch],
        compiler_params=pltpu.CompilerParams(vmem_limit_bytes=60 * 2**20, **extra),
        cost_estimate=pl.CostEstimate(flops=flops, bytes_accessed=8 * 2**20, transcendentals=0),
    )


def solution(mesh):
    num_dev = mesh.shape[AXIS]
    to_next = [(d, (d + 1) % num_dev) for d in range(num_dev)]
    to_prev = [(d, (d - 1) % num_dev) for d in range(num_dev)]

    def step(x, w_one, w_two, send, edge_src, edge_dst, edge_w, labels, mask):
        rows, halo, edges, classes = x.shape[0], send.shape[1], edge_src.shape[0], w_two.shape[1]
        tab = (2 * rows, LANES)
        half = (2 * halo, LANES)
        sds = jax.ShapeDtypeStruct
        tab_f, half_f, half_b = sds(tab, F32), sds(half, F32), sds((halo, 2 * LANES), BF16)
        tab_b = pltpu.VMEM((rows, 2 * LANES), BF16)
        one = sds((8, LANES), F32)
        dma = pltpu.SemaphoreType.DMA
        chunk_l, chunk_h = 64, 32
        lines = edges // LANES
        slots = lines + 8
        w2 = jnp.pad(w_two, ((0, 0), (0, 2 * LANES - classes))).astype(BF16)
        mask = mask.reshape(-1, LANES)
        send = send.reshape(-1) * 2

        tab_one, to_p, to_n, count = call(
            functools.partial(first_kernel, num_dev), "first", [tab_f, half_b, half_b, one], [VMEM] * 4,
            [tab_b, (8, LANES), (num_dev - 1, 8, LANES), dma((num_dev - 1,)), dma((num_dev - 1,))], collective=0,
        )(x, w_one, send.reshape(-1, LANES), mask)
        from_prev = lax.ppermute(to_n, AXIS, to_next)
        from_next = lax.ppermute(to_p, AXIS, to_prev)

        lined = lambda a: a.reshape(lines, LANES)
        ints = sds((slots, LANES), jnp.int32)
        src, dst, w, counts = call(
            functools.partial(prep_kernel, PREP_CHUNK, rows), "prep", [ints, ints, sds((slots, LANES), F32), sds((2,), jnp.int32)], [VMEM] * 3,
            [(6 * slots, LANES)], out_specs=[VMEM] * 3 + [SMEM],
        )(lined(edge_src), lined(edge_dst), lined(edge_w))
        src, dst, w = src.reshape(-1), dst.reshape(-1), w.reshape(-1)

        walk = [SMEM] * 4
        local = call(functools.partial(local_kernel, chunk_l, 4), "local_edges", tab_f, walk + [VMEM], [tab] * 4, 10**10)
        part = local(counts, src, dst, w, tab_one)
        hid, tab_two, to_p, to_n = call(
            functools.partial(hidden_kernel, chunk_h), "hidden", [sds((rows, 2 * LANES), BF16), tab_f, half_b, half_b],
            walk + [VMEM] * 5, [tab, tab_b] + [tab] * 4,
        )(counts, src, dst, w, send.reshape(-1, LANES), from_prev, from_next, part, w2)
        from_prev = lax.ppermute(to_n, AXIS, to_next)
        from_next = lax.ppermute(to_p, AXIS, to_prev)
        part = local(counts, src, dst, w, tab_two)
        loss, grad, to_p, to_n = call(
            functools.partial(loss_kernel, chunk_h, classes), "loss", [sds((8, LANES), F32), tab_f, half_f, half_f],
            walk + [VMEM] * 6, [tab] + [tab] * 4,
        )(counts, src, dst, w, count, from_prev, from_next, part, labels.reshape(-1, LANES), mask)
        got_prev = lax.ppermute(to_p, AXIS, to_prev)
        got_next = lax.ppermute(to_n, AXIS, to_next)
        part = local(counts, dst, src, w, grad)
        grad_two, grad, to_p, to_n = call(
            functools.partial(middle_kernel, chunk_h), "middle", [sds((2 * LANES, 2 * LANES), F32), tab_f, half_f, half_f],
            walk + [SMEM] + [VMEM] * 5, [tab] * 4,
        )(counts, src, dst, w, send, got_prev, got_next, part, hid, w2)
        got_prev = lax.ppermute(to_p, AXIS, to_prev)
        got_next = lax.ppermute(to_n, AXIS, to_next)
        part = local(counts, dst, src, w, grad)

        def reducer(shape, out, name, collective, extra):
            n = num_dev
            piece = (shape[0] // n, shape[1])
            outs = [sds(out, F32)] + ([one] if extra else [])
            return call(
                functools.partial(reduce_kernel, n), name, outs, [VMEM] * (3 if extra else 1),
                [(n - 1, *piece), shape, piece, dma((6, n - 1))] + ([(n - 1, 8, LANES)] if extra else []),
                collective=collective, flops=10**10,
            )

        grad_two, mean = reducer(grad_two.shape, (2 * LANES, classes), "reduce_two", 1, True)(grad_two, loss, count)
        grad_one = call(last_kernel, "last", sds((x.shape[1], 2 * LANES), F32), [SMEM] + [VMEM] * 4, [tab] * 4)(send, got_prev, got_next, part, x)
        (grad_one,) = reducer(grad_one.shape, grad_one.shape, "reduce_one", 2, False)(grad_one)
        return mean[0, 0], grad_one, grad_two

    row = P(AXIS)
    return jax.shard_map(
        step, mesh=mesh, in_specs=(row, P(), P(), row, row, row, row, row, row), out_specs=(P(), P(), P()), check_vma=False
    )
```

time: 283 us -> 204 us (0.72)
  Pallas kernels: 89.3 us -> 172 us
  blocking collectives: 73.6 us -> 0 us
  waiting for transfers between devices: 70.8 us -> 10.1 us
  between operations: 16.6 us -> 0.72 us
  other arithmetic: 11.4 us -> 0.75 us
  starting transfers between devices: 15.7 us -> 9.94 us
  local copies, waits for them, and re-layouts: 7.92 us -> 12 us
    pallas_call x5 -> x8, Pallas kernels: 41.8 us -> 124 us  [the longest x1 40.1 us: step(): reducer(grad_two.shape, (2 * LANES, classes), 'reduce_two', 1, True)]
    psum x2 -> x0, blocking collectives: 73.6 us -> none  [the longest x1 40.3 us: step(): label_count = jnp.maximum(lax.psum(jnp.sum(mask_f), AXIS), 1.0)]
    psum x1 -> x0, waiting for transfers between devices: 33 us -> none  [step(): lax.psum((jnp.sum(loss), grad_one, grad_two[:, :classes]), AXIS)]
    ppermute x2, waiting for transfers between devices: 29 us -> 8.75 us  [step(): got_prev = lax.ppermute(to_p, AXIS, to_prev)]
    sort x1 -> x0, other arithmetic: 5.68 us -> none  [step(): key, w = lax.sort((key, edge_w), num_keys=1, is_stable=False)]
    ppermute x2, starting transfers between devices: 7.52 us -> 2.29 us  [step(): got_prev = lax.ppermute(to_p, AXIS, to_prev)]
    ppermute x2, waiting for transfers between devices: 6.23 us -> 1.32 us  [step(): got_next = lax.ppermute(to_n, AXIS, to_next)]
    pallas_call x1, Pallas kernels: 11.1 us -> 14 us  [step(): call(functools.partial(loss_kernel, chunk_h, classes), 'loss', [sds((8, L...]
  transfers between devices with their start and end apart: 9 -> 8, of which waited for: 7 -> 2; matrix products, arithmetic and copies ran while one was open for 4% -> 2% of each run, Pallas kernels for 11% -> 48%
where the time goes in v2:
time: 204 us; the launch traced here: 205 us
  Pallas kernels  172 us (84%)
  local copies, waits for them, and re-layouts  12 us (6%)
  waiting for transfers between devices  10.1 us (5%)
  starting transfers between devices  9.94 us (5%)
    pallas_call x1, Pallas kernels, step(): reducer(grad_two.shape, (2 * LANES, classes), 'reduce_two', 1, True)  40.1 us
    pallas_call x2, Pallas kernels, step(): part = local(counts, dst, src, w, grad)  27 us
    pallas_call x1, Pallas kernels, step(): reducer(grad_one.shape, grad_one.shape, 'reduce_one', 2, False)(grad_one)  14.2 us
    pallas_call x1, Pallas kernels, step(): call(functools.partial(loss_kernel, chunk_h, classes), 'loss', [sds((8, L...  14 us
    pallas_call x1, Pallas kernels, step(): part = local(counts, src, dst, w, tab_one)  13.5 us
    pallas_call x1, Pallas kernels, step(): part = local(counts, src, dst, w, tab_two)  13.5 us
    pallas_call x1, Pallas kernels, step(): call(functools.partial(middle_kernel, chunk_h), 'middle', [sds((2 * LANES...  13.1 us
    pallas_call x1, Pallas kernels, step(): call(functools.partial(hidden_kernel, chunk_h), 'hidden', [sds((rows, 2 *...  12.2 us
  transfers between devices with their start and end apart: 8, of which 2 were waited for; matrix products, arithmetic and copies ran while one was open for 2% of the time, Pallas kernels for 48%

profile of v2, /device:TPU:0, one launch (start us, length us, event | category | flops | bytes accessed | tf_op | source)
XLA Modules:
  0.0 205.1 jit_solution(12948068297083326905)
XLA Ops:
  0.6 0.0 copy-start.4
  0.6 0.7 broadcast_multiply_fusion
  1.4 0.6 mul.13.send
  2.0 12.1 %first.1 = (f32[4096,128]{1,0:T(8,128)}, bf16[1024,256]{1,0:T(8,128)(2,1)}, bf16[1024,256]{1,0:T(8,128)(2,1)}, f32[8,128]{1,0:T(8,128)}) custom-call(bf16[2048,128]{1,0:T(8,128)(2,1)} %x.5, f32[128,256]{1,0:T(8,128)} %w1.1, s32[16,128]{1,0:T(8,128)} %mul.13.send, s32[16,128]{1,0:T(8,128)} %bitcast.40), custom_call_target="tpu_custom_call" | custom-call | flops 1000000000 | bytes 8388608 | tf_op jit(solution)/shard_map/first/pallas_call | solution.py:386
  14.1 0.2 collective-permute-start
  14.3 3.4 %collective-permute-start.1 = (bf16[1024,256]{1,0:T(8,128)(2,1)}, bf16[1024,256]{1,0:T(8,128)(2,1)S(1)}, u32[]{:S(2)}, u32[]{:S(2)}) collective-permute-start(bf16[1024,256]{1,0:T(8,128)(2,1)} %get-tuple-element.31), channel_id=1, source_target_pairs={{0,15},{1,0},{2,1},{3,2},{4,3},{5,4},{6,5},{7,6},{8,7},{9,8},{10,9... | collective-permute-start | bytes 1572872 | tf_op jit(solution)/shard_map/ppermute | solution.py:391
  17.7 0.0 copy-done.4
  17.7 0.1 copy.14
  17.9 0.7 pad.5.w2
  18.5 3.8 %prep.1 = (s32[72,128]{1,0:T(8,128)}, s32[72,128]{1,0:T(8,128)}, f32[72,128]{1,0:T(8,128)}, s32[2]{0:T(128)}) custom-call(s32[64,128]{1,0:T(8,128)} %bitcast.37, s32[64,128]{1,0:T(8,128)} %bitcast.38, f32[64,128]{1,0:T(8,128)} %bitcast.39), custom_call_target="tpu_custom_call" | custom-call | flops 1000000000 | bytes 8388608 | tf_op jit(solution)/shard_map/prep/pallas_call | solution.py:395
  22.4 13.5 %local_edges.4.part = f32[4096,128]{1,0:T(8,128)} custom-call(s32[2]{0:T(128)} %get-tuple-element.25.counts, s32[9216]{0:T(1024)} %bitcast.16, s32[9216]{0:T(1024)} %bitcast.23, f32[9216]{0:T(1024)} %bitcast.30, f32[4096,128]{1,0:T(8,128)} %get-tuple-element.32.table), custom_call_target="tpu_custom_call" | custom-call | flops 10000000000 | bytes 8388608 | tf_op jit(solution)/shard_map/local_edges/pallas_call | solution.py:403
  35.9 0.0 collective-permute-done.from_prev
  35.9 0.0 copy-start.5
  35.9 0.0 collective-permute-done.1.from_next
  35.9 0.8 copy-done.5
  36.7 0.0 copy-start.6
  36.7 0.8 copy-done.6
  37.5 12.2 %hidden.1 = (bf16[2048,256]{1,0:T(8,128)(2,1)}, f32[4096,128]{1,0:T(8,128)}, bf16[1024,256]{1,0:T(8,128)(2,1)}, bf16[1024,256]{1,0:T(8,128)(2,1)}) custom-call(s32[2]{0:T(128)} %get-tuple-element.25.counts, s32[9216]{0:T(1024)} %bitcast.17, s32[9216]{0:T(1024)} %bitcast.24, f32[9216]{0:T(1024)} %bitcast.31, s32[16,128]{1,0:T(8,128)} %mul.13.send, ...), custom_call_target="tpu_custom_call" | custom-call | flops 1000000000 | bytes 8388608 | tf_op jit(solution)/shard_map/hidden/pallas_call | solution.py:404
  49.7 0.0 collective-permute-start.2
  49.7 3.5 %collective-permute-start.3 = (bf16[1024,256]{1,0:T(8,128)(2,1)}, bf16[1024,256]{1,0:T(8,128)(2,1)S(1)}, u32[]{:S(2)}, u32[]{:S(2)}) collective-permute-start(bf16[1024,256]{1,0:T(8,128)(2,1)} %get-tuple-element.34), channel_id=1, source_target_pairs={{0,15},{1,0},{2,1},{3,2},{4,3},{5,4},{6,5},{7,6},{8,7},{9,8},{10,9... | collective-permute-start | bytes 1572872 | tf_op jit(solution)/shard_map/ppermute | solution.py:409
  53.2 13.5 %local_edges.5.part = f32[4096,128]{1,0:T(8,128)} custom-call(s32[2]{0:T(128)} %get-tuple-element.25.counts, s32[9216]{0:T(1024)} %bitcast.18, s32[9216]{0:T(1024)} %bitcast.25, f32[9216]{0:T(1024)} %bitcast.32, f32[4096,128]{1,0:T(8,128)} %get-tuple-element.35.table), custom_call_target="tpu_custom_call" | custom-call | flops 10000000000 | bytes 8388608 | tf_op jit(solution)/shard_map/local_edges/pallas_call | solution.py:410
  66.7 0.0 collective-permute-done.2.from_prev
  66.7 0.0 copy-start.7
  66.7 0.0 collective-permute-done.3.from_next
  66.7 0.0 copy-start.8
  66.8 0.8 copy-done.7
  67.5 0.2 copy-done.8
  67.7 14.0 %loss.1 = (f32[8,128]{1,0:T(8,128)}, f32[4096,128]{1,0:T(8,128)}, f32[2048,128]{1,0:T(8,128)}, f32[2048,128]{1,0:T(8,128)}) custom-call(s32[2]{0:T(128)} %get-tuple-element.25.counts, s32[9216]{0:T(1024)} %bitcast.19, s32[9216]{0:T(1024)} %bitcast.26, f32[9216]{0:T(1024)} %bitcast.33, f32[8,128]{1,0:T(8,128)} %get-tuple-element.29.count.refs_1_, ...), custom_call_target="tpu_custom_call" | custom-call | flops 1000000000 | bytes 8388608 | tf_op jit(solution)/shard_map/loss/pallas_call | solution.py:411
  81.8 0.0 collective-permute-start.4
  81.8 0.5 collective-permute-start.5
  82.3 0.6 copy.18
  82.9 13.5 %local_edges.6.part = f32[4096,128]{1,0:T(8,128)} custom-call(s32[2]{0:T(128)} %get-tuple-element.25.counts, s32[9216]{0:T(1024)} %bitcast.27, s32[9216]{0:T(1024)} %bitcast.20, f32[9216]{0:T(1024)} %bitcast.34, f32[4096,128]{1,0:T(8,128)} %get-tuple-element.38.table), custom_call_target="tpu_custom_call" | custom-call | flops 10000000000 | bytes 8388608 | tf_op jit(solution)/shard_map/local_edges/pallas_call | solution.py:417
  96.4 8.7 %collective-permute-done.4.got_prev = f32[2048,128]{1,0:T(8,128)S(1)} collective-permute-done((f32[2048,128]{1,0:T(8,128)}, f32[2048,128]{1,0:T(8,128)S(1)}, u32[]{:S(2)}, u32[]{:S(2)}) %collective-permute-start.4) | collective-permute-done | bytes 1048608 | tf_op jit(solution)/shard_map/ppermute | solution.py:415
  105.1 0.0 copy-start.2
  105.1 1.3 collective-permute-done.5.got_next
  106.4 0.0 copy-start.3
  106.4 0.0 copy-done.2
  106.4 1.1 copy-done.3
  107.5 13.1 %middle.1 = (f32[256,256]{1,0:T(8,128)}, f32[4096,128]{1,0:T(8,128)}, f32[2048,128]{1,0:T(8,128)}, f32[2048,128]{1,0:T(8,128)}) custom-call(s32[2]{0:T(128)} %get-tuple-element.25.counts, s32[9216]{0:T(1024)} %bitcast.21, s32[9216]{0:T(1024)} %bitcast.28, f32[9216]{0:T(1024)} %bitcast.35, s32[2048]{0:T(1024)} %bitcast.14, f32[2048,128]{1,0:T(8,128)} %copy-done.2, ...), custom_call_target="tpu_custom_call" | custom-call | flops 1000000000 | bytes 8388608 | tf_op jit(solution)/shard_map/middle/pallas_call | solution.py:418
  120.6 2.3 %collective-permute-start.6 = (f32[2048,128]{1,0:T(8,128)}, f32[2048,128]{1,0:T(8,128)S(1)}, u32[]{:S(2)}, u32[]{:S(2)}) collective-permute-start(f32[2048,128]{1,0:T(8,128)} %get-tuple-element.43), channel_id=1, source_target_pairs={{0,15},{1,0},{2,1},{3,2},{4,3},{5,4},{6,5},{7,6},{8,7},{9,8},{10,9... | collective-permute-start | bytes 3145736 | tf_op jit(solution)/shard_map/ppermute | solution.py:422
  122.9 0.0 collective-permute-start.7
  122.9 40.1 %reduce_two.1 = (f32[256,172]{1,0:T(8,128)}, f32[8,128]{1,0:T(8,128)}) custom-call(f32[256,256]{1,0:T(8,128)} %get-tuple-element.40.part, f32[8,128]{1,0:T(8,128)} %get-tuple-element.41.refs_0_, f32[8,128]{1,0:T(8,128)} %get-tuple-element.29.count.refs_1_), custom_call_target="tpu_custom_call" | custom-call | flops 10000000000 | bytes 8388608 | tf_op jit(solution)/shard_map/reduce_two/pallas_call | solution.py:436
  163.0 1.2 slice.3
  164.2 1.7 copy.15
  165.9 13.5 %local_edges.7.part = f32[4096,128]{1,0:T(8,128)} custom-call(s32[2]{0:T(128)} %get-tuple-element.25.counts, s32[9216]{0:T(1024)} %bitcast.29, s32[9216]{0:T(1024)} %bitcast.22, f32[9216]{0:T(1024)} %bitcast.36, f32[4096,128]{1,0:T(8,128)} %get-tuple-element.45.table), custom_call_target="tpu_custom_call" | custom-call | flops 10000000000 | bytes 8388608 | tf_op jit(solution)/shard_map/local_edges/pallas_call | solution.py:424
  179.4 0.0 collective-permute-done.6.got_prev
  179.4 0.0 copy-start
  179.4 0.0 collective-permute-done.7.got_next
  179.4 1.0 copy-done
  180.4 0.0 copy-start.1
  180.4 1.0 copy-done.1
  181.4 8.0 %last.1.part = f32[128,256]{1,0:T(8,128)} custom-call(s32[2048]{0:T(1024)} %bitcast.15, f32[2048,128]{1,0:T(8,128)} %copy-done, f32[2048,128]{1,0:T(8,128)} %copy-done.1, f32[4096,128]{1,0:T(8,128)} %local_edges.7.part, bf16[2048,128]{1,0:T(8,128)(2,1)} %x.5), custom_call_target="tpu_custom_call" | custom-call | flops 1000000000 | bytes 8388608 | tf_op jit(solution)/shard_map/last/pallas_call | solution.py:437
  189.3 14.2 %reduce_one.1 = f32[128,256]{1,0:T(8,128)} custom-call(f32[128,256]{1,0:T(8,128)} %last.1.part), custom_call_target="tpu_custom_call" | custom-call | flops 10000000000 | bytes 8388608 | tf_op jit(solution)/shard_map/reduce_one/pallas_call | solution.py:438
  203.6 1.6 copy.20
  (1 shorter events, 0.0 us)
Async XLA Ops:
  0.6 17.1 %copy-start.4 = (f32[256,172]{0,1:T(8,128)S(1)}, f32[256,172]{0,1:T(8,128)}, u32[]{:S(2)}) copy-start(f32[256,172]{0,1:T(8,128)} %param.11) | copy-start | bytes 528388
  14.1 21.8 %collective-permute-start = (bf16[1024,256]{1,0:T(8,128)(2,1)}, bf16[1024,256]{1,0:T(8,128)(2,1)S(1)}, u32[]{:S(2)}, u32[]{:S(2)}) collective-permute-start(bf16[1024,256]{1,0:T(8,128)(2,1)} %get-tuple-element.30), channel_id=1, source_target_pairs={{0,1},{1,2},{2,3},{3,4},{4,5},{5,6},{6,7},{7,8},{8,9},{9,10},{10,1... | collective-permute-start | bytes 1572872 | tf_op jit(solution)/shard_map/ppermute | solution.py:390
  14.3 21.6 %collective-permute-start.1 = (bf16[1024,256]{1,0:T(8,128)(2,1)}, bf16[1024,256]{1,0:T(8,128)(2,1)S(1)}, u32[]{:S(2)}, u32[]{:S(2)}) collective-permute-start(bf16[1024,256]{1,0:T(8,128)(2,1)} %get-tuple-element.31), channel_id=1, source_target_pairs={{0,15},{1,0},{2,1},{3,2},{4,3},{5,4},{6,5},{7,6},{8,7},{9,8},{10,9... | collective-permute-start | bytes 1572872 | tf_op jit(solution)/shard_map/ppermute | solution.py:391
  35.9 0.8 copy-start.5
  36.7 0.8 copy-start.6
  49.7 17.1 %collective-permute-start.2 = (bf16[1024,256]{1,0:T(8,128)(2,1)}, bf16[1024,256]{1,0:T(8,128)(2,1)S(1)}, u32[]{:S(2)}, u32[]{:S(2)}) collective-permute-start(bf16[1024,256]{1,0:T(8,128)(2,1)} %get-tuple-element.33), channel_id=1, source_target_pairs={{0,1},{1,2},{2,3},{3,4},{4,5},{5,6},{6,7},{7,8},{8,9},{9,10},{10,1... | collective-permute-start | bytes 1572872 | tf_op jit(solution)/shard_map/ppermute | solution.py:408
  49.7 17.1 %collective-permute-start.3 = (bf16[1024,256]{1,0:T(8,128)(2,1)}, bf16[1024,256]{1,0:T(8,128)(2,1)S(1)}, u32[]{:S(2)}, u32[]{:S(2)}) collective-permute-start(bf16[1024,256]{1,0:T(8,128)(2,1)} %get-tuple-element.34), channel_id=1, source_target_pairs={{0,15},{1,0},{2,1},{3,2},{4,3},{5,4},{6,5},{7,6},{8,7},{9,8},{10,9... | collective-permute-start | bytes 1572872 | tf_op jit(solution)/shard_map/ppermute | solution.py:409
  66.7 0.8 copy-start.7
  66.7 1.0 copy-start.8
  81.8 23.4 %collective-permute-start.4 = (f32[2048,128]{1,0:T(8,128)}, f32[2048,128]{1,0:T(8,128)S(1)}, u32[]{:S(2)}, u32[]{:S(2)}) collective-permute-start(f32[2048,128]{1,0:T(8,128)} %get-tuple-element.36), channel_id=1, source_target_pairs={{0,15},{1,0},{2,1},{3,2},{4,3},{5,4},{6,5},{7,6},{8,7},{9,8},{10,9... | collective-permute-start | bytes 3145736 | tf_op jit(solution)/shard_map/ppermute | solution.py:415
  81.8 24.7 %collective-permute-start.5 = (f32[2048,128]{1,0:T(8,128)}, f32[2048,128]{1,0:T(8,128)S(1)}, u32[]{:S(2)}, u32[]{:S(2)}) collective-permute-start(f32[2048,128]{1,0:T(8,128)} %get-tuple-element.37), channel_id=1, source_target_pairs={{0,1},{1,2},{2,3},{3,4},{4,5},{5,6},{6,7},{7,8},{8,9},{9,10},{10,1... | collective-permute-start | bytes 3145736 | tf_op jit(solution)/shard_map/ppermute | solution.py:416
  105.1 1.3 copy-start.2
  106.4 1.1 copy-start.3
  120.6 58.8 %collective-permute-start.6 = (f32[2048,128]{1,0:T(8,128)}, f32[2048,128]{1,0:T(8,128)S(1)}, u32[]{:S(2)}, u32[]{:S(2)}) collective-permute-start(f32[2048,128]{1,0:T(8,128)} %get-tuple-element.43), channel_id=1, source_target_pairs={{0,15},{1,0},{2,1},{3,2},{4,3},{5,4},{6,5},{7,6},{8,7},{9,8},{10,9... | collective-permute-start | bytes 3145736 | tf_op jit(solution)/shard_map/ppermute | solution.py:422
  122.9 56.6 %collective-permute-start.7 = (f32[2048,128]{1,0:T(8,128)}, f32[2048,128]{1,0:T(8,128)S(1)}, u32[]{:S(2)}, u32[]{:S(2)}) collective-permute-start(f32[2048,128]{1,0:T(8,128)} %get-tuple-element.44), channel_id=1, source_target_pairs={{0,1},{1,2},{2,3},{3,4},{4,5},{5,6},{6,7},{7,8},{8,9},{9,10},{10,1... | collective-permute-start | bytes 3145736 | tf_op jit(solution)/shard_map/ppermute | solution.py:423
  179.4 1.0 copy-start
  180.4 1.0 copy-start.1

commit v3 on v2

--- a/solution.py
+++ b/solution.py
@@ -56,17 +56,60 @@
     lax.fori_loop(first, last, body, 0)
 
 
+def one_hot_rows(idx, line, table):
+    lane = lax.broadcasted_iota(jnp.int32, (LANES, LANES), 1) * 2
+    hot = []
+    for q in range(2):
+        want = spread(idx[pl.ds(line + q, 1), :])
+        hot.append(
+            jnp.concatenate([jnp.where(want == lane + 2 * LANES * j, 1.0, 0.0).astype(BF16) for j in range(table.shape[0] // LANES)], axis=1)
+        )
+    return dot(jnp.concatenate(hot, axis=0), table[...])
+
+
+def low_lanes(rows):
+    return lax.broadcasted_iota(jnp.int32, (rows, LANES), 1) < LANES // 2
+
+
+def swap_lanes(v):
+    return pltpu.roll(v, LANES // 2, 1)
+
+
 def gather_rows(idx, line, table, out):
-    lane = lax.broadcasted_iota(jnp.int32, (LANES, LANES), 1) * 2
-    groups = table.shape[0] // LANES
-
-    @pl.loop(0, out.shape[0] // 256)
-    def _(c):
-        hot = []
-        for q in range(2):
-            want = spread(idx[pl.ds(line + c * 2 + q, 1), :])
-            hot.append(jnp.concatenate([jnp.where(want == lane + 2 * LANES * j, 1.0, 0.0).astype(BF16) for j in range(groups)], axis=1))
-        out[pl.ds(pl.multiple_of(c * 256, 256), 256), :] = dot(jnp.concatenate(hot, axis=0), table[...]).astype(BF16)
+    @pl.loop(0, out.shape[0], step=256)
+    def _(i):
+        out[pl.ds(pl.multiple_of(i, 256), 256), :] = one_hot_rows(idx, line + i // LANES, table).astype(BF16)
+
+
+def gather_packed(idx, line, table, out):
+    halo = out.shape[0] * 2 // 3
+
+    @pl.loop(0, halo // 2, step=256)
+    def _(i):
+        i = pl.multiple_of(i, 256)
+        a = one_hot_rows(idx, line + i // LANES, table)
+        b = one_hot_rows(idx, line + (halo // 2 + i) // LANES, table)
+        out[pl.ds(i, 256), :] = a[:, :LANES].astype(BF16)
+        out[pl.ds(halo // 2 + i, 256), :] = b[:, :LANES].astype(BF16)
+        out[pl.ds(halo + i, 256), :] = jnp.where(low_lanes(256), a[:, LANES:], swap_lanes(b[:, LANES:])).astype(BF16)
+
+
+def unpack_rows(got, table, start):
+    halo = got.shape[0] * 2 // 3
+
+    @pl.loop(0, halo // 2, step=256)
+    def _(i):
+        i = pl.multiple_of(i, 256)
+        a, b, both = (got[pl.ds(k + i, 256), :].astype(F32) for k in (0, halo // 2, halo))
+        put_halves(table, start + i, 256, a, jnp.where(low_lanes(256), both, 0.0))
+        put_halves(table, start + halo // 2 + i, 256, b, jnp.where(low_lanes(256), swap_lanes(both), 0.0))
+
+
+def unpack_plain(got, table, start):
+    @pl.loop(0, got.shape[0], step=256)
+    def _(i):
+        t = got[pl.ds(i, 256), :].astype(F32)
+        put_halves(table, start + i, 256, t[:, :LANES], t[:, LANES:])
 
 
 def spread(row):
@@ -88,11 +131,6 @@
                 accs[u][pl.ds(pend[u][0], 2), :] = pend[u][1]
 
 
-def send_halo(idx, table, prev_out, next_out):
-    gather_rows(idx, 0, table, prev_out)
-    gather_rows(idx, idx.shape[0] // 2, table, next_out)
-
-
 def halves(accs, i, n):
     even = functools.reduce(jnp.add, [a[pl.ds(2 * i, n, stride=2), :] for a in accs])
     odd = functools.reduce(jnp.add, [a[pl.ds(2 * i + 1, n, stride=2), :] for a in accs])
@@ -136,50 +174,69 @@
     copies = [remote(mine, theirs.at[o - 1], send_sem.at[o - 1], recv_sem.at[o - 1], lax.rem(me + o, n)) for o in range(1, n)]
     for c in copies:
         c.start()
-    send_halo(send, tab_b, to_prev, to_next)
+    gather_rows(send, 0, tab_b, to_prev)
+    gather_rows(send, send.shape[0] // 2, tab_b, to_next)
     for c in copies:
         c.wait()
     total = mine[...] + jnp.sum(theirs[...], axis=0)
     count[...] = jnp.maximum(jnp.broadcast_to(jnp.sum(total, keepdims=True), count.shape), 1.0)
 
 
-def reduce_kernel(n, part, *refs):
-    if len(refs) == 9:
-        extra, count, out, mean, got, full, mine, sems, theirs = refs
-    else:
-        out, got, full, mine, sems = refs
-        extra = None
-    me, met = greet(n)
-    rows = part.shape[0] // n
-    met()
-    peers = [lax.rem(me + o, n) for o in range(1, n)]
+def reduce_kernel(n, one, two, loss, count, one_out, two_out, mean, work, full, got_pair, got_rest, sems):
+    me = lax.axis_index(AXIS)
+    chips, core = n // 2, lax.rem(me, 2)
+    chip = lax.div(me, 2)
+    pair = me + 1 - 2 * core
+    others = [lax.rem(chip + o, chips) for o in range(1, chips)]
+    barrier = pltpu.get_barrier_semaphore()
+    for p in [pair] + [2 * c + core for c in others]:
+        pl.semaphore_signal(barrier, inc=1, device_id=(p,), device_id_type=MESH)
+    classes = two_out.shape[0]
+    lines = -(-classes // 8) * 8
+    top, wide = one.shape
+    work[0:top, :] = one[:, :LANES]
+    work[top : 2 * top, :] = one[:, LANES:]
+    work[2 * top : 2 * top + lines, :] = two[:lines, :LANES]
+    work[2 * top + lines : 2 * top + 2 * lines, :] = two[:lines, LANES:]
+    tail = 2 * top + 2 * lines
+    work[tail : tail + 8, :] = loss[...]
+    work[tail + 8 :, :] = jnp.zeros((work.shape[0] - tail - 8, LANES), F32)
+    pl.semaphore_wait(barrier, chips)
+
+    half = work.shape[0] // 2
+    piece = half // chips
+    rows = lambda start, size: pl.ds(pl.multiple_of(start, 8), size)
+    mine, other = rows(core * half, half), rows((1 - core) * half, half)
+    swap = remote(work.at[other], got_pair, sems.at[0, 0], sems.at[1, 0], pair)
+    swap.start()
+    swap.wait()
+    work[mine, :] += got_pair[...]
     scatter = [
-        remote(part.at[pl.ds(pl.multiple_of(p * rows, 8), rows)], got.at[o], sems.at[0, o], sems.at[1, o], p) for o, p in enumerate(peers)
+        remote(work.at[rows(core * half + c * piece, piece)], got_rest.at[o], sems.at[0, 1 + o], sems.at[1, 1 + o], 2 * c + core)
+        for o, c in enumerate(others)
     ]
     for c in scatter:
         c.start()
-    if extra is not None:
-        spread_out = [remote(extra, theirs.at[o], sems.at[4, o], sems.at[5, o], p) for o, p in enumerate(peers)]
-        for c in spread_out:
-            c.start()
     for c in scatter:
-        c.wait_recv()
-    own = pl.ds(pl.multiple_of(me * rows, 8), rows)
-    mine[...] = part[own, :] + jnp.sum(got[...], axis=0)
-    if extra is not None:
-        for c in spread_out:
-            c.wait()
-        total = jnp.sum(extra[...] + jnp.sum(theirs[...], axis=0), keepdims=True)
-        mean[...] = jnp.broadcast_to(total, mean.shape) / count[...]
-    gather = [remote(mine, full.at[own], sems.at[2, o], sems.at[3, o], p) for o, p in enumerate(peers)]
+        c.wait()
+    own = rows(core * half + chip * piece, piece)
+    work[own, :] += jnp.sum(got_rest[...], axis=0)
+    full[own, :] = work[own, :]
+    gather = [
+        remote(work.at[own], full.at[own], sems.at[0, chips + o], sems.at[1, chips + o], 2 * c + core) for o, c in enumerate(others)
+    ]
     for c in gather:
         c.start()
-    full[own, :] = mine[...]
-    for c in scatter:
-        c.wait_send()
     for c in gather:
         c.wait()
-    out[...] = full[:, : out.shape[1]]
+    last = remote(full.at[mine], full.at[mine], sems.at[0, 2 * chips - 1], sems.at[1, 2 * chips - 1], pair)
+    last.start()
+    last.wait()
+    one_out[:, :LANES] = full[0:top, :]
+    one_out[:, LANES:] = full[top : 2 * top, :]
+    two_out[:, :LANES] = full[2 * top : 2 * top + classes, :]
+    two_out[:, LANES:] = full[2 * top + lines : 2 * top + lines + classes, :]
+    mean[...] = jnp.sum(full[tail : tail + 8, :], keepdims=True) / count[0:1, 0:1]
 
 
 def prep_kernel(chunk, rows, src, dst, w, src_out, dst_out, w_out, counts, total):
@@ -244,15 +301,9 @@
     return counts[0] * (PREP_CHUNK // chunk), counts[1] * (PREP_CHUNK // chunk)
 
 
-def forward_halo(chunk, counts, src, dst, w, from_prev, from_next, part, htab, accs):
-    half = from_prev.shape[0]
-
-    @pl.loop(0, half, step=256)
-    def _(i):
-        for start, got in ((0, from_prev), (half, from_next)):
-            t = got[pl.ds(i, 256), :].astype(F32)
-            put_halves(htab, start + i, 256, t[:, :LANES], t[:, LANES:])
-
+def forward_halo(chunk, counts, src, dst, w, from_prev, from_next, part, htab, accs, unpack):
+    unpack(from_prev, htab, 0)
+    unpack(from_next, htab, htab.shape[0] // 4)
     copy_in(accs[0], part)
     for a in accs[1:]:
         fill_zero(a)
@@ -265,16 +316,29 @@
         fill_zero(a)
     first, last = halo_range(counts, chunk)
     walk_edges(first, last, chunk, dst, src, w, grad, accs)
-    half = back_prev.shape[0]
-
-    @pl.loop(0, half, step=STEP)
-    def _(i):
-        back_prev[pl.ds(i, STEP), :] = functools.reduce(jnp.add, [a[pl.ds(i, STEP), :] for a in accs])
-        back_next[pl.ds(i, STEP), :] = functools.reduce(jnp.add, [a[pl.ds(half + i, STEP), :] for a in accs])
+    split = accs[0].shape[0] // 2
+    if back_prev.shape[0] == split:
+
+        @pl.loop(0, split, step=STEP)
+        def _(i):
+            back_prev[pl.ds(i, STEP), :] = functools.reduce(jnp.add, [a[pl.ds(i, STEP), :] for a in accs])
+            back_next[pl.ds(i, STEP), :] = functools.reduce(jnp.add, [a[pl.ds(split + i, STEP), :] for a in accs])
+        return
+    halo = split // 2
+
+    @pl.loop(0, halo // 2, step=256)
+    def _(i):
+        i = pl.multiple_of(i, 256)
+        for start, out in ((0, back_prev), (halo, back_next)):
+            a_even, a_odd = halves(accs, start + i, 256)
+            b_even, b_odd = halves(accs, start + halo // 2 + i, 256)
+            out[pl.ds(i, 256), :] = a_even
+            out[pl.ds(halo // 2 + i, 256), :] = b_even
+            out[pl.ds(halo + i, 256), :] = jnp.where(low_lanes(256), a_odd, swap_lanes(b_odd))
 
 
 def hidden_kernel(chunk, counts, src, dst, w, send, from_prev, from_next, part, w2, hid, tab, to_prev, to_next, htab, tab_b, *accs):
-    forward_halo(chunk, counts, src, dst, w, from_prev, from_next, part, htab, accs)
+    forward_halo(chunk, counts, src, dst, w, from_prev, from_next, part, htab, accs, unpack_plain)
 
     @pl.loop(0, hid.shape[0], step=256)
     def _(i):
@@ -286,11 +350,12 @@
         t = t.astype(F32)
         put_halves(tab, i, 256, t[:, :LANES], t[:, LANES:])
 
-    send_halo(send, tab_b, to_prev, to_next)
+    gather_packed(send, 0, tab_b, to_prev)
+    gather_packed(send, send.shape[0] // 2, tab_b, to_next)
 
 
 def loss_kernel(chunk, classes, counts, src, dst, w, count, from_prev, from_next, part, labels, mask, loss, grad, back_prev, back_next, htab, *accs):
-    forward_halo(chunk, counts, src, dst, w, from_prev, from_next, part, htab, accs)
+    forward_halo(chunk, counts, src, dst, w, from_prev, from_next, part, htab, accs, unpack_rows)
     lane = lax.broadcasted_iota(jnp.int32, (LANES, LANES), 1)
     live = lane < classes - LANES
     scale = 1.0 / count[0:1, :]
@@ -324,8 +389,11 @@
     return_rows(send, 0, got_next, accs)
 
 
-def middle_kernel(chunk, counts, src, dst, w, send, got_prev, got_next, part, hid, w2, grad_two, grad, back_prev, back_next, *accs):
-    take_returns(send, part, got_prev, got_next, accs)
+def middle_kernel(chunk, counts, src, dst, w, send, got_prev, got_next, part, hid, w2, grad_two, grad, back_prev, back_next, returned, *accs):
+    split = returned.shape[0] // 2
+    unpack_rows(got_prev, returned, 0)
+    unpack_rows(got_next, returned, split // 2)
+    take_returns(send, part, returned.at[pl.ds(0, split)], returned.at[pl.ds(split, split)], accs)
     grad_two[...] = jnp.zeros_like(grad_two)
 
     @pl.loop(0, hid.shape[0], step=256)
@@ -333,7 +401,7 @@
         even, odd = halves(accs, i, 256)
         d_tab = jnp.concatenate([even, odd], axis=1).astype(BF16)
         h = hid[pl.ds(i, 256), :]
-        grad_two[...] += dot(h, d_tab, ROWS_A)
+        grad_two[...] += dot(d_tab, h, ROWS_A)
         d_hid = dot(d_tab, w2[...], COLS_A)
         d_pre = jnp.where(h > 0, d_hid, 0.0)
         put_halves(grad, i, 256, d_pre[:, :LANES], d_pre[:, LANES:])
@@ -352,12 +420,12 @@
         grad_one[...] += dot(x[pl.ds(i, 256), :], d_tab, ROWS_A)
 
 
-def call(body, name, outs, ins, scratch, flops=10**9, out_specs=None, collective=None):
+def call(body, name, outs, ins, scratch, flops=10**9, out_specs=None, collective=None, vmem=32):
     extra = {} if collective is None else dict(collective_id=collective, has_side_effects=True)
     return pl.pallas_call(
         body, name=name, out_shape=outs, in_specs=ins, out_specs=out_specs or jax.tree.map(lambda _: VMEM, outs),
         scratch_shapes=[pltpu.VMEM(s, F32) if isinstance(s, tuple) else s for s in scratch],
-        compiler_params=pltpu.CompilerParams(vmem_limit_bytes=60 * 2**20, **extra),
+        compiler_params=pltpu.CompilerParams(vmem_limit_bytes=vmem * 2**20, **extra),
         cost_estimate=pl.CostEstimate(flops=flops, bytes_accessed=8 * 2**20, transcendentals=0),
     )
 
@@ -373,6 +441,7 @@
         half = (2 * halo, LANES)
         sds = jax.ShapeDtypeStruct
         tab_f, half_f, half_b = sds(tab, F32), sds(half, F32), sds((halo, 2 * LANES), BF16)
+        pack_f, pack_b = sds((3 * halo // 2, LANES), F32), sds((3 * halo // 2, LANES), BF16)
         tab_b = pltpu.VMEM((rows, 2 * LANES), BF16)
         one = sds((8, LANES), F32)
         dma = pltpu.SemaphoreType.DMA
@@ -402,14 +471,14 @@
         local = call(functools.partial(local_kernel, chunk_l, 4), "local_edges", tab_f, walk + [VMEM], [tab] * 4, 10**10)
         part = local(counts, src, dst, w, tab_one)
         hid, tab_two, to_p, to_n = call(
-            functools.partial(hidden_kernel, chunk_h), "hidden", [sds((rows, 2 * LANES), BF16), tab_f, half_b, half_b],
+            functools.partial(hidden_kernel, chunk_h), "hidden", [sds((rows, 2 * LANES), BF16), tab_f, pack_b, pack_b],
             walk + [VMEM] * 5, [tab, tab_b] + [tab] * 4,
         )(counts, src, dst, w, send.reshape(-1, LANES), from_prev, from_next, part, w2)
         from_prev = lax.ppermute(to_n, AXIS, to_next)
         from_next = lax.ppermute(to_p, AXIS, to_prev)
         part = local(counts, src, dst, w, tab_two)
         loss, grad, to_p, to_n = call(
-            functools.partial(loss_kernel, chunk_h, classes), "loss", [sds((8, LANES), F32), tab_f, half_f, half_f],
+            functools.partial(loss_kernel, chunk_h, classes), "loss", [sds((8, LANES), F32), tab_f, pack_f, pack_f],
             walk + [VMEM] * 6, [tab] + [tab] * 4,
         )(counts, src, dst, w, count, from_prev, from_next, part, labels.reshape(-1, LANES), mask)
         got_prev = lax.ppermute(to_p, AXIS, to_prev)
@@ -417,26 +486,21 @@
         part = local(counts, dst, src, w, grad)
         grad_two, grad, to_p, to_n = call(
             functools.partial(middle_kernel, chunk_h), "middle", [sds((2 * LANES, 2 * LANES), F32), tab_f, half_f, half_f],
-            walk + [SMEM] + [VMEM] * 5, [tab] * 4,
+            walk + [SMEM] + [VMEM] * 5, [tab] * 5,
         )(counts, src, dst, w, send, got_prev, got_next, part, hid, w2)
         got_prev = lax.ppermute(to_p, AXIS, to_prev)
         got_next = lax.ppermute(to_n, AXIS, to_next)
         part = local(counts, dst, src, w, grad)
 
-        def reducer(shape, out, name, collective, extra):
-            n = num_dev
-            piece = (shape[0] // n, shape[1])
-            outs = [sds(out, F32)] + ([one] if extra else [])
-            return call(
-                functools.partial(reduce_kernel, n), name, outs, [VMEM] * (3 if extra else 1),
-                [(n - 1, *piece), shape, piece, dma((6, n - 1))] + ([(n - 1, 8, LANES)] if extra else []),
-                collective=collective, flops=10**10,
-            )
-
-        grad_two, mean = reducer(grad_two.shape, (2 * LANES, classes), "reduce_two", 1, True)(grad_two, loss, count)
         grad_one = call(last_kernel, "last", sds((x.shape[1], 2 * LANES), F32), [SMEM] + [VMEM] * 4, [tab] * 4)(send, got_prev, got_next, part, x)
-        (grad_one,) = reducer(grad_one.shape, grad_one.shape, "reduce_one", 2, False)(grad_one)
-        return mean[0, 0], grad_one, grad_two
+        lines = 2 * x.shape[1] + 2 * (-(-classes // 8) * 8) + 8
+        lines = -(-lines // (8 * num_dev)) * 8 * num_dev
+        grad_one, grad_two, mean = call(
+            functools.partial(reduce_kernel, num_dev), "reduce", [sds(grad_one.shape, F32), sds((classes, 2 * LANES), F32), sds((1, 1), F32)],
+            [VMEM] * 4, [(lines, LANES), (lines, LANES), (lines // 2, LANES), (num_dev // 2 - 1, lines // num_dev, LANES), dma((2, num_dev))],
+            collective=1, vmem=8,
+        )(grad_one, grad_two, loss, count)
+        return mean.reshape(()), grad_one, grad_two.T
 
     row = P(AXIS)
     return jax.shard_map(

time: 204 us -> 152 us (0.75); the launches traced: 205 us -> 151 us
  Pallas kernels: 172 us -> 120 us
  local copies, waits for them, and re-layouts: 12 us -> 5.45 us
    pallas_call x2 -> x1, Pallas kernels: 54.3 us -> 15.1 us  [step(): call(functools.partial(reduce_kernel, num_dev), 'reduce', [sds(grad_one.s...]
    unnamed x21 -> x27, local copies, waits for them, and re-layouts: 9.47 us -> 5.32 us
    pallas_call x1, Pallas kernels: 14 us -> 10.5 us  [step(): call(functools.partial(loss_kernel, chunk_h, classes), 'loss', [sds((8, L...]
    pallas_call x1, Pallas kernels: 12.2 us -> 9.13 us  [step(): call(functools.partial(hidden_kernel, chunk_h), 'hidden', [sds((rows, 2 *...]
    pallas_call x1, Pallas kernels: 12.1 us -> 9.56 us  [step(): call(functools.partial(first_kernel, num_dev), 'first', [tab_f, half_b, h...]
    pallas_call x1, Pallas kernels: 13.1 us -> 10.6 us  [step(): call(functools.partial(middle_kernel, chunk_h), 'middle', [sds((2 * LANES...]
    pallas_call x1, Pallas kernels: 7.96 us -> 5.55 us  [step(): call(last_kernel, 'last', sds((x.shape[1], 2 * LANES), F32), [SMEM] + [VM...]
    ppermute x2, waiting for transfers between devices: 8.75 us -> 10.9 us  [step(): got_prev = lax.ppermute(to_p, AXIS, to_prev)]
  transfers between devices with their start and end apart: 8 -> 8, of which waited for: 2 -> 2; matrix products, arithmetic and copies ran while one was open for 2% -> 0% of each run, Pallas kernels for 48% -> 40%
where the time goes in v3:
time: 152 us; the launch traced here: 151 us
  Pallas kernels  120 us (79%)
  starting transfers between devices  10.9 us (7%)
  waiting for transfers between devices  10.9 us (7%)
  local copies, waits for them, and re-layouts  5.45 us (4%)
  between operations  2.56 us (2%)
    pallas_call x2, Pallas kernels, step(): part = local(counts, dst, src, w, grad)  28.6 us
    pallas_call x1, Pallas kernels, step(): call(functools.partial(reduce_kernel, num_dev), 'reduce', [sds(grad_one.s...  15.1 us
    pallas_call x1, Pallas kernels, step(): part = local(counts, src, dst, w, tab_one)  14.3 us
    pallas_call x1, Pallas kernels, step(): part = local(counts, src, dst, w, tab_two)  14.3 us
    ppermute x2, waiting for transfers between devices, step(): got_prev = lax.ppermute(to_p, AXIS, to_prev)  10.9 us
    pallas_call x1, Pallas kernels, step(): call(functools.partial(middle_kernel, chunk_h), 'middle', [sds((2 * LANES...  10.6 us
    pallas_call x1, Pallas kernels, step(): call(functools.partial(loss_kernel, chunk_h, classes), 'loss', [sds((8, L...  10.5 us
    pallas_call x1, Pallas kernels, step(): call(functools.partial(first_kernel, num_dev), 'first', [tab_f, half_b, h...  9.56 us
  transfers between devices with their start and end apart: 8, of which 2 were waited for; matrix products, arithmetic and copies ran while one was open for 0% of the time, Pallas kernels for 40%

profile of v3, /device:TPU:0, one launch (start us, length us, event | category | flops | bytes accessed | tf_op | source)
XLA Modules:
  0.0 150.6 jit_solution(16297049094426260052)
XLA Ops:
  0.6 0.7 broadcast_multiply_fusion
  1.3 0.0 copy-start
  1.4 1.0 copy-done
  2.4 0.0 copy-start.2
  2.4 0.9 copy-done.2
  3.3 0.0 copy-start.6
  3.3 0.7 copy-done.6
  4.0 0.0 copy-start.11
  4.0 0.0 copy-start.3
  4.0 0.0 copy-start.4
  4.0 0.0 copy-start.5
  4.0 9.6 %first.1 = (f32[4096,128]{1,0:T(8,128)S(1)}, bf16[1024,256]{1,0:T(8,128)(2,1)S(1)}, bf16[1024,256]{1,0:T(8,128)(2,1)S(1)}, f32[8,128]{1,0:T(8,128)S(1)}) custom-call(bf16[2048,128]{1,0:T(8,128)(2,1)S(1)} %copy-done, f32[128,256]{1,0:T(8,128)S(1)} %copy-done.2, s32[16,128]{1,0:T(8,128)S(1)} %mul.13.send, s32[16,128]{1,0:T(8,128)S(1)} %bitcast.42), custom_call_target="tpu_custom_call" | custom-call | flops 1000000000 | bytes 8388608 | tf_op jit(solution)/shard_map/first/pallas_call | solution.py:455
  13.6 0.0 copy-start.9
  13.6 1.3 copy-done.9
  14.9 0.1 collective-permute-start
  15.0 3.4 %collective-permute-start.1 = (bf16[1024,256]{1,0:T(8,128)(2,1)S(1)}, bf16[1024,256]{1,0:T(8,128)(2,1)S(1)}, u32[]{:S(2)}, u32[]{:S(2)}) collective-permute-start(bf16[1024,256]{1,0:T(8,128)(2,1)S(1)} %get-tuple-element.32), channel_id=1, source_target_pairs={{0,15},{1,0},{2,1},{3,2},{4,3},{5,4},{6,5},{7,6},{8,7},{9,8},{10,9... | collective-permute-start | bytes 1572872 | tf_op jit(solution)/shard_map/ppermute | solution.py:460
  18.4 0.0 copy-done.11
  18.5 0.1 copy.13
  18.6 0.0 copy-start.10
  18.6 0.0 copy-done.3
  18.6 0.0 copy-done.4
  18.6 0.0 copy-done.5
  18.6 2.4 %prep.1 = (s32[72,128]{1,0:T(8,128)S(1)}, s32[72,128]{1,0:T(8,128)S(1)}, f32[72,128]{1,0:T(8,128)S(1)}, s32[2]{0:T(128)S(1)}) custom-call(s32[64,128]{1,0:T(8,128)S(1)} %bitcast.39, s32[64,128]{1,0:T(8,128)S(1)} %bitcast.40, f32[64,128]{1,0:T(8,128)S(1)} %bitcast.41), custom_call_target="tpu_custom_call" | custom-call | flops 1000000000 | bytes 8388608 | tf_op jit(solution)/shard_map/prep/pallas_call | solution.py:464
  21.1 0.0 copy-done.10
  21.1 14.3 %local_edges.4.part = f32[4096,128]{1,0:T(8,128)S(1)} custom-call(s32[2]{0:T(128)S(1)} %get-tuple-element.26.counts, s32[9216]{0:T(1024)S(1)} %bitcast.18, s32[9216]{0:T(1024)S(1)} %bitcast.25, f32[9216]{0:T(1024)S(1)} %bitcast.32, f32[4096,128]{1,0:T(8,128)S(1)} %copy-done.10), custom_call_target="tpu_custom_call" | custom-call | flops 10000000000 | bytes 8388608 | tf_op jit(solution)/shard_map/local_edges/pallas_call | solution.py:472
  35.4 0.0 collective-permute-done.from_prev
  35.4 0.0 collective-permute-done.1.from_next
  35.4 9.1 %hidden.1 = (bf16[2048,256]{1,0:T(8,128)(2,1)S(1)}, f32[4096,128]{1,0:T(8,128)S(1)}, bf16[1536,128]{1,0:T(8,128)(2,1)S(1)}, bf16[1536,128]{1,0:T(8,128)(2,1)S(1)}) custom-call(s32[2]{0:T(128)S(1)} %get-tuple-element.26.counts, s32[9216]{0:T(1024)S(1)} %bitcast.19, s32[9216]{0:T(1024)S(1)} %bitcast.26, f32[9216]{0:T(1024)S(1)} %bitcast.33, ...), custom_call_target="tpu_custom_call" | custom-call | flops 1000000000 | bytes 8388608 | tf_op jit(solution)/shard_map/hidden/pallas_call | solution.py:473
  44.6 0.1 collective-permute-start.2
  44.6 3.5 %collective-permute-start.3 = (bf16[1536,128]{1,0:T(8,128)(2,1)S(1)}, bf16[1536,128]{1,0:T(8,128)(2,1)S(1)}, u32[]{:S(2)}, u32[]{:S(2)}) collective-permute-start(bf16[1536,128]{1,0:T(8,128)(2,1)S(1)} %get-tuple-element.35), channel_id=1, source_target_pairs={{0,15},{1,0},{2,1},{3,2},{4,3},{5,4},{6,5},{7,6},{8,7},{9,8},{10,9... | collective-permute-start | bytes 1179656 | tf_op jit(solution)/shard_map/ppermute | solution.py:478
  48.2 0.0 copy-start.7
  48.2 0.0 copy-start.8
  48.2 14.3 %local_edges.5.part = f32[4096,128]{1,0:T(8,128)S(1)} custom-call(s32[2]{0:T(128)S(1)} %get-tuple-element.26.counts, s32[9216]{0:T(1024)S(1)} %bitcast.20, s32[9216]{0:T(1024)S(1)} %bitcast.27, f32[9216]{0:T(1024)S(1)} %bitcast.34, f32[4096,128]{1,0:T(8,128)S(1)} %get-tuple-element.36.table), custom_call_target="tpu_custom_call" | custom-call | flops 10000000000 | bytes 8388608 | tf_op jit(solution)/shard_map/local_edges/pallas_call | solution.py:479
  62.5 0.0 collective-permute-done.2.from_prev
  62.5 0.0 collective-permute-done.3.from_next
  62.5 0.0 copy-done.7
  62.5 0.0 copy-done.8
  62.5 10.5 %loss.1 = (f32[8,128]{1,0:T(8,128)S(1)}, f32[4096,128]{1,0:T(8,128)S(1)}, f32[1536,128]{1,0:T(8,128)S(1)}, f32[1536,128]{1,0:T(8,128)S(1)}) custom-call(s32[2]{0:T(128)S(1)} %get-tuple-element.26.counts, s32[9216]{0:T(1024)S(1)} %bitcast.21, s32[9216]{0:T(1024)S(1)} %bitcast.28, f32[9216]{0:T(1024)S(1)} %bitcast.35, f32[8,128]{1,0:T(8,128)S(1)} %get-tuple-element.30.count, ...), custom_call_target="tpu_custom_call" | custom-call | flops 1000000000 | bytes 8388608 | tf_op jit(solution)/shard_map/loss/pallas_call | solution.py:480
  73.0 0.1 collective-permute-start.4
  73.1 0.5 collective-permute-start.5
  73.6 14.3 %local_edges.6.part = f32[4096,128]{1,0:T(8,128)S(1)} custom-call(s32[2]{0:T(128)S(1)} %get-tuple-element.26.counts, s32[9216]{0:T(1024)S(1)} %bitcast.29, s32[9216]{0:T(1024)S(1)} %bitcast.22, f32[9216]{0:T(1024)S(1)} %bitcast.36, f32[4096,128]{1,0:T(8,128)S(1)} %get-tuple-element.39.table), custom_call_target="tpu_custom_call" | custom-call | flops 10000000000 | bytes 8388608 | tf_op jit(solution)/shard_map/local_edges/pallas_call | solution.py:486
  87.9 2.9 %collective-permute-done.4.got_prev = f32[1536,128]{1,0:T(8,128)S(1)} collective-permute-done((f32[1536,128]{1,0:T(8,128)S(1)}, f32[1536,128]{1,0:T(8,128)S(1)}, u32[]{:S(2)}, u32[]{:S(2)}) %collective-permute-start.4) | collective-permute-done | bytes 786464 | tf_op jit(solution)/shard_map/ppermute | solution.py:484
  90.8 0.0 collective-permute-done.5.got_next
  90.8 10.6 %middle.1 = (f32[256,256]{1,0:T(8,128)S(1)}, f32[4096,128]{1,0:T(8,128)S(1)}, f32[2048,128]{1,0:T(8,128)S(1)}, f32[2048,128]{1,0:T(8,128)S(1)}) custom-call(s32[2]{0:T(128)S(1)} %get-tuple-element.26.counts, s32[9216]{0:T(1024)S(1)} %bitcast.23, s32[9216]{0:T(1024)S(1)} %bitcast.30, f32[9216]{0:T(1024)S(1)} %bitcast.37, s32[2048]{0:T(1024)S(1)} %bitcast.16, ...), custom_call_target="tpu_custom_call" | custom-call | flops 1000000000 | bytes 8388608 | tf_op jit(solution)/shard_map/middle/pallas_call | solution.py:487
  101.4 3.2 %collective-permute-start.6 = (f32[2048,128]{1,0:T(8,128)S(1)}, f32[2048,128]{1,0:T(8,128)S(1)}, u32[]{:S(2)}, u32[]{:S(2)}) collective-permute-start(f32[2048,128]{1,0:T(8,128)S(1)} %get-tuple-element.41), channel_id=1, source_target_pairs={{0,15},{1,0},{2,1},{3,2},{4,3},{5,4},{6,5},{7,6},{8,7},{9,8},{10,9... | collective-permute-start | bytes 3145736 | tf_op jit(solution)/shard_map/ppermute | solution.py:491
  104.6 0.0 collective-permute-start.7
  104.6 0.0 copy-start.1
  104.6 14.3 %local_edges.7.part = f32[4096,128]{1,0:T(8,128)S(1)} custom-call(s32[2]{0:T(128)S(1)} %get-tuple-element.26.counts, s32[9216]{0:T(1024)S(1)} %bitcast.31, s32[9216]{0:T(1024)S(1)} %bitcast.24, f32[9216]{0:T(1024)S(1)} %bitcast.38, f32[4096,128]{1,0:T(8,128)S(1)} %get-tuple-element.43.table), custom_call_target="tpu_custom_call" | custom-call | flops 10000000000 | bytes 8388608 | tf_op jit(solution)/shard_map/local_edges/pallas_call | solution.py:493
  118.9 8.0 %collective-permute-done.6.got_prev = f32[2048,128]{1,0:T(8,128)S(1)} collective-permute-done((f32[2048,128]{1,0:T(8,128)S(1)}, f32[2048,128]{1,0:T(8,128)S(1)}, u32[]{:S(2)}, u32[]{:S(2)}) %collective-permute-start.6) | collective-permute-done | bytes 1048608 | tf_op jit(solution)/shard_map/ppermute | solution.py:491
  126.9 0.0 collective-permute-done.7.got_next
  126.9 0.0 copy-done.1
  126.9 5.6 %last.1.one = f32[128,256]{1,0:T(8,128)S(1)} custom-call(s32[2048]{0:T(1024)S(1)} %bitcast.17, f32[2048,128]{1,0:T(8,128)S(1)} %collective-permute-done.6.got_prev, f32[2048,128]{1,0:T(8,128)S(1)} %collective-permute-done.7.got_next, f32[4096,128]{1,0:T(8,128)S(1)} %local_edges.7.part, bf16[2048,128]{1,0:T(8,128)(2,1)S(1)} %copy-done.1), custom_call_target="tpu_custom_call" | custom-call | flops 1000000000 | bytes 8388608 | tf_op jit(solution)/shard_map/last/pallas_call | solution.py:495
  132.5 15.1 %reduce.1 = (f32[128,256]{1,0:T(8,128)S(1)}, f32[172,256]{1,0:T(8,128)S(1)}, f32[1,1]{1,0:T(1,128)}) custom-call(f32[128,256]{1,0:T(8,128)S(1)} %last.1.one, f32[256,256]{1,0:T(8,128)S(1)} %get-tuple-element.44.two, f32[8,128]{1,0:T(8,128)S(1)} %get-tuple-element.45.loss, f32[8,128]{1,0:T(8,128)S(1)} %get-tuple-element.30.count), custom_call_target="tpu_custom_call" | custom-call | flops 1000000000 | bytes 8388608 | tf_op jit(solution)/shard_map/reduce/pallas_call | solution.py:498
  148.1 0.7 copy.21
  148.8 0.7 copy.22
  (4 shorter events, 0.0 us)
Async XLA Ops:
  1.3 1.0 copy-start
  2.4 0.9 copy-start.2
  3.3 0.7 copy-start.6
  4.0 14.5 %copy-start.11 = (f32[256,172]{0,1:T(8,128)S(1)}, f32[256,172]{0,1:T(8,128)}, u32[]{:S(2)}) copy-start(f32[256,172]{0,1:T(8,128)} %param.11) | copy-start | bytes 528388
  4.0 14.6 %copy-start.3 = (s32[8192]{0:T(1024)S(1)}, s32[8192]{0:T(1024)}, u32[]{:S(2)}) copy-start(s32[8192]{0:T(1024)} %param.13) | copy-start | bytes 98308
  4.0 14.6 %copy-start.4 = (s32[8192]{0:T(1024)S(1)}, s32[8192]{0:T(1024)}, u32[]{:S(2)}) copy-start(s32[8192]{0:T(1024)} %param.14) | copy-start | bytes 98308
  4.0 14.6 %copy-start.5 = (f32[8192]{0:T(1024)S(1)}, f32[8192]{0:T(1024)}, u32[]{:S(2)}) copy-start(f32[8192]{0:T(1024)} %param.15) | copy-start | bytes 98308
  13.6 1.3 copy-start.9
  14.9 20.5 %collective-permute-start = (bf16[1024,256]{1,0:T(8,128)(2,1)S(1)}, bf16[1024,256]{1,0:T(8,128)(2,1)S(1)}, u32[]{:S(2)}, u32[]{:S(2)}) collective-permute-start(bf16[1024,256]{1,0:T(8,128)(2,1)S(1)} %get-tuple-element.31), channel_id=1, source_target_pairs={{0,1},{1,2},{2,3},{3,4},{4,5},{5,6},{6,7},{7,8},{8,9},{9,10},{10,1... | collective-permute-start | bytes 1572872 | tf_op jit(solution)/shard_map/ppermute | solution.py:459
  15.0 20.4 %collective-permute-start.1 = (bf16[1024,256]{1,0:T(8,128)(2,1)S(1)}, bf16[1024,256]{1,0:T(8,128)(2,1)S(1)}, u32[]{:S(2)}, u32[]{:S(2)}) collective-permute-start(bf16[1024,256]{1,0:T(8,128)(2,1)S(1)} %get-tuple-element.32), channel_id=1, source_target_pairs={{0,15},{1,0},{2,1},{3,2},{4,3},{5,4},{6,5},{7,6},{8,7},{9,8},{10,9... | collective-permute-start | bytes 1572872 | tf_op jit(solution)/shard_map/ppermute | solution.py:460
  18.6 2.5 %copy-start.10 = (f32[4096,128]{1,0:T(8,128)S(1)}, f32[4096,128]{1,0:T(8,128)}, u32[]{:S(2)}) copy-start(f32[4096,128]{1,0:T(8,128)} %copy-done.9) | copy-start | bytes 6291460
  44.6 17.9 %collective-permute-start.2 = (bf16[1536,128]{1,0:T(8,128)(2,1)S(1)}, bf16[1536,128]{1,0:T(8,128)(2,1)S(1)}, u32[]{:S(2)}, u32[]{:S(2)}) collective-permute-start(bf16[1536,128]{1,0:T(8,128)(2,1)S(1)} %get-tuple-element.34), channel_id=1, source_target_pairs={{0,1},{1,2},{2,3},{3,4},{4,5},{5,6},{6,7},{7,8},{8,9},{9,10},{10,1... | collective-permute-start | bytes 1179656 | tf_op jit(solution)/shard_map/ppermute | solution.py:477
  44.6 17.9 %collective-permute-start.3 = (bf16[1536,128]{1,0:T(8,128)(2,1)S(1)}, bf16[1536,128]{1,0:T(8,128)(2,1)S(1)}, u32[]{:S(2)}, u32[]{:S(2)}) collective-permute-start(bf16[1536,128]{1,0:T(8,128)(2,1)S(1)} %get-tuple-element.35), channel_id=1, source_target_pairs={{0,15},{1,0},{2,1},{3,2},{4,3},{5,4},{6,5},{7,6},{8,7},{9,8},{10,9... | collective-permute-start | bytes 1179656 | tf_op jit(solution)/shard_map/ppermute | solution.py:478
  48.2 14.4 %copy-start.7 = (s32[2048]{0:T(1024)S(1)}, s32[2048]{0:T(1024)}, u32[]{:S(2)}) copy-start(s32[2048]{0:T(1024)} %param.17) | copy-start | bytes 24580
  48.2 14.4 %copy-start.8 = (s32[2048]{0:T(1024)S(1)}, s32[2048]{0:T(1024)}, u32[]{:S(2)}) copy-start(s32[2048]{0:T(1024)} %param.16) | copy-start | bytes 24580
  73.0 17.8 %collective-permute-start.4 = (f32[1536,128]{1,0:T(8,128)S(1)}, f32[1536,128]{1,0:T(8,128)S(1)}, u32[]{:S(2)}, u32[]{:S(2)}) collective-permute-start(f32[1536,128]{1,0:T(8,128)S(1)} %get-tuple-element.37), channel_id=1, source_target_pairs={{0,15},{1,0},{2,1},{3,2},{4,3},{5,4},{6,5},{7,6},{8,7},{9,8},{10,9... | collective-permute-start | bytes 2359304 | tf_op jit(solution)/shard_map/ppermute | solution.py:484
  73.1 17.7 %collective-permute-start.5 = (f32[1536,128]{1,0:T(8,128)S(1)}, f32[1536,128]{1,0:T(8,128)S(1)}, u32[]{:S(2)}, u32[]{:S(2)}) collective-permute-start(f32[1536,128]{1,0:T(8,128)S(1)} %get-tuple-element.38), channel_id=1, source_target_pairs={{0,1},{1,2},{2,3},{3,4},{4,5},{5,6},{6,7},{7,8},{8,9},{9,10},{10,1... | collective-permute-start | bytes 2359304 | tf_op jit(solution)/shard_map/ppermute | solution.py:485
  101.4 25.5 %collective-permute-start.6 = (f32[2048,128]{1,0:T(8,128)S(1)}, f32[2048,128]{1,0:T(8,128)S(1)}, u32[]{:S(2)}, u32[]{:S(2)}) collective-permute-start(f32[2048,128]{1,0:T(8,128)S(1)} %get-tuple-element.41), channel_id=1, source_target_pairs={{0,15},{1,0},{2,1},{3,2},{4,3},{5,4},{6,5},{7,6},{8,7},{9,8},{10,9... | collective-permute-start | bytes 3145736 | tf_op jit(solution)/shard_map/ppermute | solution.py:491
  104.6 22.3 %collective-permute-start.7 = (f32[2048,128]{1,0:T(8,128)S(1)}, f32[2048,128]{1,0:T(8,128)S(1)}, u32[]{:S(2)}, u32[]{:S(2)}) collective-permute-start(f32[2048,128]{1,0:T(8,128)S(1)} %get-tuple-element.42), channel_id=1, source_target_pairs={{0,1},{1,2},{2,3},{3,4},{4,5},{5,6},{6,7},{7,8},{8,9},{9,10},{10,1... | collective-permute-start | bytes 3145736 | tf_op jit(solution)/shard_map/ppermute | solution.py:492
  104.6 22.3 %copy-start.1 = (bf16[2048,128]{1,0:T(8,128)(2,1)S(1)}, bf16[2048,128]{1,0:T(8,128)(2,1)}, u32[]{:S(2)}) copy-start(bf16[2048,128]{1,0:T(8,128)(2,1)} %x.5) | copy-start | bytes 1572868

commit v4 on v3

--- a/solution.py
+++ b/solution.py
@@ -42,13 +42,14 @@
 
     def body(c, _):
         base = c * chunk
+        w_chunk = w.at[pl.ds(pl.multiple_of(base, chunk), chunk)]
         for g in range(0, chunk, group):
             pend = []
             for u in range(group):
                 k = base + g + u
                 s = pl.multiple_of(from_idx[k], 2)
                 d = pl.multiple_of(to_idx[k], 2)
-                pend.append((d, accs[u][pl.ds(d, 2), :] + table[pl.ds(s, 2), :] * w[k]))
+                pend.append((d, accs[u][pl.ds(d, 2), :] + table[pl.ds(s, 2), :] * w_chunk[g + u : g + u + 1, :]))
             for u in range(group):
                 accs[u][pl.ds(pend[u][0], 2), :] = pend[u][1]
         return 0
@@ -56,13 +57,13 @@
     lax.fori_loop(first, last, body, 0)
 
 
-def one_hot_rows(idx, line, table):
-    lane = lax.broadcasted_iota(jnp.int32, (LANES, LANES), 1) * 2
+def one_hot_rows(idx, which, start, table):
+    lane = lax.broadcasted_iota(jnp.int32, (LANES, LANES), 1)
     hot = []
     for q in range(2):
-        want = spread(idx[pl.ds(line + q, 1), :])
+        want = spread(idx[which : which + 1, pl.ds(pl.multiple_of(start + q * LANES, LANES), LANES)])
         hot.append(
-            jnp.concatenate([jnp.where(want == lane + 2 * LANES * j, 1.0, 0.0).astype(BF16) for j in range(table.shape[0] // LANES)], axis=1)
+            jnp.concatenate([jnp.where(want == lane + LANES * j, 1.0, 0.0).astype(BF16) for j in range(table.shape[0] // LANES)], axis=1)
         )
     return dot(jnp.concatenate(hot, axis=0), table[...])
 
@@ -75,20 +76,20 @@
     return pltpu.roll(v, LANES // 2, 1)
 
 
-def gather_rows(idx, line, table, out):
+def gather_rows(idx, which, table, out):
     @pl.loop(0, out.shape[0], step=256)
     def _(i):
-        out[pl.ds(pl.multiple_of(i, 256), 256), :] = one_hot_rows(idx, line + i // LANES, table).astype(BF16)
-
-
-def gather_packed(idx, line, table, out):
+        out[pl.ds(pl.multiple_of(i, 256), 256), :] = one_hot_rows(idx, which, i, table).astype(BF16)
+
+
+def gather_packed(idx, which, table, out):
     halo = out.shape[0] * 2 // 3
 
     @pl.loop(0, halo // 2, step=256)
     def _(i):
         i = pl.multiple_of(i, 256)
-        a = one_hot_rows(idx, line + i // LANES, table)
-        b = one_hot_rows(idx, line + (halo // 2 + i) // LANES, table)
+        a = one_hot_rows(idx, which, i, table)
+        b = one_hot_rows(idx, which, halo // 2 + i, table)
         out[pl.ds(i, 256), :] = a[:, :LANES].astype(BF16)
         out[pl.ds(halo // 2 + i, 256), :] = b[:, :LANES].astype(BF16)
         out[pl.ds(halo + i, 256), :] = jnp.where(low_lanes(256), a[:, LANES:], swap_lanes(b[:, LANES:])).astype(BF16)
@@ -156,7 +157,7 @@
     )
 
 
-def first_kernel(n, x, w1, send, mask, tab, to_prev, to_next, count, tab_b, mine, theirs, send_sem, recv_sem):
+def first_kernel(n, x, w1, send, mask, after, tab, to_prev, to_next, count, tab_b, mine, theirs, send_sem, recv_sem):
     me, met = greet(n)
     rows = x.shape[0]
     mask_f = mask[...].astype(F32)
@@ -175,7 +176,7 @@
     for c in copies:
         c.start()
     gather_rows(send, 0, tab_b, to_prev)
-    gather_rows(send, send.shape[0] // 2, tab_b, to_next)
+    gather_rows(send, 1, tab_b, to_next)
     for c in copies:
         c.wait()
     total = mine[...] + jnp.sum(theirs[...], axis=0)
@@ -239,9 +240,12 @@
     mean[...] = jnp.sum(full[tail : tail + 8, :], keepdims=True) / count[0:1, 0:1]
 
 
-def prep_kernel(chunk, rows, src, dst, w, src_out, dst_out, w_out, counts, total):
+def prep_kernel(chunk, rows, src, dst, w, send, src_out, dst_out, w_out, back, counts, total):
     lines = src.shape[0]
     slots = src_out.shape[0]
+    per = send.shape[1] // LANES
+    for i in range(2 * per):
+        back[i : i + 1, :] = send[i // per : i // per + 1, (i % per) * LANES : (i % per + 1) * LANES] * 2
     live = w[...] != 0.0
     halo = src[...] >= rows
     at = lambda shape, axis: lax.broadcasted_iota(jnp.int32, shape, axis)
@@ -284,7 +288,11 @@
     high = plane(2).astype(jnp.int32)
     src_out[...] = ((high >> 3) * 256 + plane(0).astype(jnp.int32)) * 2
     dst_out[...] = ((high & 7) * 256 + plane(1).astype(jnp.int32)) * 2
-    w_out[...] = (plane(3) + plane(4) + plane(5)) * 2.0
+    total[0:slots, :] = (plane(3) + plane(4) + plane(5)) * 2.0
+
+    @pl.loop(0, slots)
+    def _(r):
+        w_out[pl.ds(pl.multiple_of(r * LANES, LANES), LANES), :] = spread(total[pl.ds(r, 1), :])
 
 
 def local_kernel(chunk, n_acc, counts, from_idx, to_idx, w, table, out, *accs):
@@ -337,7 +345,15 @@
             out[pl.ds(halo + i, 256), :] = jnp.where(low_lanes(256), a_odd, swap_lanes(b_odd))
 
 
-def hidden_kernel(chunk, counts, src, dst, w, send, from_prev, from_next, part, w2, hid, tab, to_prev, to_next, htab, tab_b, *accs):
+def padded(w, buf):
+    low = w.shape[0] // 8 * 8
+    buf[low:, :] = jnp.zeros((buf.shape[0] - low, buf.shape[1]), F32)
+    buf[0 : w.shape[0], :] = w[...]
+    return buf[...].astype(BF16)
+
+
+def hidden_kernel(chunk, counts, src, dst, w, send, from_prev, from_next, part, w2, hid, tab, to_prev, to_next, htab, tab_b, w2_pad, *accs):
+    w2_b = padded(w2, w2_pad)
     forward_halo(chunk, counts, src, dst, w, from_prev, from_next, part, htab, accs, unpack_plain)
 
     @pl.loop(0, hid.shape[0], step=256)
@@ -345,13 +361,13 @@
         even, odd = halves(accs, i, 256)
         h = jnp.concatenate([jnp.maximum(even, 0.0), jnp.maximum(odd, 0.0)], axis=1).astype(BF16)
         hid[pl.ds(i, 256), :] = h
-        t = dot(h, w2[...]).astype(BF16)
+        t = dot(h, w2_b, COLS_A).astype(BF16)
         tab_b[pl.ds(i, 256), :] = t
         t = t.astype(F32)
         put_halves(tab, i, 256, t[:, :LANES], t[:, LANES:])
 
     gather_packed(send, 0, tab_b, to_prev)
-    gather_packed(send, send.shape[0] // 2, tab_b, to_next)
+    gather_packed(send, 1, tab_b, to_next)
 
 
 def loss_kernel(chunk, classes, counts, src, dst, w, count, from_prev, from_next, part, labels, mask, loss, grad, back_prev, back_next, htab, *accs):
@@ -361,22 +377,23 @@
     scale = 1.0 / count[0:1, :]
     loss[...] = jnp.zeros_like(loss)
 
-    @pl.loop(0, labels.shape[0])
-    def _(b):
-        even, odd = halves(accs, b * LANES, LANES)
-        label = spread(labels[pl.ds(b, 1), :])
-        keep = spread(mask[pl.ds(b, 1), :]).astype(F32)
-        odd = jnp.where(live, odd, -jnp.inf)
-        top = jnp.max(jnp.maximum(even, odd), axis=1, keepdims=True)
-        total = jnp.sum(jnp.exp(even - top) + jnp.exp(odd - top), axis=1, keepdims=True)
-        norm = top + jnp.log(total)
-        hit_even, hit_odd = lane == label, lane + LANES == label
-        picked = jnp.where(hit_even, even, 0.0) + jnp.where(hit_odd, odd, 0.0)
-        per_row = jnp.where(lane == 0, norm, 0.0) - picked
-        loss[...] += jnp.sum((keep * per_row).reshape(LANES // 8, 8, LANES), axis=0)
-        d_even = (jnp.exp(even - norm) - hit_even.astype(F32)) * (keep * scale)
-        d_odd = (jnp.exp(odd - norm) - hit_odd.astype(F32)) * (keep * scale)
-        put_halves(grad, b * LANES, LANES, d_even, d_odd)
+    @pl.loop(0, labels.shape[0] // 2)
+    def _(pair):
+        for b in (pair * 2, pair * 2 + 1):
+            even, odd = halves(accs, b * LANES, LANES)
+            label = spread(labels[pl.ds(b, 1), :])
+            keep = spread(mask[pl.ds(b, 1), :]).astype(F32)
+            odd = jnp.where(live, odd, -jnp.inf)
+            top = jnp.max(jnp.maximum(even, odd), axis=1, keepdims=True)
+            total = jnp.sum(jnp.exp(even - top) + jnp.exp(odd - top), axis=1, keepdims=True)
+            norm = top + jnp.log(total)
+            hit_even, hit_odd = lane == label, lane + LANES == label
+            picked = jnp.where(hit_even, even, 0.0) + jnp.where(hit_odd, odd, 0.0)
+            per_row = jnp.where(lane == 0, norm, 0.0) - picked
+            loss[...] += jnp.sum((keep * per_row).reshape(LANES // 8, 8, LANES), axis=0)
+            d_even = (jnp.exp(even - norm) - hit_even.astype(F32)) * (keep * scale)
+            d_odd = (jnp.exp(odd - norm) - hit_odd.astype(F32)) * (keep * scale)
+            put_halves(grad, b * LANES, LANES, d_even, d_odd)
 
     backward_halo(chunk, counts, src, dst, w, grad, back_prev, back_next, accs)
 
@@ -389,7 +406,8 @@
     return_rows(send, 0, got_next, accs)
 
 
-def middle_kernel(chunk, counts, src, dst, w, send, got_prev, got_next, part, hid, w2, grad_two, grad, back_prev, back_next, returned, *accs):
+def middle_kernel(chunk, counts, src, dst, w, send, got_prev, got_next, part, hid, w2, grad_two, grad, back_prev, back_next, returned, w2_pad, *accs):
+    w2_b = padded(w2, w2_pad)
     split = returned.shape[0] // 2
     unpack_rows(got_prev, returned, 0)
     unpack_rows(got_next, returned, split // 2)
@@ -402,7 +420,7 @@
         d_tab = jnp.concatenate([even, odd], axis=1).astype(BF16)
         h = hid[pl.ds(i, 256), :]
         grad_two[...] += dot(d_tab, h, ROWS_A)
-        d_hid = dot(d_tab, w2[...], COLS_A)
+        d_hid = dot(d_tab, w2_b)
         d_pre = jnp.where(h > 0, d_hid, 0.0)
         put_halves(grad, i, 256, d_pre[:, :LANES], d_pre[:, LANES:])
 
@@ -420,7 +438,7 @@
         grad_one[...] += dot(x[pl.ds(i, 256), :], d_tab, ROWS_A)
 
 
-def call(body, name, outs, ins, scratch, flops=10**9, out_specs=None, collective=None, vmem=32):
+def call(body, name, outs, ins, scratch, flops=10**9, out_specs=None, collective=None, vmem=14):
     extra = {} if collective is None else dict(collective_id=collective, has_side_effects=True)
     return pl.pallas_call(
         body, name=name, out_shape=outs, in_specs=ins, out_specs=out_specs or jax.tree.map(lambda _: VMEM, outs),
@@ -448,32 +466,32 @@
         chunk_l, chunk_h = 64, 32
         lines = edges // LANES
         slots = lines + 8
-        w2 = jnp.pad(w_two, ((0, 0), (0, 2 * LANES - classes))).astype(BF16)
+        w2 = w_two.T
+        w2_pad = (2 * LANES, 2 * LANES)
         mask = mask.reshape(-1, LANES)
-        send = send.reshape(-1) * 2
+
+        lined = lambda a: a.reshape(lines, LANES)
+        ints = sds((slots, LANES), jnp.int32)
+        src, dst, w, back, counts = call(
+            functools.partial(prep_kernel, PREP_CHUNK, rows), "prep", [ints, ints, sds((slots * LANES, LANES), F32), sds((2 * halo // LANES, LANES), jnp.int32), sds((2,), jnp.int32)], [VMEM] * 4,
+            [(6 * slots, LANES)], out_specs=[VMEM] * 4 + [SMEM], vmem=8,
+        )(lined(edge_src), lined(edge_dst), lined(edge_w), send)
+        src, dst, back = src.reshape(-1), dst.reshape(-1), back.reshape(-1)
 
         tab_one, to_p, to_n, count = call(
-            functools.partial(first_kernel, num_dev), "first", [tab_f, half_b, half_b, one], [VMEM] * 4,
-            [tab_b, (8, LANES), (num_dev - 1, 8, LANES), dma((num_dev - 1,)), dma((num_dev - 1,))], collective=0,
-        )(x, w_one, send.reshape(-1, LANES), mask)
+            functools.partial(first_kernel, num_dev), "first", [tab_f, half_b, half_b, one], [VMEM] * 4 + [SMEM],
+            [tab_b, (8, LANES), (num_dev - 1, 8, LANES), dma((num_dev - 1,)), dma((num_dev - 1,))], collective=0, vmem=8,
+        )(x, w_one, send, mask, counts)
         from_prev = lax.ppermute(to_n, AXIS, to_next)
         from_next = lax.ppermute(to_p, AXIS, to_prev)
 
-        lined = lambda a: a.reshape(lines, LANES)
-        ints = sds((slots, LANES), jnp.int32)
-        src, dst, w, counts = call(
-            functools.partial(prep_kernel, PREP_CHUNK, rows), "prep", [ints, ints, sds((slots, LANES), F32), sds((2,), jnp.int32)], [VMEM] * 3,
-            [(6 * slots, LANES)], out_specs=[VMEM] * 3 + [SMEM],
-        )(lined(edge_src), lined(edge_dst), lined(edge_w))
-        src, dst, w = src.reshape(-1), dst.reshape(-1), w.reshape(-1)
-
-        walk = [SMEM] * 4
+        walk = [SMEM] * 3 + [VMEM]
         local = call(functools.partial(local_kernel, chunk_l, 4), "local_edges", tab_f, walk + [VMEM], [tab] * 4, 10**10)
         part = local(counts, src, dst, w, tab_one)
         hid, tab_two, to_p, to_n = call(
             functools.partial(hidden_kernel, chunk_h), "hidden", [sds((rows, 2 * LANES), BF16), tab_f, pack_b, pack_b],
-            walk + [VMEM] * 5, [tab, tab_b] + [tab] * 4,
-        )(counts, src, dst, w, send.reshape(-1, LANES), from_prev, from_next, part, w2)
+            walk + [VMEM] * 5, [tab, tab_b, w2_pad] + [tab] * 4,
+        )(counts, src, dst, w, send, from_prev, from_next, part, w2)
         from_prev = lax.ppermute(to_n, AXIS, to_next)
         from_next = lax.ppermute(to_p, AXIS, to_prev)
         part = local(counts, src, dst, w, tab_two)
@@ -486,13 +504,13 @@
         part = local(counts, dst, src, w, grad)
         grad_two, grad, to_p, to_n = call(
             functools.partial(middle_kernel, chunk_h), "middle", [sds((2 * LANES, 2 * LANES), F32), tab_f, half_f, half_f],
-            walk + [SMEM] + [VMEM] * 5, [tab] * 5,
-        )(counts, src, dst, w, send, got_prev, got_next, part, hid, w2)
+            walk + [SMEM] + [VMEM] * 5, [tab, w2_pad] + [tab] * 4,
+        )(counts, src, dst, w, back, got_prev, got_next, part, hid, w2)
         got_prev = lax.ppermute(to_p, AXIS, to_prev)
         got_next = lax.ppermute(to_n, AXIS, to_next)
         part = local(counts, dst, src, w, grad)
 
-        grad_one = call(last_kernel, "last", sds((x.shape[1], 2 * LANES), F32), [SMEM] + [VMEM] * 4, [tab] * 4)(send, got_prev, got_next, part, x)
+        grad_one = call(last_kernel, "last", sds((x.shape[1], 2 * LANES), F32), [SMEM] + [VMEM] * 4, [tab] * 4)(back, got_prev, got_next, part, x)
         lines = 2 * x.shape[1] + 2 * (-(-classes // 8) * 8) + 8
         lines = -(-lines // (8 * num_dev)) * 8 * num_dev
         grad_one, grad_two, mean = call(

time: 152 us -> 149 us (0.980); the launches traced: 151 us -> 149 us
  waiting for transfers between devices: 10.9 us -> 37.6 us
  Pallas kernels: 120 us -> 96.6 us
  starting transfers between devices: 10.9 us -> 8.26 us
    ppermute x2, waiting for transfers between devices: 10.9 us -> 24.6 us  [step(): got_prev = lax.ppermute(to_p, AXIS, to_prev)]
    pallas_call x2, Pallas kernels: 28.6 us -> 15.4 us  [step(): part = local(counts, dst, src, w, grad)]
    pallas_call x1, Pallas kernels: 2.42 us -> 10.1 us  [step(): call(functools.partial(prep_kernel, PREP_CHUNK, rows), 'prep', [ints, int...]
    ppermute x2, waiting for transfers between devices: 0.01 us -> 7.05 us  [step(): got_next = lax.ppermute(to_n, AXIS, to_next)]
    pallas_call x1, Pallas kernels: 14.3 us -> 7.72 us  [step(): part = local(counts, src, dst, w, tab_one)]
    pallas_call x1, Pallas kernels: 14.3 us -> 7.72 us  [step(): part = local(counts, src, dst, w, tab_two)]
    ppermute x2, waiting for transfers between devices: 0.01 us -> 5.94 us  [step(): from_prev = lax.ppermute(to_n, AXIS, to_next)]
    ppermute x2, starting transfers between devices: 3.25 us -> 0.1 us  [step(): got_prev = lax.ppermute(to_p, AXIS, to_prev)]
  transfers between devices with their start and end apart: 8 -> 8, of which waited for: 2 -> 6; matrix products, arithmetic and copies ran while one was open for 0% -> 0% of each run, Pallas kernels for 40% -> 21%
where the time goes in v4:
time: 149 us
  Pallas kernels  96.6 us (65%)
  waiting for transfers between devices  37.6 us (25%)
  starting transfers between devices  8.26 us (6%)
  local copies, waits for them, and re-layouts  4.37 us (3%)
  between operations  2.54 us (2%)
    ppermute x2, waiting for transfers between devices, step(): got_prev = lax.ppermute(to_p, AXIS, to_prev)  24.6 us
    pallas_call x2, Pallas kernels, step(): part = local(counts, dst, src, w, grad)  15.4 us
    pallas_call x1, Pallas kernels, step(): call(functools.partial(reduce_kernel, num_dev), 'reduce', [sds(grad_one.s...  12.8 us
    pallas_call x1, Pallas kernels, step(): call(functools.partial(first_kernel, num_dev), 'first', [tab_f, half_b, h...  10.1 us
    pallas_call x1, Pallas kernels, step(): call(functools.partial(prep_kernel, PREP_CHUNK, rows), 'prep', [ints, int...  10.1 us
    pallas_call x1, Pallas kernels, step(): call(functools.partial(middle_kernel, chunk_h), 'middle', [sds((2 * LANES...  9.92 us
    pallas_call x1, Pallas kernels, step(): call(functools.partial(hidden_kernel, chunk_h), 'hidden', [sds((rows, 2 *...  8.69 us
    pallas_call x1, Pallas kernels, step(): call(functools.partial(loss_kernel, chunk_h, classes), 'loss', [sds((8, L...  8.58 us
  transfers between devices with their start and end apart: 8, of which 6 were waited for; matrix products, arithmetic and copies ran while one was open for 0% of the time, Pallas kernels for 21%

profile of v4, /device:TPU:0, one launch (start us, length us, event | category | flops | bytes accessed | tf_op | source)
XLA Modules:
  0.0 149.4 jit_solution(1505472355589283596)
XLA Ops:
  0.6 0.0 copy-start.1
  0.6 0.0 copy-start.2
  0.7 0.7 copy-done.2
  1.4 0.0 copy-start.7
  1.4 0.8 copy-done.7
  2.2 0.0 copy-start.8
  2.2 0.8 copy-done.8
  2.9 0.0 copy-start.9
  2.9 0.8 copy-done.9
  3.7 0.0 copy-start.4
  3.7 0.0 copy-start.6
  3.7 10.1 %prep.1 = (s32[72,128]{1,0:T(8,128)S(1)}, s32[72,128]{1,0:T(8,128)S(1)}, f32[9216,128]{1,0:T(8,128)S(1)}, s32[16,128]{1,0:T(8,128)S(1)}, s32[2]{0:T(128)S(1)}) custom-call(s32[64,128]{1,0:T(8,128)S(1)} %bitcast.33, s32[64,128]{1,0:T(8,128)S(1)} %bitcast.34, f32[64,128]{1,0:T(8,128)S(1)} %bitcast.35, s32[2,1024]{1,0:T(2,128)S(1)} %copy-done.2), custom_call_target="tpu_custom_call" | custom-call | flops 1000000000 | bytes 8388608 | tf_op jit(solution)/shard_map/prep/pallas_call | solution.py:475
  13.8 0.0 copy-done.1
  13.8 0.0 copy-done.4
  13.8 0.0 copy-done.6
  13.8 10.1 %first.1 = (f32[4096,128]{1,0:T(8,128)S(1)}, bf16[1024,256]{1,0:T(8,128)(2,1)S(1)}, bf16[1024,256]{1,0:T(8,128)(2,1)S(1)}, f32[8,128]{1,0:T(8,128)S(1)}) custom-call(bf16[2048,128]{1,0:T(8,128)(2,1)S(1)} %copy-done.1, f32[128,256]{1,0:T(8,128)S(1)} %copy-done.6, s32[2,1024]{1,0:T(2,128)S(1)} %copy-done.2, s32[16,128]{1,0:T(8,128)S(1)} %bitcast.30, ...), custom_call_target="tpu_custom_call" | custom-call | flops 1000000000 | bytes 8388608 | tf_op jit(solution)/shard_map/first/pallas_call | solution.py:481
  23.9 0.2 collective-permute-start
  24.0 3.4 %collective-permute-start.1 = (bf16[1024,256]{1,0:T(8,128)(2,1)S(1)}, bf16[1024,256]{1,0:T(8,128)(2,1)S(1)}, u32[]{:S(2)}, u32[]{:S(2)}) collective-permute-start(bf16[1024,256]{1,0:T(8,128)(2,1)S(1)} %get-tuple-element.34), channel_id=1, source_target_pairs={{0,15},{1,0},{2,1},{3,2},{4,3},{5,4},{6,5},{7,6},{8,7},{9,8},{10,9... | collective-permute-start | bytes 1572872 | tf_op jit(solution)/shard_map/ppermute | solution.py:486
  27.5 0.0 copy-start
  27.5 0.0 copy-start.3
  27.5 7.7 %local_edges.4.part = f32[4096,128]{1,0:T(8,128)S(1)} custom-call(s32[2]{0:T(128)S(1)} %get-tuple-element.28.after.counts, s32[9216]{0:T(1024)S(1)} %bitcast.13, s32[9216]{0:T(1024)S(1)} %bitcast.20, f32[9216,128]{1,0:T(8,128)S(1)} %get-tuple-element.31.w, f32[4096,128]{1,0:T(8,128)S(1)} %get-tuple-element.35.table), custom_call_target="tpu_custom_call" | custom-call | flops 10000000000 | bytes 8388608 | tf_op jit(solution)/shard_map/local_edges/pallas_call | solution.py:490
  35.2 4.5 %collective-permute-done.from_prev = bf16[1024,256]{1,0:T(8,128)(2,1)S(1)} collective-permute-done((bf16[1024,256]{1,0:T(8,128)(2,1)S(1)}, bf16[1024,256]{1,0:T(8,128)(2,1)S(1)}, u32[]{:S(2)}, u32[]{:S(2)}) %collective-permute-start) | collective-permute-done | bytes 524320 | tf_op jit(solution)/shard_map/ppermute | solution.py:485
  39.7 0.0 collective-permute-done.1.from_next
  39.7 0.0 copy-done
  39.7 0.0 copy-done.3
  39.7 8.7 %hidden.1 = (bf16[2048,256]{1,0:T(8,128)(2,1)S(1)}, f32[4096,128]{1,0:T(8,128)S(1)}, bf16[1536,128]{1,0:T(8,128)(2,1)S(1)}, bf16[1536,128]{1,0:T(8,128)(2,1)S(1)}) custom-call(s32[2]{0:T(128)S(1)} %get-tuple-element.28.after.counts, s32[9216]{0:T(1024)S(1)} %bitcast.14, s32[9216]{0:T(1024)S(1)} %bitcast.21, f32[9216,128]{1,0:T(8,128)S(1)} %get-tuple-element.31.w, ...), custom_call_target="tpu_custom_call" | custom-call | flops 1000000000 | bytes 8388608 | tf_op jit(solution)/shard_map/hidden/pallas_call | solution.py:491
  48.4 0.1 collective-permute-start.2
  48.4 3.5 %collective-permute-start.3 = (bf16[1536,128]{1,0:T(8,128)(2,1)S(1)}, bf16[1536,128]{1,0:T(8,128)(2,1)S(1)}, u32[]{:S(2)}, u32[]{:S(2)}) collective-permute-start(bf16[1536,128]{1,0:T(8,128)(2,1)S(1)} %get-tuple-element.37), channel_id=1, source_target_pairs={{0,15},{1,0},{2,1},{3,2},{4,3},{5,4},{6,5},{7,6},{8,7},{9,8},{10,9... | collective-permute-start | bytes 1179656 | tf_op jit(solution)/shard_map/ppermute | solution.py:496
  52.0 0.0 copy-start.5
  52.0 7.7 %local_edges.5.part = f32[4096,128]{1,0:T(8,128)S(1)} custom-call(s32[2]{0:T(128)S(1)} %get-tuple-element.28.after.counts, s32[9216]{0:T(1024)S(1)} %bitcast.15, s32[9216]{0:T(1024)S(1)} %bitcast.22, f32[9216,128]{1,0:T(8,128)S(1)} %get-tuple-element.31.w, f32[4096,128]{1,0:T(8,128)S(1)} %get-tuple-element.38.table), custom_call_target="tpu_custom_call" | custom-call | flops 10000000000 | bytes 8388608 | tf_op jit(solution)/shard_map/local_edges/pallas_call | solution.py:497
  59.7 1.4 collective-permute-done.2.from_prev
  61.1 0.0 collective-permute-done.3.from_next
  61.2 0.0 copy-done.5
  61.2 8.6 %loss.1 = (f32[8,128]{1,0:T(8,128)S(1)}, f32[4096,128]{1,0:T(8,128)S(1)}, f32[1536,128]{1,0:T(8,128)S(1)}, f32[1536,128]{1,0:T(8,128)S(1)}) custom-call(s32[2]{0:T(128)S(1)} %get-tuple-element.28.after.counts, s32[9216]{0:T(1024)S(1)} %bitcast.16, s32[9216]{0:T(1024)S(1)} %bitcast.23, f32[9216,128]{1,0:T(8,128)S(1)} %get-tuple-element.31.w, ...), custom_call_target="tpu_custom_call" | custom-call | flops 1000000000 | bytes 8388608 | tf_op jit(solution)/shard_map/loss/pallas_call | solution.py:498
  69.7 0.1 collective-permute-start.4
  69.8 0.5 collective-permute-start.5
  70.3 7.7 %local_edges.6.part = f32[4096,128]{1,0:T(8,128)S(1)} custom-call(s32[2]{0:T(128)S(1)} %get-tuple-element.28.after.counts, s32[9216]{0:T(1024)S(1)} %bitcast.24, s32[9216]{0:T(1024)S(1)} %bitcast.17, f32[9216,128]{1,0:T(8,128)S(1)} %get-tuple-element.31.w, f32[4096,128]{1,0:T(8,128)S(1)} %get-tuple-element.41.table), custom_call_target="tpu_custom_call" | custom-call | flops 10000000000 | bytes 8388608 | tf_op jit(solution)/shard_map/local_edges/pallas_call | solution.py:504
  78.0 9.5 %collective-permute-done.4.got_prev = f32[1536,128]{1,0:T(8,128)S(1)} collective-permute-done((f32[1536,128]{1,0:T(8,128)S(1)}, f32[1536,128]{1,0:T(8,128)S(1)}, u32[]{:S(2)}, u32[]{:S(2)}) %collective-permute-start.4) | collective-permute-done | bytes 786464 | tf_op jit(solution)/shard_map/ppermute | solution.py:502
  87.5 3.1 %collective-permute-done.5.got_next = f32[1536,128]{1,0:T(8,128)S(1)} collective-permute-done((f32[1536,128]{1,0:T(8,128)S(1)}, f32[1536,128]{1,0:T(8,128)S(1)}, u32[]{:S(2)}, u32[]{:S(2)}) %collective-permute-start.5) | collective-permute-done | bytes 786464 | tf_op jit(solution)/shard_map/ppermute | solution.py:503
  90.6 9.9 %middle.1 = (f32[256,256]{1,0:T(8,128)S(1)}, f32[4096,128]{1,0:T(8,128)S(1)}, f32[2048,128]{1,0:T(8,128)S(1)}, f32[2048,128]{1,0:T(8,128)S(1)}) custom-call(s32[2]{0:T(128)S(1)} %get-tuple-element.28.after.counts, s32[9216]{0:T(1024)S(1)} %bitcast.18, s32[9216]{0:T(1024)S(1)} %bitcast.25, f32[9216,128]{1,0:T(8,128)S(1)} %get-tuple-element.31.w, ...), custom_call_target="tpu_custom_call" | custom-call | flops 1000000000 | bytes 8388608 | tf_op jit(solution)/shard_map/middle/pallas_call | solution.py:505
  100.5 0.1 collective-permute-start.6
  100.6 0.5 collective-permute-start.7
  101.1 7.7 %local_edges.7.part = f32[4096,128]{1,0:T(8,128)S(1)} custom-call(s32[2]{0:T(128)S(1)} %get-tuple-element.28.after.counts, s32[9216]{0:T(1024)S(1)} %bitcast.26, s32[9216]{0:T(1024)S(1)} %bitcast.19, f32[9216,128]{1,0:T(8,128)S(1)} %get-tuple-element.31.w, f32[4096,128]{1,0:T(8,128)S(1)} %get-tuple-element.45.table), custom_call_target="tpu_custom_call" | custom-call | flops 10000000000 | bytes 8388608 | tf_op jit(solution)/shard_map/local_edges/pallas_call | solution.py:511
  108.8 15.1 %collective-permute-done.6.got_prev = f32[2048,128]{1,0:T(8,128)S(1)} collective-permute-done((f32[2048,128]{1,0:T(8,128)S(1)}, f32[2048,128]{1,0:T(8,128)S(1)}, u32[]{:S(2)}, u32[]{:S(2)}) %collective-permute-start.6) | collective-permute-done | bytes 1048608 | tf_op jit(solution)/shard_map/ppermute | solution.py:509
  123.9 4.0 %collective-permute-done.7.got_next = f32[2048,128]{1,0:T(8,128)S(1)} collective-permute-done((f32[2048,128]{1,0:T(8,128)S(1)}, f32[2048,128]{1,0:T(8,128)S(1)}, u32[]{:S(2)}, u32[]{:S(2)}) %collective-permute-start.7) | collective-permute-done | bytes 1048608 | tf_op jit(solution)/shard_map/ppermute | solution.py:510
  127.9 5.6 %last.1.one = f32[128,256]{1,0:T(8,128)S(1)} custom-call(s32[2048]{0:T(1024)S(1)} %bitcast.29, f32[2048,128]{1,0:T(8,128)S(1)} %collective-permute-done.6.got_prev, f32[2048,128]{1,0:T(8,128)S(1)} %collective-permute-done.7.got_next, f32[4096,128]{1,0:T(8,128)S(1)} %local_edges.7.part, bf16[2048,128]{1,0:T(8,128)(2,1)S(1)} %copy-done.1), custom_call_target="tpu_custom_call" | custom-call | flops 1000000000 | bytes 8388608 | tf_op jit(solution)/shard_map/last/pallas_call | solution.py:513
  133.5 12.8 %reduce.1 = (f32[128,256]{1,0:T(8,128)S(1)}, f32[172,256]{1,0:T(8,128)S(1)}, f32[1,1]{1,0:T(1,128)}) custom-call(f32[128,256]{1,0:T(8,128)S(1)} %last.1.one, f32[256,256]{1,0:T(8,128)S(1)} %get-tuple-element.46.two, f32[8,128]{1,0:T(8,128)S(1)} %get-tuple-element.47.loss, f32[8,128]{1,0:T(8,128)S(1)} %get-tuple-element.32.count), custom_call_target="tpu_custom_call" | custom-call | flops 1000000000 | bytes 8388608 | tf_op jit(solution)/shard_map/reduce/pallas_call | solution.py:516
  146.9 0.7 copy.16
  147.6 0.7 copy.17
Async XLA Ops:
  0.6 13.1 %copy-start.1 = (bf16[2048,128]{1,0:T(8,128)(2,1)S(1)}, bf16[2048,128]{1,0:T(8,128)(2,1)}, u32[]{:S(2)}) copy-start(bf16[2048,128]{1,0:T(8,128)(2,1)} %x.3) | copy-start | bytes 1572868
  0.6 0.8 copy-start.2
  1.4 0.8 copy-start.7
  2.2 0.8 copy-start.8
  2.9 0.8 copy-start.9
  3.7 10.1 %copy-start.4 = (s32[2048]{0:T(1024)S(1)}, s32[2048]{0:T(1024)}, u32[]{:S(2)}) copy-start(s32[2048]{0:T(1024)} %param.17) | copy-start | bytes 24580
  3.7 10.1 %copy-start.6 = (f32[128,256]{1,0:T(8,128)S(1)}, f32[128,256]{1,0:T(8,128)}, u32[]{:S(2)}) copy-start(f32[128,256]{1,0:T(8,128)} %w1.1) | copy-start | bytes 393220
  23.9 15.8 %collective-permute-start = (bf16[1024,256]{1,0:T(8,128)(2,1)S(1)}, bf16[1024,256]{1,0:T(8,128)(2,1)S(1)}, u32[]{:S(2)}, u32[]{:S(2)}) collective-permute-start(bf16[1024,256]{1,0:T(8,128)(2,1)S(1)} %get-tuple-element.33), channel_id=1, source_target_pairs={{0,1},{1,2},{2,3},{3,4},{4,5},{5,6},{6,7},{7,8},{8,9},{9,10},{10,1... | collective-permute-start | bytes 1572872 | tf_op jit(solution)/shard_map/ppermute | solution.py:485
  24.0 15.7 %collective-permute-start.1 = (bf16[1024,256]{1,0:T(8,128)(2,1)S(1)}, bf16[1024,256]{1,0:T(8,128)(2,1)S(1)}, u32[]{:S(2)}, u32[]{:S(2)}) collective-permute-start(bf16[1024,256]{1,0:T(8,128)(2,1)S(1)} %get-tuple-element.34), channel_id=1, source_target_pairs={{0,15},{1,0},{2,1},{3,2},{4,3},{5,4},{6,5},{7,6},{8,7},{9,8},{10,9... | collective-permute-start | bytes 1572872 | tf_op jit(solution)/shard_map/ppermute | solution.py:486
  27.5 12.2 %copy-start = (f32[256,172]{0,1:T(8,128)S(1)}, f32[256,172]{0,1:T(8,128)}, u32[]{:S(2)}) copy-start(f32[256,172]{0,1:T(8,128)} %param.11) | copy-start | bytes 528388
  27.5 12.2 %copy-start.3 = (s32[2,1024]{1,0:T(2,128)S(1)}, s32[2,1024]{1,0:T(2,128)}, u32[]{:S(2)}) copy-start(s32[2,1024]{1,0:T(2,128)} %send.5) | copy-start | bytes 24580
  48.4 12.8 %collective-permute-start.2 = (bf16[1536,128]{1,0:T(8,128)(2,1)S(1)}, bf16[1536,128]{1,0:T(8,128)(2,1)S(1)}, u32[]{:S(2)}, u32[]{:S(2)}) collective-permute-start(bf16[1536,128]{1,0:T(8,128)(2,1)S(1)} %get-tuple-element.36), channel_id=1, source_target_pairs={{0,1},{1,2},{2,3},{3,4},{4,5},{5,6},{6,7},{7,8},{8,9},{9,10},{10,1... | collective-permute-start | bytes 1179656 | tf_op jit(solution)/shard_map/ppermute | solution.py:495
  48.4 12.7 %collective-permute-start.3 = (bf16[1536,128]{1,0:T(8,128)(2,1)S(1)}, bf16[1536,128]{1,0:T(8,128)(2,1)S(1)}, u32[]{:S(2)}, u32[]{:S(2)}) collective-permute-start(bf16[1536,128]{1,0:T(8,128)(2,1)S(1)} %get-tuple-element.37), channel_id=1, source_target_pairs={{0,15},{1,0},{2,1},{3,2},{4,3},{5,4},{6,5},{7,6},{8,7},{9,8},{10,9... | collective-permute-start | bytes 1179656 | tf_op jit(solution)/shard_map/ppermute | solution.py:496
  52.0 9.2 %copy-start.5 = (s32[2048]{0:T(1024)S(1)}, s32[2048]{0:T(1024)}, u32[]{:S(2)}) copy-start(s32[2048]{0:T(1024)} %param.16) | copy-start | bytes 24580
  69.7 17.8 %collective-permute-start.4 = (f32[1536,128]{1,0:T(8,128)S(1)}, f32[1536,128]{1,0:T(8,128)S(1)}, u32[]{:S(2)}, u32[]{:S(2)}) collective-permute-start(f32[1536,128]{1,0:T(8,128)S(1)} %get-tuple-element.39), channel_id=1, source_target_pairs={{0,15},{1,0},{2,1},{3,2},{4,3},{5,4},{6,5},{7,6},{8,7},{9,8},{10,9... | collective-permute-start | bytes 2359304 | tf_op jit(solution)/shard_map/ppermute | solution.py:502
  69.8 20.8 %collective-permute-start.5 = (f32[1536,128]{1,0:T(8,128)S(1)}, f32[1536,128]{1,0:T(8,128)S(1)}, u32[]{:S(2)}, u32[]{:S(2)}) collective-permute-start(f32[1536,128]{1,0:T(8,128)S(1)} %get-tuple-element.40), channel_id=1, source_target_pairs={{0,1},{1,2},{2,3},{3,4},{4,5},{5,6},{6,7},{7,8},{8,9},{9,10},{10,1... | collective-permute-start | bytes 2359304 | tf_op jit(solution)/shard_map/ppermute | solution.py:503
  100.5 23.4 %collective-permute-start.6 = (f32[2048,128]{1,0:T(8,128)S(1)}, f32[2048,128]{1,0:T(8,128)S(1)}, u32[]{:S(2)}, u32[]{:S(2)}) collective-permute-start(f32[2048,128]{1,0:T(8,128)S(1)} %get-tuple-element.43), channel_id=1, source_target_pairs={{0,15},{1,0},{2,1},{3,2},{4,3},{5,4},{6,5},{7,6},{8,7},{9,8},{10,9... | collective-permute-start | bytes 3145736 | tf_op jit(solution)/shard_map/ppermute | solution.py:509
  100.6 27.3 %collective-permute-start.7 = (f32[2048,128]{1,0:T(8,128)S(1)}, f32[2048,128]{1,0:T(8,128)S(1)}, u32[]{:S(2)}, u32[]{:S(2)}) collective-permute-start(f32[2048,128]{1,0:T(8,128)S(1)} %get-tuple-element.44), channel_id=1, source_target_pairs={{0,1},{1,2},{2,3},{3,4},{4,5},{5,6},{6,7},{7,8},{8,9},{9,10},{10,1... | collective-permute-start | bytes 3145736 | tf_op jit(solution)/shard_map/ppermute | solution.py:510

commit v5 on v4

--- a/solution.py
+++ b/solution.py
@@ -240,12 +240,9 @@
     mean[...] = jnp.sum(full[tail : tail + 8, :], keepdims=True) / count[0:1, 0:1]
 
 
-def prep_kernel(chunk, rows, src, dst, w, send, src_out, dst_out, w_out, back, counts, total):
+def prep_kernel(chunk, rows, src, dst, w, src_out, dst_out, w_out, counts, total):
     lines = src.shape[0]
     slots = src_out.shape[0]
-    per = send.shape[1] // LANES
-    for i in range(2 * per):
-        back[i : i + 1, :] = send[i // per : i // per + 1, (i % per) * LANES : (i % per + 1) * LANES] * 2
     live = w[...] != 0.0
     halo = src[...] >= rows
     at = lambda shape, axis: lax.broadcasted_iota(jnp.int32, shape, axis)
@@ -290,9 +287,10 @@
     dst_out[...] = ((high & 7) * 256 + plane(1).astype(jnp.int32)) * 2
     total[0:slots, :] = (plane(3) + plane(4) + plane(5)) * 2.0
 
-    @pl.loop(0, slots)
+    @pl.loop(0, slots // 8)
     def _(r):
-        w_out[pl.ds(pl.multiple_of(r * LANES, LANES), LANES), :] = spread(total[pl.ds(r, 1), :])
+        for q in range(8):
+            w_out[pl.ds(pl.multiple_of((r * 8 + q) * LANES, LANES), LANES), :] = spread(total[pl.ds(r * 8 + q, 1), :])
 
 
 def local_kernel(chunk, n_acc, counts, from_idx, to_idx, w, table, out, *accs):
@@ -352,8 +350,11 @@
     return buf[...].astype(BF16)
 
 
-def hidden_kernel(chunk, counts, src, dst, w, send, from_prev, from_next, part, w2, hid, tab, to_prev, to_next, htab, tab_b, w2_pad, *accs):
+def hidden_kernel(chunk, counts, src, dst, w, send, from_prev, from_next, part, w2, hid, tab, to_prev, to_next, back, htab, tab_b, w2_pad, *accs):
     w2_b = padded(w2, w2_pad)
+    per = send.shape[1] // LANES
+    for i in range(2 * per):
+        back[i : i + 1, :] = send[i // per : i // per + 1, (i % per) * LANES : (i % per + 1) * LANES] * 2
     forward_halo(chunk, counts, src, dst, w, from_prev, from_next, part, htab, accs, unpack_plain)
 
     @pl.loop(0, hid.shape[0], step=256)
@@ -472,11 +473,11 @@
 
         lined = lambda a: a.reshape(lines, LANES)
         ints = sds((slots, LANES), jnp.int32)
-        src, dst, w, back, counts = call(
-            functools.partial(prep_kernel, PREP_CHUNK, rows), "prep", [ints, ints, sds((slots * LANES, LANES), F32), sds((2 * halo // LANES, LANES), jnp.int32), sds((2,), jnp.int32)], [VMEM] * 4,
-            [(6 * slots, LANES)], out_specs=[VMEM] * 4 + [SMEM], vmem=8,
-        )(lined(edge_src), lined(edge_dst), lined(edge_w), send)
-        src, dst, back = src.reshape(-1), dst.reshape(-1), back.reshape(-1)
+        src, dst, w, counts = call(
+            functools.partial(prep_kernel, PREP_CHUNK, rows), "prep", [ints, ints, sds((slots * LANES, LANES), F32), sds((2,), jnp.int32)], [VMEM] * 3,
+            [(6 * slots, LANES)], out_specs=[VMEM] * 3 + [SMEM], vmem=8,
+        )(lined(edge_src), lined(edge_dst), lined(edge_w))
+        src, dst = src.reshape(-1), dst.reshape(-1)
 
         tab_one, to_p, to_n, count = call(
             functools.partial(first_kernel, num_dev), "first", [tab_f, half_b, half_b, one], [VMEM] * 4 + [SMEM],
@@ -488,12 +489,13 @@
         walk = [SMEM] * 3 + [VMEM]
         local = call(functools.partial(local_kernel, chunk_l, 4), "local_edges", tab_f, walk + [VMEM], [tab] * 4, 10**10)
         part = local(counts, src, dst, w, tab_one)
-        hid, tab_two, to_p, to_n = call(
-            functools.partial(hidden_kernel, chunk_h), "hidden", [sds((rows, 2 * LANES), BF16), tab_f, pack_b, pack_b],
+        hid, tab_two, to_p, to_n, back = call(
+            functools.partial(hidden_kernel, chunk_h), "hidden", [sds((rows, 2 * LANES), BF16), tab_f, pack_b, pack_b, sds((2 * halo // LANES, LANES), jnp.int32)],
             walk + [VMEM] * 5, [tab, tab_b, w2_pad] + [tab] * 4,
         )(counts, src, dst, w, send, from_prev, from_next, part, w2)
         from_prev = lax.ppermute(to_n, AXIS, to_next)
         from_next = lax.ppermute(to_p, AXIS, to_prev)
+        back = back.reshape(-1)
         part = local(counts, src, dst, w, tab_two)
         loss, grad, to_p, to_n = call(
             functools.partial(loss_kernel, chunk_h, classes), "loss", [sds((8, LANES), F32), tab_f, pack_f, pack_f],

time: 149 us -> 142 us (0.953)
  Pallas kernels: 96.6 us -> 92.6 us
  waiting for transfers between devices: 37.6 us -> 34.1 us
    pallas_call x1, Pallas kernels: 10.1 us -> 4.59 us  [step(): call(functools.partial(prep_kernel, PREP_CHUNK, rows), 'prep', [ints, int...]
    ppermute x2, waiting for transfers between devices: 24.6 us -> 22.6 us  [step(): got_prev = lax.ppermute(to_p, AXIS, to_prev)]
    ppermute x2, waiting for transfers between devices: 5.94 us -> 4.41 us  [step(): from_prev = lax.ppermute(to_n, AXIS, to_next)]
    unnamed x22 -> x20, local copies, waits for them, and re-layouts: 4.37 us -> 3.68 us
  transfers between devices with their start and end apart: 8 -> 8, of which waited for: 6 -> 6; matrix products, arithmetic and copies ran while one was open for 0% -> 0% of each run, Pallas kernels for 21% -> 23%
where the time goes in v5:
time: 142 us; the launch traced here: 141 us
  Pallas kernels  92.6 us (65%)
  waiting for transfers between devices  34.1 us (24%)
  starting transfers between devices  8.26 us (6%)
  local copies, waits for them, and re-layouts  3.68 us (3%)
  between operations  2.57 us (2%)
    ppermute x2, waiting for transfers between devices, step(): got_prev = lax.ppermute(to_p, AXIS, to_prev)  22.6 us
    pallas_call x2, Pallas kernels, step(): part = local(counts, dst, src, w, grad)  16.4 us
    pallas_call x1, Pallas kernels, step(): call(functools.partial(reduce_kernel, num_dev), 'reduce', [sds(grad_one.s...  13.1 us
    pallas_call x1, Pallas kernels, step(): call(functools.partial(first_kernel, num_dev), 'first', [tab_f, half_b, h...  10.1 us
    pallas_call x1, Pallas kernels, step(): call(functools.partial(middle_kernel, chunk_h), 'middle', [sds((2 * LANES...  9.74 us
    pallas_call x1, Pallas kernels, step(): call(functools.partial(hidden_kernel, chunk_h), 'hidden', [sds((rows, 2 *...  8.52 us
    pallas_call x1, Pallas kernels, step(): call(functools.partial(loss_kernel, chunk_h, classes), 'loss', [sds((8, L...  8.22 us
    pallas_call x1, Pallas kernels, step(): part = local(counts, src, dst, w, tab_one)  8.19 us
  transfers between devices with their start and end apart: 8, of which 6 were waited for; matrix products, arithmetic and copies ran while one was open for 0% of the time, Pallas kernels for 23%

profile of v5, /device:TPU:0, one launch (start us, length us, event | category | flops | bytes accessed | tf_op | source)
XLA Modules:
  0.0 141.1 jit_solution(15020234971739060536)
XLA Ops:
  0.6 0.0 copy-start.2
  0.6 0.0 copy-start.1
  0.7 0.0 copy-start.3
  0.7 0.0 copy-start.5
  0.7 0.0 copy-start.6
  0.7 0.8 copy-done.6
  1.5 0.0 copy-start.7
  1.5 0.8 copy-done.7
  2.3 0.0 copy-start.8
  2.3 0.8 copy-done.8
  3.0 4.6 %prep.1 = (s32[72,128]{1,0:T(8,128)S(1)}, s32[72,128]{1,0:T(8,128)S(1)}, f32[9216,128]{1,0:T(8,128)S(1)}, s32[2]{0:T(128)S(1)}) custom-call(s32[64,128]{1,0:T(8,128)S(1)} %bitcast.33, s32[64,128]{1,0:T(8,128)S(1)} %bitcast.34, f32[64,128]{1,0:T(8,128)S(1)} %bitcast.35), custom_call_target="tpu_custom_call" | custom-call | flops 1000000000 | bytes 8388608 | tf_op jit(solution)/shard_map/prep/pallas_call | solution.py:476
  7.6 0.0 copy-done.2
  7.6 0.0 copy-done.1
  7.6 0.0 copy-done.3
  7.6 0.0 copy-done.5
  7.6 10.1 %first.1 = (f32[4096,128]{1,0:T(8,128)S(1)}, bf16[1024,256]{1,0:T(8,128)(2,1)S(1)}, bf16[1024,256]{1,0:T(8,128)(2,1)S(1)}, f32[8,128]{1,0:T(8,128)S(1)}) custom-call(bf16[2048,128]{1,0:T(8,128)(2,1)S(1)} %copy-done.1, f32[128,256]{1,0:T(8,128)S(1)} %copy-done.5, s32[2,1024]{1,0:T(2,128)S(1)} %copy-done.2, s32[16,128]{1,0:T(8,128)S(1)} %bitcast.30, ...), custom_call_target="tpu_custom_call" | custom-call | flops 1000000000 | bytes 8388608 | tf_op jit(solution)/shard_map/first/pallas_call | solution.py:482
  17.7 0.2 collective-permute-start
  17.9 3.4 %collective-permute-start.1 = (bf16[1024,256]{1,0:T(8,128)(2,1)S(1)}, bf16[1024,256]{1,0:T(8,128)(2,1)S(1)}, u32[]{:S(2)}, u32[]{:S(2)}) collective-permute-start(bf16[1024,256]{1,0:T(8,128)(2,1)S(1)} %get-tuple-element.32), channel_id=1, source_target_pairs={{0,15},{1,0},{2,1},{3,2},{4,3},{5,4},{6,5},{7,6},{8,7},{9,8},{10,9... | collective-permute-start | bytes 1572872 | tf_op jit(solution)/shard_map/ppermute | solution.py:487
  21.3 0.0 copy-start
  21.3 8.2 %local_edges.4.part = f32[4096,128]{1,0:T(8,128)S(1)} custom-call(s32[2]{0:T(128)S(1)} %get-tuple-element.27.after.counts, s32[9216]{0:T(1024)S(1)} %bitcast.13, s32[9216]{0:T(1024)S(1)} %bitcast.20, f32[9216,128]{1,0:T(8,128)S(1)} %get-tuple-element.30.w, f32[4096,128]{1,0:T(8,128)S(1)} %get-tuple-element.33.table), custom_call_target="tpu_custom_call" | custom-call | flops 10000000000 | bytes 8388608 | tf_op jit(solution)/shard_map/local_edges/pallas_call | solution.py:491
  29.5 4.0 %collective-permute-done.from_prev = bf16[1024,256]{1,0:T(8,128)(2,1)S(1)} collective-permute-done((bf16[1024,256]{1,0:T(8,128)(2,1)S(1)}, bf16[1024,256]{1,0:T(8,128)(2,1)S(1)}, u32[]{:S(2)}, u32[]{:S(2)}) %collective-permute-start) | collective-permute-done | bytes 524320 | tf_op jit(solution)/shard_map/ppermute | solution.py:486
  33.5 0.0 collective-permute-done.1.from_next
  33.5 0.0 copy-done
  33.5 8.5 %hidden.1 = (bf16[2048,256]{1,0:T(8,128)(2,1)S(1)}, f32[4096,128]{1,0:T(8,128)S(1)}, bf16[1536,128]{1,0:T(8,128)(2,1)S(1)}, bf16[1536,128]{1,0:T(8,128)(2,1)S(1)}, s32[16,128]{1,0:T(8,128)S(1)}) custom-call(s32[2]{0:T(128)S(1)} %get-tuple-element.27.after.counts, s32[9216]{0:T(1024)S(1)} %bitcast.14, s32[9216]{0:T(1024)S(1)} %bitcast.21, ...), custom_call_target="tpu_custom_call" | custom-call | flops 1000000000 | bytes 8388608 | tf_op jit(solution)/shard_map/hidden/pallas_call | solution.py:492
  42.1 0.1 collective-permute-start.2
  42.1 3.5 %collective-permute-start.3 = (bf16[1536,128]{1,0:T(8,128)(2,1)S(1)}, bf16[1536,128]{1,0:T(8,128)(2,1)S(1)}, u32[]{:S(2)}, u32[]{:S(2)}) collective-permute-start(bf16[1536,128]{1,0:T(8,128)(2,1)S(1)} %get-tuple-element.37), channel_id=1, source_target_pairs={{0,15},{1,0},{2,1},{3,2},{4,3},{5,4},{6,5},{7,6},{8,7},{9,8},{10,9... | collective-permute-start | bytes 1179656 | tf_op jit(solution)/shard_map/ppermute | solution.py:497
  45.7 0.0 copy-start.4
  45.7 8.2 %local_edges.5.part = f32[4096,128]{1,0:T(8,128)S(1)} custom-call(s32[2]{0:T(128)S(1)} %get-tuple-element.27.after.counts, s32[9216]{0:T(1024)S(1)} %bitcast.15, s32[9216]{0:T(1024)S(1)} %bitcast.22, f32[9216,128]{1,0:T(8,128)S(1)} %get-tuple-element.30.w, f32[4096,128]{1,0:T(8,128)S(1)} %get-tuple-element.38.table), custom_call_target="tpu_custom_call" | custom-call | flops 10000000000 | bytes 8388608 | tf_op jit(solution)/shard_map/local_edges/pallas_call | solution.py:499
  53.9 0.4 collective-permute-done.2.from_prev
  54.3 0.0 collective-permute-done.3.from_next
  54.3 0.0 copy-done.4
  54.3 8.2 %loss.1 = (f32[8,128]{1,0:T(8,128)S(1)}, f32[4096,128]{1,0:T(8,128)S(1)}, f32[1536,128]{1,0:T(8,128)S(1)}, f32[1536,128]{1,0:T(8,128)S(1)}) custom-call(s32[2]{0:T(128)S(1)} %get-tuple-element.27.after.counts, s32[9216]{0:T(1024)S(1)} %bitcast.16, s32[9216]{0:T(1024)S(1)} %bitcast.23, f32[9216,128]{1,0:T(8,128)S(1)} %get-tuple-element.30.w, ...), custom_call_target="tpu_custom_call" | custom-call | flops 1000000000 | bytes 8388608 | tf_op jit(solution)/shard_map/loss/pallas_call | solution.py:500
  62.5 0.1 collective-permute-start.4
  62.5 0.5 collective-permute-start.5
  63.0 8.2 %local_edges.6.part = f32[4096,128]{1,0:T(8,128)S(1)} custom-call(s32[2]{0:T(128)S(1)} %get-tuple-element.27.after.counts, s32[9216]{0:T(1024)S(1)} %bitcast.24, s32[9216]{0:T(1024)S(1)} %bitcast.17, f32[9216,128]{1,0:T(8,128)S(1)} %get-tuple-element.30.w, f32[4096,128]{1,0:T(8,128)S(1)} %get-tuple-element.41.table), custom_call_target="tpu_custom_call" | custom-call | flops 10000000000 | bytes 8388608 | tf_op jit(solution)/shard_map/local_edges/pallas_call | solution.py:506
  71.2 7.9 %collective-permute-done.4.got_prev = f32[1536,128]{1,0:T(8,128)S(1)} collective-permute-done((f32[1536,128]{1,0:T(8,128)S(1)}, f32[1536,128]{1,0:T(8,128)S(1)}, u32[]{:S(2)}, u32[]{:S(2)}) %collective-permute-start.4) | collective-permute-done | bytes 786464 | tf_op jit(solution)/shard_map/ppermute | solution.py:504
  79.2 5.0 %collective-permute-done.5.got_next = f32[1536,128]{1,0:T(8,128)S(1)} collective-permute-done((f32[1536,128]{1,0:T(8,128)S(1)}, f32[1536,128]{1,0:T(8,128)S(1)}, u32[]{:S(2)}, u32[]{:S(2)}) %collective-permute-start.5) | collective-permute-done | bytes 786464 | tf_op jit(solution)/shard_map/ppermute | solution.py:505
  84.2 9.7 %middle.1 = (f32[256,256]{1,0:T(8,128)S(1)}, f32[4096,128]{1,0:T(8,128)S(1)}, f32[2048,128]{1,0:T(8,128)S(1)}, f32[2048,128]{1,0:T(8,128)S(1)}) custom-call(s32[2]{0:T(128)S(1)} %get-tuple-element.27.after.counts, s32[9216]{0:T(1024)S(1)} %bitcast.18, s32[9216]{0:T(1024)S(1)} %bitcast.25, f32[9216,128]{1,0:T(8,128)S(1)} %get-tuple-element.30.w, ...), custom_call_target="tpu_custom_call" | custom-call | flops 1000000000 | bytes 8388608 | tf_op jit(solution)/shard_map/middle/pallas_call | solution.py:507
  94.0 0.1 collective-permute-start.6
  94.0 0.5 collective-permute-start.7
  94.5 8.2 %local_edges.7.part = f32[4096,128]{1,0:T(8,128)S(1)} custom-call(s32[2]{0:T(128)S(1)} %get-tuple-element.27.after.counts, s32[9216]{0:T(1024)S(1)} %bitcast.26, s32[9216]{0:T(1024)S(1)} %bitcast.19, f32[9216,128]{1,0:T(8,128)S(1)} %get-tuple-element.30.w, f32[4096,128]{1,0:T(8,128)S(1)} %get-tuple-element.45.table), custom_call_target="tpu_custom_call" | custom-call | flops 10000000000 | bytes 8388608 | tf_op jit(solution)/shard_map/local_edges/pallas_call | solution.py:513
  102.7 14.7 %collective-permute-done.6.got_prev = f32[2048,128]{1,0:T(8,128)S(1)} collective-permute-done((f32[2048,128]{1,0:T(8,128)S(1)}, f32[2048,128]{1,0:T(8,128)S(1)}, u32[]{:S(2)}, u32[]{:S(2)}) %collective-permute-start.6) | collective-permute-done | bytes 1048608 | tf_op jit(solution)/shard_map/ppermute | solution.py:511
  117.4 2.0 %collective-permute-done.7.got_next = f32[2048,128]{1,0:T(8,128)S(1)} collective-permute-done((f32[2048,128]{1,0:T(8,128)S(1)}, f32[2048,128]{1,0:T(8,128)S(1)}, u32[]{:S(2)}, u32[]{:S(2)}) %collective-permute-start.7) | collective-permute-done | bytes 1048608 | tf_op jit(solution)/shard_map/ppermute | solution.py:512
  119.4 5.6 %last.1.one = f32[128,256]{1,0:T(8,128)S(1)} custom-call(s32[2048]{0:T(1024)S(1)} %bitcast.29, f32[2048,128]{1,0:T(8,128)S(1)} %collective-permute-done.6.got_prev, f32[2048,128]{1,0:T(8,128)S(1)} %collective-permute-done.7.got_next, f32[4096,128]{1,0:T(8,128)S(1)} %local_edges.7.part, bf16[2048,128]{1,0:T(8,128)(2,1)S(1)} %copy-done.1), custom_call_target="tpu_custom_call" | custom-call | flops 1000000000 | bytes 8388608 | tf_op jit(solution)/shard_map/last/pallas_call | solution.py:515
  124.9 13.1 %reduce.1 = (f32[128,256]{1,0:T(8,128)S(1)}, f32[172,256]{1,0:T(8,128)S(1)}, f32[1,1]{1,0:T(1,128)}) custom-call(f32[128,256]{1,0:T(8,128)S(1)} %last.1.one, f32[256,256]{1,0:T(8,128)S(1)} %get-tuple-element.46.two, f32[8,128]{1,0:T(8,128)S(1)} %get-tuple-element.47.loss, f32[8,128]{1,0:T(8,128)S(1)} %get-tuple-element.35.count), custom_call_target="tpu_custom_call" | custom-call | flops 1000000000 | bytes 8388608 | tf_op jit(solution)/shard_map/reduce/pallas_call | solution.py:518
  138.7 0.7 copy.16
  139.3 0.7 copy.17
Async XLA Ops:
  0.6 7.0 %copy-start.2 = (s32[2,1024]{1,0:T(2,128)S(1)}, s32[2,1024]{1,0:T(2,128)}, u32[]{:S(2)}) copy-start(s32[2,1024]{1,0:T(2,128)} %send.3) | copy-start | bytes 24580
  0.6 7.0 %copy-start.1 = (bf16[2048,128]{1,0:T(8,128)(2,1)S(1)}, bf16[2048,128]{1,0:T(8,128)(2,1)}, u32[]{:S(2)}) copy-start(bf16[2048,128]{1,0:T(8,128)(2,1)} %x.3) | copy-start | bytes 1572868
  0.7 7.0 %copy-start.3 = (s32[2048]{0:T(1024)S(1)}, s32[2048]{0:T(1024)}, u32[]{:S(2)}) copy-start(s32[2048]{0:T(1024)} %param.17) | copy-start | bytes 24580
  0.7 7.0 %copy-start.5 = (f32[128,256]{1,0:T(8,128)S(1)}, f32[128,256]{1,0:T(8,128)}, u32[]{:S(2)}) copy-start(f32[128,256]{1,0:T(8,128)} %w1.1) | copy-start | bytes 393220
  0.7 0.8 copy-start.6
  1.5 0.8 copy-start.7
  2.3 0.8 copy-start.8
  17.7 15.8 %collective-permute-start = (bf16[1024,256]{1,0:T(8,128)(2,1)S(1)}, bf16[1024,256]{1,0:T(8,128)(2,1)S(1)}, u32[]{:S(2)}, u32[]{:S(2)}) collective-permute-start(bf16[1024,256]{1,0:T(8,128)(2,1)S(1)} %get-tuple-element.31), channel_id=1, source_target_pairs={{0,1},{1,2},{2,3},{3,4},{4,5},{5,6},{6,7},{7,8},{8,9},{9,10},{10,1... | collective-permute-start | bytes 1572872 | tf_op jit(solution)/shard_map/ppermute | solution.py:486
  17.9 15.6 %collective-permute-start.1 = (bf16[1024,256]{1,0:T(8,128)(2,1)S(1)}, bf16[1024,256]{1,0:T(8,128)(2,1)S(1)}, u32[]{:S(2)}, u32[]{:S(2)}) collective-permute-start(bf16[1024,256]{1,0:T(8,128)(2,1)S(1)} %get-tuple-element.32), channel_id=1, source_target_pairs={{0,15},{1,0},{2,1},{3,2},{4,3},{5,4},{6,5},{7,6},{8,7},{9,8},{10,9... | collective-permute-start | bytes 1572872 | tf_op jit(solution)/shard_map/ppermute | solution.py:487
  21.3 12.2 %copy-start = (f32[256,172]{0,1:T(8,128)S(1)}, f32[256,172]{0,1:T(8,128)}, u32[]{:S(2)}) copy-start(f32[256,172]{0,1:T(8,128)} %param.11) | copy-start | bytes 528388
  42.1 12.2 %collective-permute-start.2 = (bf16[1536,128]{1,0:T(8,128)(2,1)S(1)}, bf16[1536,128]{1,0:T(8,128)(2,1)S(1)}, u32[]{:S(2)}, u32[]{:S(2)}) collective-permute-start(bf16[1536,128]{1,0:T(8,128)(2,1)S(1)} %get-tuple-element.36), channel_id=1, source_target_pairs={{0,1},{1,2},{2,3},{3,4},{4,5},{5,6},{6,7},{7,8},{8,9},{9,10},{10,1... | collective-permute-start | bytes 1179656 | tf_op jit(solution)/shard_map/ppermute | solution.py:496
  42.1 12.1 %collective-permute-start.3 = (bf16[1536,128]{1,0:T(8,128)(2,1)S(1)}, bf16[1536,128]{1,0:T(8,128)(2,1)S(1)}, u32[]{:S(2)}, u32[]{:S(2)}) collective-permute-start(bf16[1536,128]{1,0:T(8,128)(2,1)S(1)} %get-tuple-element.37), channel_id=1, source_target_pairs={{0,15},{1,0},{2,1},{3,2},{4,3},{5,4},{6,5},{7,6},{8,7},{9,8},{10,9... | collective-permute-start | bytes 1179656 | tf_op jit(solution)/shard_map/ppermute | solution.py:497
  45.7 8.6 %copy-start.4 = (s32[2048]{0:T(1024)S(1)}, s32[2048]{0:T(1024)}, u32[]{:S(2)}) copy-start(s32[2048]{0:T(1024)} %param.16) | copy-start | bytes 24580
  62.5 16.7 %collective-permute-start.4 = (f32[1536,128]{1,0:T(8,128)S(1)}, f32[1536,128]{1,0:T(8,128)S(1)}, u32[]{:S(2)}, u32[]{:S(2)}) collective-permute-start(f32[1536,128]{1,0:T(8,128)S(1)} %get-tuple-element.39), channel_id=1, source_target_pairs={{0,15},{1,0},{2,1},{3,2},{4,3},{5,4},{6,5},{7,6},{8,7},{9,8},{10,9... | collective-permute-start | bytes 2359304 | tf_op jit(solution)/shard_map/ppermute | solution.py:504
  62.5 21.7 %collective-permute-start.5 = (f32[1536,128]{1,0:T(8,128)S(1)}, f32[1536,128]{1,0:T(8,128)S(1)}, u32[]{:S(2)}, u32[]{:S(2)}) collective-permute-start(f32[1536,128]{1,0:T(8,128)S(1)} %get-tuple-element.40), channel_id=1, source_target_pairs={{0,1},{1,2},{2,3},{3,4},{4,5},{5,6},{6,7},{7,8},{8,9},{9,10},{10,1... | collective-permute-start | bytes 2359304 | tf_op jit(solution)/shard_map/ppermute | solution.py:505
  94.0 23.4 %collective-permute-start.6 = (f32[2048,128]{1,0:T(8,128)S(1)}, f32[2048,128]{1,0:T(8,128)S(1)}, u32[]{:S(2)}, u32[]{:S(2)}) collective-permute-start(f32[2048,128]{1,0:T(8,128)S(1)} %get-tuple-element.43), channel_id=1, source_target_pairs={{0,15},{1,0},{2,1},{3,2},{4,3},{5,4},{6,5},{7,6},{8,7},{9,8},{10,9... | collective-permute-start | bytes 3145736 | tf_op jit(solution)/shard_map/ppermute | solution.py:511
  94.0 25.4 %collective-permute-start.7 = (f32[2048,128]{1,0:T(8,128)S(1)}, f32[2048,128]{1,0:T(8,128)S(1)}, u32[]{:S(2)}, u32[]{:S(2)}) collective-permute-start(f32[2048,128]{1,0:T(8,128)S(1)} %get-tuple-element.44), channel_id=1, source_target_pairs={{0,1},{1,2},{2,3},{3,4},{4,5},{5,6},{6,7},{7,8},{8,9},{9,10},{10,1... | collective-permute-start | bytes 3145736 | tf_op jit(solution)/shard_map/ppermute | solution.py:512
